TPU v7x, 128 devices: a whole 4x4x4 slice. The times are simulated.
128 devices in a mesh: rows: 32 (over y, x, core), cols: 4 (over z).
Axes of the slice: x: 4, y: 4, z: 4, core: 2. Of those that a mesh axis runs over, the one named last changes fastest.
Arguments:
- token_ids: int32 [64, 2048], P('rows', 'cols'), may hold values from 0 to 524287, as said below
- lengths: int32 [64], P('rows'), may hold values from 1 to 2048
- table: bfloat16 [524288, 512], P('rows', 'cols'), may hold values from -6 to 6
- attn_gain: float32 [512], replicated, may hold values from 0.1 to 1.9
- w_qkv: bfloat16 [512, 1536], replicated, may hold values from -2 to 2
- w_out: bfloat16 [512, 512], replicated, may hold values from -0.25 to 0.25
- mlp_gain: float32 [512], replicated, may hold values from 0.1 to 1.9
- w_in: bfloat16 [512, 4096], replicated, may hold values from -0.25 to 0.25
- w_down: bfloat16 [2048, 512], replicated, may hold values from -0.125 to 0.125
Outputs:
- layer_out: bfloat16 [64, 2048, 512], P('rows', 'cols')
Inputs may be any that keep to these rules, and one draw needn't show every extreme that they name: `token_ids`: ids lie in 0 to 524287. In each aligned block of 2 histories (4096 positions) at most 341 ids fall in any one block of 16384 consecutive table rows, and in every such block of histories some block of table rows receives exactly 341.
All inputs are finite; a program needn't handle non-finite values.
Results may differ from a plain program's by a relative error of at most 0.012.
Values may be sent and summed in bfloat16 or wider, within the bound.
A program may use at most 192 MiB of HBM per device.

v0:
```python
import jax
import jax.numpy as jnp
from jax import lax
from jax.sharding import PartitionSpec as P

D = 512
HEADS = 8
FF = 2048


def in_order(blocks, dim):
    blocks = jnp.moveaxis(blocks, 0, dim)
    dims = blocks.shape
    return blocks.reshape(*dims[:dim], dims[dim] * dims[dim + 1], *dims[dim + 2 :])


def sent_to_all(shard, axis):
    copies = jnp.broadcast_to(shard, (lax.axis_size(axis), *shard.shape))
    return lax.all_to_all(copies, axis, split_axis=0, concat_axis=0, tiled=True)


def gathered_copies(shard, axis, dim):
    return in_order(sent_to_all(shard, axis), dim)


def rms_norm(values_f32, gain):
    mean_sq = jnp.mean(values_f32 * values_f32, axis=-1, keepdims=True)
    return values_f32 * lax.rsqrt(mean_sq + 1e-06) * gain


def local(token_ids, lengths, table, attn_gain, w_qkv, w_out, mlp_gain, w_in, w_down):
    batch_dev, quarter = token_ids.shape
    col_count = lax.axis_size("cols")
    row_count = lax.axis_size("rows")
    full_len = quarter * col_count
    block_rows, col_width = table.shape
    zero_bf = jnp.zeros((), jnp.bfloat16)
    own_ids = gathered_copies(token_ids, "cols", 1)
    flat_ids = own_ids.reshape(-1)
    token_count = flat_ids.shape[0]
    capacity = 8 * token_count // (3 * row_count)
    owner_block = flat_ids // block_rows
    onehot = (owner_block[:, None] == jnp.arange(row_count, dtype=jnp.int32)[None, :]).astype(
        jnp.int32
    )
    slot_rank = jnp.sum((jnp.cumsum(onehot, axis=0) - 1) * onehot, axis=1)
    slot_index = owner_block * capacity + slot_rank
    requests = jnp.full((row_count * capacity,), -1, jnp.int32)
    requests = (
        requests.at[slot_index]
        .set(flat_ids - owner_block * block_rows)
        .reshape(row_count, capacity)
    )
    asked = lax.all_to_all(requests, "rows", split_axis=0, concat_axis=0, tiled=True)
    looked = jnp.take(table, jnp.maximum(asked, 0), axis=0)
    looked = jnp.where((asked >= 0)[..., None], looked, zero_bf)
    returned = lax.all_to_all(looked, "rows", split_axis=0, concat_axis=0, tiled=True)
    embedded = returned.reshape(row_count * capacity, col_width)[slot_index]
    embedded = embedded.reshape(batch_dev, full_len, col_width)
    sequence = lax.all_to_all(embedded, "cols", split_axis=1, concat_axis=2, tiled=True)
    residual = sequence.astype(jnp.float32)
    normed = rms_norm(residual, attn_gain).astype(jnp.bfloat16)
    projected = jnp.einsum("bqe,ef->bqf", normed, w_qkv, preferred_element_type=jnp.float32).astype(
        jnp.bfloat16
    )
    head_dim = D // HEADS
    queries = projected[..., :D].reshape(batch_dev, quarter, HEADS, head_dim)
    keys = projected[..., D : 2 * D]
    values = projected[..., 2 * D :]
    query_pos = lax.axis_index("cols") * quarter + jnp.arange(quarter, dtype=jnp.int32)
    running_max = jnp.full((batch_dev, HEADS, quarter), -1e30, jnp.float32)
    key_piece = lax.all_gather(keys, "cols", axis=1, tiled=True)
    value_piece = lax.all_gather(values, "cols", axis=1, tiled=True)
    piece_len = key_piece.shape[1]
    key_heads = key_piece.reshape(batch_dev, piece_len, HEADS, head_dim)
    value_heads = value_piece.reshape(batch_dev, piece_len, HEADS, head_dim)
    scores = (
        jnp.einsum("bqhd,bkhd->bhqk", queries, key_heads, preferred_element_type=jnp.float32)
        * 0.125
    )
    key_pos = jnp.arange(piece_len, dtype=jnp.int32)
    causal = key_pos[None, :] <= query_pos[:, None]
    inside = key_pos[None, :] < lengths[:, None]
    valid = causal[None, None, :, :] & inside[:, None, None, :]
    scores = jnp.where(valid, scores, -1e30)
    new_max = jnp.maximum(running_max, jnp.max(scores, axis=-1))
    probs = jnp.where(valid, jnp.exp(scores - new_max[..., None]), 0.0)
    running_sum = jnp.sum(probs, axis=-1)
    weighted = jnp.einsum(
        "bhqk,bkhd->bhqd",
        probs.astype(jnp.bfloat16),
        value_heads,
        preferred_element_type=jnp.float32,
    )
    final_max, final_sum, weighted = (new_max, running_sum, weighted)
    summed = weighted / final_sum[..., None]
    attended = (
        jnp.transpose(summed, (0, 2, 1, 3)).reshape(batch_dev, quarter, D).astype(jnp.bfloat16)
    )
    hidden = (
        residual + jnp.einsum("bqe,ef->bqf", attended, w_out, preferred_element_type=jnp.float32)
    ).astype(jnp.bfloat16)
    hidden_f32 = hidden.astype(jnp.float32)
    normed_two = rms_norm(hidden_f32, mlp_gain).astype(jnp.bfloat16)
    gate_up = jnp.einsum("bqe,ef->bqf", normed_two, w_in, preferred_element_type=jnp.float32)
    act = (jax.nn.silu(gate_up[..., :FF]) * gate_up[..., FF:]).astype(jnp.bfloat16)
    return (
        hidden_f32 + jnp.einsum("bqf,fe->bqe", act, w_down, preferred_element_type=jnp.float32)
    ).astype(jnp.bfloat16)


def solution(mesh):
    in_specs = (P("rows", "cols"), P("rows"), P("rows", "cols"), P(), P(), P(), P(), P(), P())
    out_specs = P("rows", "cols", None)
    return jax.shard_map(local, mesh=mesh, in_specs=in_specs, out_specs=out_specs, check_vma=False)
```

profile of v0, /device:TPU:1, one launch (start us, length us, event | category | flops | bytes accessed | tf_op | source)
XLA Modules:
  0.0 354.8 jit_solution(12214605746236327788)
XLA Ops:
  6.5 0.8 broadcast_in_dim.67
  7.4 9.8 %all_to_all.28 = s32[4,2,512]{2,1,0:T(2,128)S(1)} all-to-all(s32[4,2,512]{2,1,0:T(2,128)S(1)} %broadcast_in_dim.67), channel_id=1, replica_groups=mesh['rows'=32,'cols'=4] {'cols'}, dimensions={0} | all-to-all | bytes 32768 | tf_op jit(solution)/shard_map/all_to_all | solution.py:19
  17.3 0.1 fusion.33
  17.4 9.2 %reduce-window.6 = s32[32,32,128]{2,1,0:T(8,128)S(1)} reduce-window(s32[32,32,128]{2,1,0:T(8,128)S(1)} %fusion.33, s32[]{:T(128)} %constant.29.clone.1), window={size=1x1x128 pad=0_0x0_0x127_0}, to_apply=%region_0.1 | reduce-window | flops 16646144 | bytes 1048580 | tf_op jit(solution)/shard_map/reduce-window
  26.6 0.8 slice_reduce_fusion
  27.4 0.2 reduce-window.9
  27.6 0.2 add_add_fusion
  27.8 0.3 fusion.31
  28.2 0.1 compare_select_fusion
  28.3 15.5 %scatter_custom_fusion = s32[10912]{0:T(1024)S(1)} fusion(s32[4096]{0:T(1024)S(1)} %bitcast.80, s32[4096]{0:T(1024)S(1)} %get-tuple-element.10, s32[]{:T(128)} %constant.27.clone.1), kind=kCustom, calls=%fused_computation.65 | custom fusion | bytes 43652 | tf_op jit(solution)/shard_map/scatter | solution.py:51
  43.8 0.2 all_to_all.20
  44.0 16.3 %all_to_all.29 = s32[32,1,341]{2,1,0:T(1,128)S(1)} all-to-all(s32[32,1,341]{2,1,0:T(1,128)S(1)} %all_to_all.20), channel_id=1, replica_groups=mesh['rows'=32,'cols'=4] {'rows'}, dimensions={0} | all-to-all | bytes 87296 | tf_op jit(solution)/shard_map/all_to_all | solution.py:54
  60.3 0.1 reshape.255
  60.4 23.7 %gather_fusion = bf16[10912,128]{1,0:T(8,128)(2,1)} fusion(bf16[16384,128]{1,0:T(8,128)(2,1)} %param.11, s32[11264]{0:T(1024)S(1)} %pad_clamp_fusion), kind=kCustom, calls=%fused_computation | custom fusion | bytes 5630592 | tf_op jit(solution)/shard_map/jit(_take)/gather | solution.py:55
  84.1 4.4 %reshape.254 = bf16[32,341,128]{2,1,0:T(8,128)(2,1)} reshape(bf16[10912,128]{1,0:T(8,128)(2,1)} %gather_fusion) | data formatting | bytes 5586944 | tf_op jit(solution)/shard_map/jit(_take)/gather | solution.py:55
  88.6 6.0 %select_select_fusion = bf16[32,341,128]{2,1,0:T(8,128)(2,1)} fusion(bf16[32,341,128]{2,1,0:T(8,128)(2,1)} %reshape.254, pred[32,341]{1,0:T(8,128)(4,1)S(1)} %get-tuple-element.9, pred[32,341]{1,0:T(8,128)(4,1)S(1)} %get-tuple-element.8), kind=kLoop, calls=%fused_computation.21 | loop fusion | flops 2793472 | bytes 5608768 | tf_op jit(solution)/shard_map/jit(_where)/select_n | solution.py:56
  94.6 4.8 %all-to-all-start.2 = ((bf16[32,341,128]{2,1,0:T(8,128)(2,1)}), bf16[32,341,128]{2,1,0:T(8,128)(2,1)}, u32[]{:S(2)}, u32[]{:S(2)}) async-start(bf16[32,341,128]{2,1,0:T(8,128)(2,1)} %select_select_fusion), calls=%async_computation.2 | async-start | bytes 5636096 | tf_op jit(solution)/shard_map/all_to_all | solution.py:57
  99.4 0.0 all-gather.3.cloned.1.call-start
  99.4 36.1 %all-to-all-done.2 = bf16[32,341,128]{2,1,0:T(8,128)(2,1)} async-done(((bf16[32,341,128]{2,1,0:T(8,128)(2,1)}), bf16[32,341,128]{2,1,0:T(8,128)(2,1)}, u32[]{:S(2)}, u32[]{:S(2)}) %all-to-all-start.2) | async-done | bytes 2793504 | tf_op jit(solution)/shard_map/all_to_all | solution.py:57
  135.5 4.4 %reshape.246 = bf16[10912,128]{1,0:T(8,128)(2,1)} reshape(bf16[32,341,128]{2,1,0:T(8,128)(2,1)} %all-to-all-done.2) | data formatting | bytes 5586944 | tf_op jit(solution)/shard_map/reshape | solution.py:58
  139.9 13.2 %gather_fusion.1 = bf16[4096,128]{1,0:T(8,128)(2,1)S(1)} fusion(bf16[10912,128]{1,0:T(8,128)(2,1)} %reshape.246, s32[4096]{0:T(1024)S(1)} %broadcast_clamp_fusion), kind=kCustom, calls=%fused_computation.1 | custom fusion | bytes 2113536 | tf_op jit(solution)/shard_map/gather | solution.py:58
  153.1 8.7 %copy.63 = bf16[2,2048,128]{2,0,1:T(2,128)(2,1)S(1)} copy(bf16[2,2048,128]{2,1,0:T(8,128)(2,1)S(1)} %bitcast.73) | data formatting | bytes 2097152 | tf_op jit(solution)/shard_map/reshape | solution.py:59
  161.8 14.9 %all_to_all.30 = bf16[2,2048,128]{2,0,1:T(2,128)(2,1)S(1)} all-to-all(bf16[2,2048,128]{2,0,1:T(2,128)(2,1)S(1)} %copy.63), channel_id=1, replica_groups=mesh['rows'=32,'cols'=4] {'cols'}, dimensions={1} | all-to-all | bytes 2097152 | tf_op jit(solution)/shard_map/all_to_all | solution.py:60
  176.7 1.5 copy_convert_fusion
  178.2 2.9 copy.65
  181.2 0.6 multiply_reduce_fusion
  181.9 1.8 fusion.18
  183.7 3.2 convolution_convert_fusion
  187.0 1.7 fusion.44
  188.6 0.0 all-gather.3.cloned.1.call-update
  188.7 0.0 all-gather.5.cloned.1.call-start
  188.7 0.1 iota_compare_fusion.3
  188.8 0.7 iota_compare_fusion
  189.5 2.6 broadcast_and_fusion
  192.1 1.3 copy.67
  193.4 0.0 all-gather.5.cloned.1.call-update
  193.4 43.3 %all-gather.3.cloned.1.call-done = bf16[2,2048,512]{2,1,0:T(8,128)(2,1)} async-done(((bf16[2,512,512]{2,1,0:T(8,128)(2,1)}), bf16[2,2048,512]{2,1,0:T(8,128)(2,1)}) %all-gather.3.cloned.1.call-update) | async-done | bytes 4194320 | tf_op jit(solution)/shard_map/all_gather | solution.py:72
  236.7 6.3 %copy.68 = bf16[2,2048,512]{1,2,0:T(8,128)(2,1)} copy(bf16[2,2048,512]{2,1,0:T(8,128)(2,1)} %all-gather.3.cloned.1.call-done) | data formatting | bytes 8388608 | tf_op jit(solution)/shard_map/all_gather | solution.py:72
  243.0 27.9 %fusion = (f32[2,8,512]{2,1,0:T(8,128)S(1)}, f32[2,8,512,2048]{3,2,1,0:T(8,128)}) fusion(pred[2,512,2048]{2,1,0:T(8,128)(4,1)} %broadcast_and_fusion, bf16[2,512,8,64]{1,3,2,0:T(8,128)(2,1)} %bitcast.72, bf16[2,2048,8,64]{1,3,2,0:T(8,128)(2,1)} %bitcast.70), kind=kOutput, calls=%fused_computation.5 | convolution fusion | flops 2197807104 | bytes 74481664 | tf_op jit(solution)/shard_map/bqhd,bkhd->bhqk/dot_general | solution.py:78
  271.0 22.5 %fusion.1 = f32[2,8,512]{2,1,0:T(8,128)S(1)} fusion(f32[2,8,512,2048]{3,2,1,0:T(8,128)} %get-tuple-element.15, f32[2,8,512]{2,1,0:T(8,128)S(1)} %broadcast_maximum_fusion, pred[2,512,2048]{2,1,0:T(8,128)(4,1)S(1)} %copy-done.1), kind=kLoop, calls=%fused_computation.6 | loop fusion | flops 83877888 | bytes 69271552 | tf_op jit(solution)/shard_map/reduce_sum | solution.py:88
  293.4 0.0 all-gather.5.cloned.1.call-done
  293.5 6.3 %copy.69 = bf16[2,2048,512]{1,2,0:T(8,128)(2,1)} copy(bf16[2,2048,512]{2,1,0:T(8,128)(2,1)} %all-gather.5.cloned.1.call-done) | data formatting | bytes 8388608 | tf_op jit(solution)/shard_map/all_gather | solution.py:73
  299.8 27.0 %fusion.16 = bf16[2,512,8,64]{1,3,2,0:T(8,128)(2,1)S(1)} fusion(bf16[2,2048,8,64]{1,3,2,0:T(8,128)(2,1)} %bitcast.74, f32[2,8,512,2048]{3,2,1,0:T(8,128)} %get-tuple-element.15, f32[2,8,512]{2,1,0:T(8,128)S(1)} %broadcast_maximum_fusion, pred[2,512,2048]{2,1,0:T(8,128)(4,1)} %broadcast_and_fusion, f32[2,512,8]{1,2,0:T(8,128)S(1)} %bitcast.84), kind=kOutput, calls=%fused_computation.28 | convolution fusion | flops 2232418304 | bytes 74514432 | tf_op jit(solution)/shard_map/bhqk,bkhd->bhqd/dot_general | solution.py:89
  326.8 2.7 fusion.11
  329.5 0.3 copy-done.4
  329.7 8.3 %fusion.7 = f32[2,512,4096]{2,1,0:T(8,128)} fusion(bf16[512,4096]{1,0:T(8,128)(2,1)S(1)} %copy-done.4, bf16[2,512,512]{1,2,0:T(8,128)(2,1)S(1)} %get-tuple-element.17, f32[512]{0:T(512)S(1)} %copy-done.5, f32[2,512]{1,0:T(2,128)S(1)} %add_rsqrt_fusion), kind=kOutput, calls=%fused_computation.12 | convolution fusion | flops 4297064448 | bytes 22026240 | tf_op jit(solution)/shard_map/bqe,ef->bqf/dot_general | solution.py:105
  338.1 8.6 %fusion.14 = bf16[2,512,512]{1,2,0:T(8,128)(2,1)S(1)} fusion(bf16[2,512,512]{1,2,0:T(8,128)(2,1)S(1)} %get-tuple-element.17, bf16[2048,512]{1,0:T(8,128)(2,1)S(1)} %copy-done, f32[2,512,4096]{2,1,0:T(8,128)} %fusion.7), kind=kOutput, calls=%fused_computation.25 | convolution fusion | flops 2161639424 | bytes 20971520 | tf_op jit(solution)/shard_map/bqf,fe->bqe/dot_general | solution.py:108
  346.6 1.3 copy.74
  (27 shorter events, 0.2 us)
Async XLA Ops:
  6.5 331.5 %copy-start = (bf16[2048,512]{1,0:T(8,128)(2,1)S(1)}, bf16[2048,512]{1,0:T(8,128)(2,1)}, u32[]{:S(2)}) copy-start(bf16[2048,512]{1,0:T(8,128)(2,1)} %param.17) | copy-start | bytes 6291460
  94.6 40.9 %all-to-all-start.2 = ((bf16[32,341,128]{2,1,0:T(8,128)(2,1)}), bf16[32,341,128]{2,1,0:T(8,128)(2,1)}, u32[]{:S(2)}, u32[]{:S(2)}) async-start(bf16[32,341,128]{2,1,0:T(8,128)(2,1)} %select_select_fusion), calls=%async_computation.2 | async-start | bytes 5636096 | tf_op jit(solution)/shard_map/all_to_all | solution.py:57
  99.4 137.4 %all-gather.3.cloned.1.call-start = ((), (), s32[]{:S(2)}) async-start(), calls=%async_computation.4 | async-start | bytes 5242880 | tf_op jit(solution)/shard_map/all_gather | solution.py:72
  176.7 5.1 %copy-start.2 = (f32[512]{0:T(512)S(1)}, f32[512]{0:T(512)}, u32[]{:S(2)}) copy-start(f32[512]{0:T(512)} %param.12) | copy-start | bytes 6148
  186.9 1.8 copy-start.3
  188.7 104.8 %all-gather.5.cloned.1.call-start = ((), (), s32[]{:S(2)}) async-start(), calls=%async_computation.5 | async-start | bytes 5242880 | tf_op jit(solution)/shard_map/all_gather | solution.py:73
  243.0 27.9 %copy-start.1 = (pred[2,512,2048]{2,1,0:T(8,128)(4,1)S(1)}, pred[2,512,2048]{2,1,0:T(8,128)(4,1)}, u32[]{:S(2)}) copy-start(pred[2,512,2048]{2,1,0:T(8,128)(4,1)} %broadcast_and_fusion) | copy-start | bytes 6291460
  326.7 3.0 copy-start.4
  326.8 3.0 copy-start.5
Sparse Core Ops, SparseCore 0:
  188.8 47.9 all-gather.2
  238.4 48.5 all-gather.4
where the time goes:
time: 356 us; the launch traced here: 355 us
  local copies, waits for them, and re-layouts  92 us (26%)
  waiting for transfers between devices  79.4 us (22%)
  matrix products  77.7 us (22%)
  other arithmetic  46 us (13%)
  blocking collectives  41.1 us (12%)
  between operations  13.7 us (4%)
  starting transfers between devices  4.87 us (1%)
    all_gather x1, waiting for transfers between devices, local(): key_piece = lax.all_gather(keys, 'cols', axis=1, tiled=True)  43.3 us
    all_to_all x1, waiting for transfers between devices, local(): lax.all_to_all(looked, 'rows', split_axis=0, concat_axis=0, tiled=True)  36.1 us
    gather x2, local copies, waits for them, and re-layouts, local(): looked = jnp.take(table, jnp.maximum(asked, 0), axis=0)  28.1 us
    dot_general x1, matrix products, local(): jnp.einsum('bqhd,bkhd->bhqk', queries, key_heads, preferred_element_type=...  27.9 us
    dot_general x1, matrix products, local(): jnp.einsum('bhqk,bkhd->bhqd', probs.astype(jnp.bfloat16), value_heads, pr...  27 us
    reduce_sum x1, other arithmetic, local(): running_sum = jnp.sum(probs, axis=-1)  22.5 us
    all_to_all x1, blocking collectives, local(): lax.all_to_all(requests, 'rows', split_axis=0, concat_axis=0, tiled=True)  16.3 us
    scatter x1, local copies, waits for them, and re-layouts, local(): requests = requests.at[slot_index].set(flat_ids - owner_block * block_row...  15.5 us
  transfers between devices with their start and end apart: 3, of which 2 were waited for; matrix products, arithmetic and copies ran while one was open for 17% of the time, Pallas kernels for 0%

commit v1 on v0

v1 whole, which is shorter than its diff:
```python
import functools

import jax
import jax.numpy as jnp
from jax import lax
from jax.experimental import pallas as pl
from jax.experimental.pallas import tpu as pltpu
from jax.sharding import PartitionSpec as P

D = 512
FF = 2048
CAP = 344
BF = jnp.bfloat16
F32 = jnp.float32
MESH = pl.DeviceIdType.MESH
ANY = pl.BlockSpec(memory_space=pl.ANY)
VM = pl.BlockSpec(memory_space=pltpu.VMEM)
SM = pl.BlockSpec(memory_space=pltpu.SMEM)
LOG2E = 1.4426950408889634
NEG = -1e30


def dot(a, b):
    return jnp.dot(a, b, preferred_element_type=F32)


def dot_t(a, b):
    return lax.dot_general(a, b, (((1,), (1,)), ((), ())), preferred_element_type=F32)


def place():
    r, z = lax.axis_index("rows"), lax.axis_index("cols")
    return r, z, r // 8, (r // 2) % 4, r % 2


def greet(devices):
    barrier = pltpu.get_barrier_semaphore()
    for device in devices:
        pl.semaphore_signal(barrier, inc=1, device_id=device, device_id_type=MESH)
    pl.semaphore_wait(barrier, len(devices))


def remote(src, dst, send_sem, recv_sem, device):
    return pltpu.make_async_remote_copy(
        src_ref=src, dst_ref=dst, send_sem=send_sem, recv_sem=recv_sem,
        device_id=device, device_id_type=MESH)


def params(collective_id=None, vmem=60):
    kw = {}
    if collective_id is not None:
        kw = dict(collective_id=collective_id, has_side_effects=True)
    return pltpu.CompilerParams(vmem_limit_bytes=vmem * 2**20, **kw)


def ids_kernel(ids_ref, out_ref, send_sem, recv_sem):
    r, z, _, _, _ = place()
    peers = [(r, (z + s) % 4) for s in (1, 2, 3)]
    greet(peers)
    copies = []
    for s, device in enumerate(peers):
        copy = remote(ids_ref, out_ref.at[z], send_sem.at[s], recv_sem.at[s], device)
        copy.start()
        copies.append(copy)
    out_ref[z] = ids_ref[...]
    for copy in copies:
        copy.wait()


def request_kernel(len_ref, ids_ref, msg_ref, slot_ref):
    ids = ids_ref[...]
    owner = ids >> 14
    low, high = (ids & 127).astype(F32), ((ids >> 7) & 127).astype(F32)
    before = (lax.broadcasted_iota(jnp.int32, (128, 128), 0)
              < lax.broadcasted_iota(jnp.int32, (128, 128), 1)).astype(F32).astype(BF)
    above = (lax.broadcasted_iota(jnp.int32, (32, 32), 1)
             < lax.broadcasted_iota(jnp.int32, (32, 32), 0)).astype(F32).astype(BF)
    ones = jnp.ones((128, 128), BF)
    rank = jnp.zeros((32, 128), F32)
    for o in range(32):
        hit = owner == o
        one = jnp.where(hit, 1.0, 0.0).astype(BF)
        prior = dot(one, before) + dot(dot(above, one).astype(BF), ones)
        rank = rank + jnp.where(hit, prior, 0.0)
    rank_i = rank.astype(jnp.int32)
    slot_ref[...] = owner * CAP + rank_i
    owners = lax.broadcasted_iota(jnp.int32, (32, 128), 0)
    ks = lax.broadcasted_iota(jnp.int32, (384, 128), 0)
    acc = jnp.zeros((64, 384), F32)
    count = jnp.zeros((32, 128), F32)
    for a in range(32):
        hit = owners == owner[a : a + 1, :]
        count = count + jnp.where(hit, 1.0, 0.0)
        left = jnp.concatenate(
            [jnp.where(hit, low[a : a + 1, :], 0.0), jnp.where(hit, high[a : a + 1, :], 0.0)], axis=0)
        right = jnp.where(ks == rank_i[a : a + 1, :], 1.0, 0.0)
        acc = acc + dot_t(left.astype(BF), right.astype(BF))
    req = (acc[32:] * 128.0 + acc[:32]).astype(jnp.int32)
    for j in range(3):
        msg_ref[:, j, :] = req[:, 128 * j : 128 * j + 128]
    total = jnp.sum(count, axis=1, keepdims=True).astype(jnp.int32)
    lane = lax.broadcasted_iota(jnp.int32, (32, 128), 1)
    tail = jnp.where(lane == 0, total, 0)
    tail = jnp.where(lane == 1, len_ref[0], jnp.where(lane == 2, len_ref[1], tail))
    msg_ref[:, 3, :] = tail


def ask_kernel(msg_ref, out_ref, send_sem, recv_sem):
    r, z, _, _, _ = place()
    peers = [((r + s) % 32, z) for s in range(1, 32)]
    greet(peers)
    copies = []
    for s, device in enumerate(peers):
        copy = remote(msg_ref.at[device[0]], out_ref.at[r], send_sem.at[s], recv_sem.at[s], device)
        copy.start()
        copies.append(copy)
    out_ref[r] = msg_ref[r]
    for copy in copies:
        copy.wait()


def lookup_kernel(asked_ref, table_ref, out_ref, wide, stage):
    def widen(i, _):
        rows = pl.ds(pl.multiple_of(i * 256, 256), 256)
        wide[rows, :] = table_ref[rows, :].astype(F32)
        return 0

    lax.fori_loop(0, 64, widen, 0)
    stage[...] = jnp.zeros_like(stage)

    def block(p, _):
        def some(j, _):
            base = j * 16
            row, col = base // 128, lax.rem(base, 128)
            for i in range(16):
                stage[pl.ds(base + i, 1), :] = wide[pl.ds(asked_ref[p, row, col + i], 1), :]
            return 0

        lax.fori_loop(0, (asked_ref[p, 3, 0] + 15) // 16, some, 0)
        out_ref[p] = stage[0:CAP, :].astype(BF)
        return 0

    lax.fori_loop(0, 32, block, 0)


def routes():
    out = []
    for dy in range(4):
        for dx in range(4):
            for dk in range(2):
                if dx == dy == dk == 0:
                    continue
                side = 1 if dk == 0 else 3
                hop = None
                if dx == 2 or dy == 2:
                    hop = (side if dy == 2 else 0, side if dx == 2 else 0)
                out.append((dy, dx, dk, hop))
    key = lambda f: (f[3] is None, (f[0] * 5 + f[1] * 3 + f[2] * 7) % 11)
    return sorted(out, key=key)


def back_kernel(src_ref, out_ref, relay, own, send_sem, recv_sem, hop_send, hop_recv, own_sem):
    r, z, y, x, k = place()

    def row(dy, dx, dk):
        return (((y + dy) % 4) * 4 + (x + dx) % 4) * 2 + (k + dk) % 2

    flows = routes()
    hops = [f for f in flows if f[3] is not None]
    direct = [f for f in flows if f[3] is None]
    greet([((r + s) % 32, z) for s in range(1, 32)])
    first, final = [], []
    for i, (dy, dx, dk, (hy, hx)) in enumerate(hops):
        copy = remote(src_ref.at[row(dy, dx, dk)], relay.at[i], hop_send.at[i], hop_recv.at[i], (row(hy, hx, 0), z))
        copy.start()
        first.append(copy)
    for i, (dy, dx, dk, _) in enumerate(direct):
        copy = remote(src_ref.at[row(dy, dx, dk)], out_ref.at[r], send_sem.at[i], recv_sem.at[i], (row(dy, dx, dk), z))
        copy.start()
        final.append(copy)
    take = pltpu.make_async_copy(src_ref.at[r], own, own_sem)
    take.start()
    take.wait()
    put = pltpu.make_async_copy(own, out_ref.at[r], own_sem)
    put.start()
    for i, (dy, dx, dk, (hy, hx)) in enumerate(hops):
        first[i].wait_recv()
        n = len(direct) + i
        copy = remote(relay.at[i], out_ref.at[row(-hy, -hx, 0)], send_sem.at[n], recv_sem.at[n],
                      (row(dy - hy, dx - hx, dk), z))
        copy.start()
        final.append(copy)
    put.wait()
    for copy in first:
        copy.wait_send()
    for copy in final:
        copy.wait()


def compact_kernel(slot_ref, src_ref, out_ref, wide, stage):
    def widen(i, _):
        wide[pl.ds(pl.multiple_of(i * CAP, 8), CAP), :] = src_ref[i].astype(F32)
        return 0

    lax.fori_loop(0, 32, widen, 0)

    def some(j, _):
        a, col = j // 8, lax.rem(j, 8) * 16
        h, zz, jj = lax.rem(a, 8) // 4, a // 8, lax.rem(a, 4)
        base = h * 2048 + zz * 512 + jj * 128 + col
        for i in range(16):
            stage[pl.ds(base + i, 1), :] = wide[pl.ds(slot_ref[a, col + i], 1), :]
        return 0

    lax.fori_loop(0, 256, some, 0)

    def narrow(i, _):
        rows = pl.ds(pl.multiple_of(i * 256, 256), 256)
        out_ref[rows, :] = stage[rows, :].astype(BF)
        return 0

    lax.fori_loop(0, 16, narrow, 0)


def spread_kernel(src_ref, out_ref, relay, send_sem, relay_send, relay_recv, recv_sem, pass_send, pass_recv,
                  own_send, own_recv, own_sem, bounce):
    r, z, y, x, k = place()
    base = r - k
    other = (base + 1 - k, z)
    up, down = (z + 1) % 4, (z + 3) % 4
    holder = z // 2

    def part(i):
        return pl.ds(1024 * i, 1024)

    mine = part(0) if False else pl.ds(pl.multiple_of(1024 * k, 1024), 1024)
    theirs = pl.ds(pl.multiple_of(1024 * (1 - k), 1024), 1024)
    peers = [(base + 1 - k, z)]
    for kk in range(2):
        for s in (1, 3):
            peers.append((base + kk, (z + s) % 4))
    greet(peers)

    def far(h, half):
        step = 1 if half == 0 else 3
        return remote(src_ref.at[h, part(half)], relay, relay_send, relay_recv, (base + half, (z + step) % 4))

    def near(h, half, step):
        return remote(src_ref.at[h, part(half)], out_ref.at[z, part(half)],
                      send_sem.at[step // 2, half], recv_sem.at[step // 2], (base + half, (z + step) % 4))

    def own(h):
        return remote(src_ref.at[h], out_ref.at[z], own_send, own_recv, other)

    def inner(h):
        return (pltpu.make_async_copy(src_ref.at[h], bounce, own_sem),
                pltpu.make_async_copy(bounce, out_ref.at[z], own_sem))

    dist = [(2 * k + h - z) % 4 for h in range(2)]
    for h in range(2):
        @pl.when(dist[h] == 2)
        def _():
            for half in range(2):
                remote(src_ref.at[h, part(half)], relay, relay_send.at[half], relay_recv,
                       (base + half, up if half == 0 else down)).start()

    for h in range(2):
        for step in (1, 3):
            @pl.when(dist[h] == step)
            def _():
                for half in range(2):
                    near(h, half, step).start()

        @pl.when(dist[h] == 0)
        def _():
            own(h).start()
            take, put = inner(h)
            take.start()
            take.wait()
            put.start()

    back = jnp.where(k == 0, down, up)
    ahead = jnp.where(k == 0, up, down)
    relayed = remote(relay, out_ref.at[back, mine], pass_send.at[3], recv_sem.at[2], (r, ahead))
    remote(src_ref.at[0, part(0)], relay, relay_send.at[0], relay_recv, (r, ahead)).wait_recv()
    relayed.start()
    passed = []
    for i, source in enumerate((down, up, (z + 2) % 4)):
        got = out_ref.at[source, mine]
        remote(got, got, send_sem.at[0, 0], recv_sem.at[i], other).wait_recv()
        copy = remote(got, got, pass_send.at[i], pass_recv.at[i], other)
        copy.start()
        passed.append(copy)

    for i, copy in enumerate(passed):
        copy.wait_send()
        source = (down, up, (z + 2) % 4)[i]
        remote(out_ref.at[source, theirs], out_ref.at[source, theirs], pass_send.at[i], pass_recv.at[i],
               other).wait_recv()
    relayed.wait_send()

    for h in range(2):
        @pl.when(dist[h] == 2)
        def _():
            for half in range(2):
                remote(src_ref.at[h, part(half)], relay, relay_send.at[half], relay_recv,
                       (base + half, up if half == 0 else down)).wait_send()
        for step in (1, 3):
            @pl.when(dist[h] == step)
            def _():
                for half in range(2):
                    near(h, half, step).wait_send()

        @pl.when(dist[h] == 0)
        def _():
            own(h).wait_send()
            inner(h)[1].wait()

    @pl.when(k != holder)
    def _():
        own(0).wait_recv()


def layer_kernel(len_ref, x_ref, gain_ref, wqkv_ref, wout_ref, gain2_ref, win_hbm, wdown_hbm, out_ref,
                 nrm, qs, ke, ko, ve, vo, sc, att, win_ref, wdown_ref, sems):
    k = lax.axis_index("rows") % 2
    get_in = pltpu.make_async_copy(win_hbm, win_ref, sems.at[0])
    get_down = pltpu.make_async_copy(wdown_hbm, wdown_ref, sems.at[1])
    get_in.start()
    get_down.start()
    length = len_ref[0]
    quarters = (k, 3 - k)

    def norm(i, _):
        rows = pl.ds(pl.multiple_of(i * 256, 256), 256)
        parts = [x_ref[c, rows, :].astype(F32) for c in range(4)]
        square = parts[0] * parts[0]
        for part in parts[1:]:
            square = square + part * part
        scale = lax.rsqrt(jnp.sum(square, axis=1, keepdims=True) * (1.0 / D) + 1e-6)
        for c in range(4):
            nrm[rows, 128 * c : 128 * c + 128] = (parts[c] * scale * gain_ref[:, 128 * c : 128 * c + 128]).astype(BF)
        return 0

    lax.fori_loop(0, 8, norm, 0)

    def project(i, _):
        rows = pl.ds(pl.multiple_of(i * 256, 256), 256)
        here = nrm[rows, :]
        keys = dot(here, wqkv_ref[:, D : 2 * D])
        vals = dot(here, wqkv_ref[:, 2 * D :])
        lane = lax.broadcasted_iota(jnp.int32, (256, 128), 1)
        pos = lax.broadcasted_iota(jnp.int32, (256, 128), 0) + i * 256
        bias = jnp.where(pos < length, 0.0, NEG)
        for c in range(4):
            cols = slice(128 * c, 128 * c + 128)
            ke[rows, cols] = jnp.where(lane == 64, bias, keys[:, cols]).astype(BF)
            ko[rows, cols] = jnp.where(lane == 0, bias, keys[:, cols]).astype(BF)
            ve[rows, cols] = jnp.where(lane == 64, 1.0, vals[:, cols]).astype(BF)
            vo[rows, cols] = jnp.where(lane == 0, 1.0, vals[:, cols]).astype(BF)
        return 0

    lax.fori_loop(0, 8, project, 0)
    for a in range(2):
        rows = pl.ds(pl.multiple_of(quarters[a] * 512, 512), 512)
        qs[512 * a : 512 * a + 512, :] = (dot(nrm[rows, :], wqkv_ref[:, :D]) * (0.125 * LOG2E)).astype(BF)

    def attend(kk):
        def heads(hp, _):
            cols = pl.ds(pl.multiple_of(hp * 128, 128), 128)
            lane = lax.broadcasted_iota(jnp.int32, (256, 128), 1)
            tri = (lax.broadcasted_iota(jnp.int32, (256, 256), 1)
                   <= lax.broadcasted_iota(jnp.int32, (256, 256), 0))
            for a, quarter in enumerate((kk, 3 - kk)):
                for j in range(2):
                    n = 2 * quarter + j + 1
                    at = 512 * a + 256 * j
                    q = qs[at : at + 256, cols].astype(F32)
                    accs = []
                    for odd in range(2):
                        kref, vref = (ko, vo) if odd else (ke, ve)
                        if odd:
                            qa = jnp.where(lane >= 64, q, jnp.where(lane == 0, 1.0, 0.0)).astype(BF)
                        else:
                            qa = jnp.where(lane < 64, q, jnp.where(lane == 64, 1.0, 0.0)).astype(BF)
                        top = None
                        for c in range(n):
                            s = dot_t(qa, kref[256 * c : 256 * c + 256, cols])
                            if c == n - 1:
                                s = jnp.where(tri, s, NEG)
                            sc[odd, c] = s
                            m = jnp.maximum(s[:, :128], s[:, 128:])
                            top = m if top is None else jnp.maximum(top, m)
                        top = jnp.max(top, axis=1, keepdims=True)
                        acc = jnp.zeros((256, 128), F32)
                        for c in range(n):
                            p = jnp.exp2(sc[odd, c] - top).astype(BF)
                            acc = acc + dot(p, vref[256 * c : 256 * c + 256, cols])
                        accs.append(acc)
                    even = accs[0] / accs[0][:, 64:65]
                    odd_ = accs[1] / accs[1][:, 0:1]
                    att[at : at + 256, cols] = jnp.where(lane < 64, even, odd_).astype(BF)
            return 0

        lax.fori_loop(0, 4, heads, 0)

    for kk in range(2):
        @pl.when(k == kk)
        def _():
            attend(kk)

    get_in.wait()
    get_down.wait()

    def mlp(i, _):
        rows = pl.ds(pl.multiple_of(i * 256, 256), 256)
        quarter = jnp.where(i < 2, quarters[0], quarters[1])
        src = pl.ds(pl.multiple_of(quarter * 512 + lax.rem(i, 2) * 256, 256), 256)
        resid = jnp.concatenate([x_ref[c, src, :].astype(F32) for c in range(4)], axis=1)
        hidden = (resid + dot(att[rows, :], wout_ref[...])).astype(BF).astype(F32)
        scale = lax.rsqrt(jnp.mean(hidden * hidden, axis=1, keepdims=True) + 1e-6)
        normed = (hidden * scale * gain2_ref[...]).astype(BF)
        out = hidden
        for f in range(4):
            cols = slice(512 * f, 512 * f + 512)
            up_cols = slice(FF + 512 * f, FF + 512 * f + 512)
            gate = dot(normed, win_ref[:, cols])
            up = dot(normed, win_ref[:, up_cols])
            act = (gate / (1.0 + jnp.exp(-gate)) * up).astype(BF)
            out = out + dot(act, wdown_ref[cols, :])
        out_ref[rows, :] = out.astype(BF)
        return 0

    lax.fori_loop(0, 4, mlp, 0)


def give_kernel(src_ref, out_ref, relay, bounce, send_sem, far_send, relay_recv, recv_sem, pass_send, own_sem):
    r, z, y, x, k = place()
    base = r - k
    up, down = (z + 1) % 4, (z + 3) % 4
    across = (z + 2) % 4
    holder, slot = z // 2, z % 2
    peers = [(base + 1 - k, z)]
    for kk in range(2):
        for s in (1, 3):
            peers.append((base + kk, (z + s) % 4))
    greet(peers)

    def worker(q):
        return jnp.where((q == 0) | (q == 3), 0, 1)

    def piece(q, rows=pl.ds(0, 512)):
        at = jnp.where(q < 2, 0, 1)
        return src_ref.at[at, rows]

    halves = (pl.ds(0, 256), pl.ds(256, 256))
    via = (up, down)

    def far(half):
        return remote(piece(across, halves[half]), relay, far_send.at[half], relay_recv, (r, via[half]))

    def near(i):
        return remote(piece(via[i]), out_ref.at[slot], send_sem.at[i], recv_sem.at[slot, 0], (base + holder, via[i]))

    def own():
        return remote(piece(z), out_ref.at[slot], send_sem.at[2], recv_sem.at[slot, 0], (base + 1 - k, z))

    @pl.when(worker(across) == k)
    def _():
        far(0).start()
        far(1).start()

    for i in range(2):
        @pl.when(worker(via[i]) == k)
        def _():
            near(i).start()

    @pl.when((worker(z) == k) & (holder != k))
    def _():
        own().start()

    @pl.when((worker(z) == k) & (holder == k))
    def _():
        take = pltpu.make_async_copy(piece(z), bounce, own_sem)
        take.start()
        take.wait()
        put = pltpu.make_async_copy(bounce, out_ref.at[slot], own_sem)
        put.start()
        put.wait()

    def passing(half):
        source, target = (down, up) if half == 0 else (up, down)
        return remote(relay, out_ref.at[source % 2, halves[half]], pass_send, recv_sem.at[source % 2, half],
                      (base + source // 2, target))

    for half in range(2):
        @pl.when(worker(via[half]) == k)
        def _():
            far(half).wait_recv()
            passing(half).start()
            passing(half).wait_send()

    for h in range(2):
        source = 2 * k + h
        dist = (source - z) % 4
        @pl.when((dist == 1) | (dist == 3) | ((dist == 0) & (worker(z) != k)))
        def _():
            remote(src_ref.at[0], out_ref.at[h], send_sem.at[0], recv_sem.at[h, 0], (base + 1 - k, z)).wait_recv()
        @pl.when(dist == 2)
        def _():
            for half in range(2):
                remote(src_ref.at[0, halves[half]], out_ref.at[h, halves[half]], send_sem.at[0],
                       recv_sem.at[h, half], (base + 1 - k, z)).wait_recv()

    @pl.when(worker(across) == k)
    def _():
        far(0).wait_send()
        far(1).wait_send()

    for i in range(2):
        @pl.when(worker(via[i]) == k)
        def _():
            near(i).wait_send()

    @pl.when((worker(z) == k) & (holder != k))
    def _():
        own().wait_send()


def local(token_ids, lengths, table, attn_gain, w_qkv, w_out, mlp_gain, w_in, w_down):
    dma = pltpu.SemaphoreType.DMA
    ids = pl.pallas_call(
        ids_kernel,
        out_shape=jax.ShapeDtypeStruct((4, 8, 128), jnp.int32),
        in_specs=[VM], out_specs=VM,
        scratch_shapes=[dma((3,)), dma((3,))],
        compiler_params=params(1),
    )(token_ids.reshape(8, 128))
    msg, slot = pl.pallas_call(
        request_kernel,
        out_shape=[jax.ShapeDtypeStruct((32, 4, 128), jnp.int32), jax.ShapeDtypeStruct((32, 128), jnp.int32)],
        in_specs=[SM, VM], out_specs=[VM, VM],
        compiler_params=params(),
    )(lengths, ids.reshape(32, 128))
    asked = pl.pallas_call(
        ask_kernel,
        out_shape=jax.ShapeDtypeStruct((32, 4, 128), jnp.int32),
        in_specs=[VM], out_specs=VM,
        scratch_shapes=[dma((31,)), dma((31,))],
        compiler_params=params(2),
    )(msg)
    looked = pl.pallas_call(
        lookup_kernel,
        out_shape=jax.ShapeDtypeStruct((32, CAP, 128), BF),
        in_specs=[SM, VM], out_specs=VM,
        scratch_shapes=[pltpu.VMEM((16384, 128), F32), pltpu.VMEM((352, 128), F32)],
        compiler_params=params(),
    )(asked, table)
    returned = pl.pallas_call(
        back_kernel,
        out_shape=jax.ShapeDtypeStruct((32, CAP, 128), BF),
        in_specs=[ANY], out_specs=ANY,
        scratch_shapes=[pltpu.VMEM((14, CAP, 128), BF), pltpu.VMEM((CAP, 128), BF), dma((31,)), dma((31,)),
                        dma((14,)), dma((14,)), dma],
        compiler_params=params(3),
    )(looked)
    embedded = pl.pallas_call(
        compact_kernel,
        out_shape=jax.ShapeDtypeStruct((4096, 128), BF),
        in_specs=[SM, VM], out_specs=VM,
        scratch_shapes=[pltpu.VMEM((32 * CAP, 128), F32), pltpu.VMEM((4096, 128), F32)],
        compiler_params=params(),
    )(slot, returned)
    full = pl.pallas_call(
        spread_kernel,
        out_shape=jax.ShapeDtypeStruct((4, 2048, 128), BF),
        in_specs=[ANY], out_specs=ANY,
        scratch_shapes=[pltpu.VMEM((1024, 128), BF), dma((2, 2)), dma((2,)), dma, dma((3,)), dma((4,)), dma((3,)),
                        dma, dma, dma, pltpu.VMEM((2048, 128), BF)],
        compiler_params=params(4),
    )(embedded.reshape(2, 2048, 128))
    r, z = lax.axis_index("rows"), lax.axis_index("cols")
    length = lax.dynamic_slice(asked, (r - r % 2 + z // 2, 3, 1 + z % 2), (1, 1, 1)).reshape(1)
    done = pl.pallas_call(
        layer_kernel,
        out_shape=jax.ShapeDtypeStruct((1024, D), BF),
        in_specs=[SM, VM, VM, VM, VM, VM, ANY, ANY], out_specs=VM,
        scratch_shapes=[pltpu.VMEM((2048, D), BF), pltpu.VMEM((1024, D), BF)]
        + [pltpu.VMEM((2048, D), BF)] * 4
        + [pltpu.VMEM((2, 8, 256, 256), F32), pltpu.VMEM((1024, D), BF),
           pltpu.VMEM((D, 2 * FF), BF), pltpu.VMEM((FF, D), BF), dma((2,))],
        compiler_params=params(),
    )(length, full, attn_gain.reshape(1, D), w_qkv, w_out, mlp_gain.reshape(1, D), w_in, w_down)
    return pl.pallas_call(
        give_kernel,
        out_shape=jax.ShapeDtypeStruct((2, 512, D), BF),
        in_specs=[ANY], out_specs=ANY,
        scratch_shapes=[pltpu.VMEM((256, D), BF), pltpu.VMEM((512, D), BF), dma((3,)), dma((2,)), dma, dma((2, 2)),
                        dma, dma],
        compiler_params=params(5),
    )(done.reshape(2, 512, D))


def solution(mesh):
    in_specs = (P("rows", "cols"), P("rows"), P("rows", "cols"), P(), P(), P(), P(), P(), P())
    return jax.shard_map(local, mesh=mesh, in_specs=in_specs, out_specs=P("rows", "cols", None), check_vma=False)
```

time: 356 us -> 177 us (0.50)
  Pallas kernels: 0 us -> 172 us
  local copies, waits for them, and re-layouts: 92 us -> 4.89 us
  waiting for transfers between devices: 79.4 us -> 0 us
  matrix products: 77.7 us -> 0 us
  other arithmetic: 46 us -> 0 us
  blocking collectives: 41.1 us -> 0 us
  between operations: 13.7 us -> 0.05 us
  starting transfers between devices: 4.87 us -> 0 us
    pallas_call x0 -> x9, Pallas kernels: none -> 172 us  [the longest x1 38.9 us: local(): pl.pallas_call(back_kernel, out_shape=jax.ShapeDtypeStruct((32, CAP, 128)...]
    dot_general x6 -> x0, matrix products: 77.7 us -> none  [the longest x1 27.9 us: local(): jnp.einsum('bqhd,bkhd->bhqk', queries, key_heads, preferred_element_type=...]
    all_gather x2 -> x0, waiting for transfers between devices: 43.3 us -> none  [the longest x1 43.3 us: local(): key_piece = lax.all_gather(keys, 'cols', axis=1, tiled=True)]
    gather x3 -> x0, local copies, waits for them, and re-layouts: 41.3 us -> none  [the longest x2 28.1 us: local(): looked = jnp.take(table, jnp.maximum(asked, 0), axis=0)]
    all_to_all x3 -> x0, blocking collectives: 41.1 us -> none  [the longest x1 16.3 us: local(): lax.all_to_all(requests, 'rows', split_axis=0, concat_axis=0, tiled=True)]
    all_to_all x1 -> x0, waiting for transfers between devices: 36.1 us -> none  [local(): lax.all_to_all(looked, 'rows', split_axis=0, concat_axis=0, tiled=True)]
    reduce_sum x4 -> x0, other arithmetic: 23.4 us -> none  [the longest x1 22.5 us: local(): running_sum = jnp.sum(probs, axis=-1)]
    scatter x1 -> x0, local copies, waits for them, and re-layouts: 15.5 us -> none  [local(): requests = requests.at[slot_index].set(flat_ids - owner_block * block_row...]
  transfers between devices with their start and end apart: 3 -> 0, of which waited for: 2 -> 0; matrix products, arithmetic and copies ran while one was open for 17% -> 0% of each run, Pallas kernels for 0% -> 0%
where the time goes in v1:
time: 177 us
  Pallas kernels  172 us (97%)
  local copies, waits for them, and re-layouts  4.89 us (3%)
    pallas_call x1, Pallas kernels, local(): pl.pallas_call(back_kernel, out_shape=jax.ShapeDtypeStruct((32, CAP, 128)...  38.9 us
    pallas_call x1, Pallas kernels, local(): pl.pallas_call(layer_kernel, out_shape=jax.ShapeDtypeStruct((1024, D), BF...  37.3 us
    pallas_call x1, Pallas kernels, local(): pl.pallas_call(spread_kernel, out_shape=jax.ShapeDtypeStruct((4, 2048, 12...  19.2 us
    pallas_call x1, Pallas kernels, local(): pl.pallas_call(lookup_kernel, out_shape=jax.ShapeDtypeStruct((32, CAP, 12...  17.6 us
    pallas_call x1, Pallas kernels, local(): pl.pallas_call(compact_kernel, out_shape=jax.ShapeDtypeStruct((4096, 128)...  17.2 us
    pallas_call x1, Pallas kernels, local(): pl.pallas_call(give_kernel, out_shape=jax.ShapeDtypeStruct((2, 512, D), B...  15.6 us
    pallas_call x1, Pallas kernels, local(): pl.pallas_call(ask_kernel, out_shape=jax.ShapeDtypeStruct((32, 4, 128), j...  12.8 us
    pallas_call x1, Pallas kernels, local(): pl.pallas_call(ids_kernel, out_shape=jax.ShapeDtypeStruct((4, 8, 128), jn...  8.13 us

profile of v1, /device:TPU:1, one launch (start us, length us, event | category | flops | bytes accessed | tf_op | source)
XLA Modules:
  0.0 176.9 jit_solution(13143200370866146960)
XLA Ops:
  0.0 1.3 reshape.21.ids_ref
  1.3 8.1 %shard_map.91 = s32[4,8,128]{2,1,0:T(8,128)} custom-call(s32[8,128]{1,0:T(8,128)} %reshape.21.ids_ref), custom_call_target="tpu_custom_call" | custom-call | tf_op jit(solution)/shard_map/pallas_call | solution.py:532
  9.4 5.2 %shard_map.92 = (s32[32,4,128]{2,1,0:T(4,128)}, s32[32,128]{1,0:T(8,128)}) custom-call(s32[2]{0:T(128)} %len_ref.1, s32[32,128]{1,0:T(8,128)} %bitcast.8), custom_call_target="tpu_custom_call" | custom-call | tf_op jit(solution)/shard_map/pallas_call | solution.py:539
  14.6 12.8 %shard_map.93.asked_ref = s32[32,4,128]{2,1,0:T(4,128)} custom-call(s32[32,4,128]{2,1,0:T(4,128)} %get-tuple-element.7.msg_ref), custom_call_target="tpu_custom_call" | custom-call | tf_op jit(solution)/shard_map/pallas_call | solution.py:545
  27.5 1.3 constant_dynamic-slice_fusion
  28.8 17.6 %shard_map.94.src_ref = bf16[32,344,128]{2,1,0:T(8,128)(2,1)} custom-call(s32[32,4,128]{2,1,0:T(4,128)} %shard_map.93.asked_ref, bf16[16384,128]{1,0:T(8,128)(2,1)} %table_ref.1), custom_call_target="tpu_custom_call" | custom-call | tf_op jit(solution)/shard_map/pallas_call | solution.py:552
  46.4 38.9 %shard_map.95.src_ref = bf16[32,344,128]{2,1,0:T(8,128)(2,1)} custom-call(bf16[32,344,128]{2,1,0:T(8,128)(2,1)} %shard_map.94.src_ref), custom_call_target="tpu_custom_call" | custom-call | tf_op jit(solution)/shard_map/pallas_call | solution.py:559
  85.3 17.2 %shard_map.96 = bf16[4096,128]{1,0:T(8,128)(2,1)} custom-call(s32[32,128]{1,0:T(8,128)} %get-tuple-element.8.slot_ref, bf16[32,344,128]{2,1,0:T(8,128)(2,1)} %shard_map.95.src_ref), custom_call_target="tpu_custom_call" | custom-call | tf_op jit(solution)/shard_map/pallas_call | solution.py:567
  102.5 19.2 %shard_map.97.x_ref = bf16[4,2048,128]{2,1,0:T(8,128)(2,1)} custom-call(bf16[2,2048,128]{2,1,0:T(8,128)(2,1)} %bitcast.6), custom_call_target="tpu_custom_call" | custom-call | tf_op jit(solution)/shard_map/pallas_call | solution.py:574
  121.7 37.3 %shard_map.98 = bf16[1024,512]{1,0:T(8,128)(2,1)} custom-call(s32[1]{0:T(128)} %bitcast.1.len_ref, bf16[4,2048,128]{2,1,0:T(8,128)(2,1)} %shard_map.97.x_ref, f32[1,512]{1,0:T(1,128)} %bitcast.9, bf16[512,1536]{1,0:T(8,128)(2,1)} %wqkv_ref.1, bf16[512,512]{1,0:T(8,128)(2,1)} %wout_ref.1, f32[1,512]{1,0:T(1,128)} %bitcast.10, bf16[512,4096]{1,0:T(8,128)(2,1)} %win_hbm.1, ...), custom_call_target="tpu_custom_call" | custom-call | tf_op jit(solution)/shard_map/pallas_call | solution.py:584
  159.0 15.6 %shard_map.99 = bf16[2,512,512]{2,1,0:T(8,128)(2,1)} custom-call(bf16[2,512,512]{2,1,0:T(8,128)(2,1)} %bitcast.7), custom_call_target="tpu_custom_call" | custom-call | tf_op jit(solution)/shard_map/pallas_call | solution.py:594
  174.6 2.3 %copy.11 = bf16[2,512,512]{2,1,0:T(8,128)(2,1)} copy(bf16[2,512,512]{2,1,0:T(8,128)(2,1)} %shard_map.99) | data formatting | bytes 2097152

commit v2 on v1

--- a/solution.py
+++ b/solution.py
@@ -53,62 +53,58 @@
     return pltpu.CompilerParams(vmem_limit_bytes=vmem * 2**20, **kw)
 
 
-def ids_kernel(ids_ref, out_ref, send_sem, recv_sem):
+def ask_kernel(len_ref, mine_ref, out_ref, slot_ref, ids_ref, msg_ref, ids_send, ids_recv, send_sem, recv_sem):
     r, z, _, _, _ = place()
-    peers = [(r, (z + s) % 4) for s in (1, 2, 3)]
-    greet(peers)
+    near = [(r, (z + s) % 4) for s in (1, 2, 3)]
+    peers = [((r + s) % 32, z) for s in range(1, 32)]
+    greet(near + peers)
     copies = []
-    for s, device in enumerate(peers):
-        copy = remote(ids_ref, out_ref.at[z], send_sem.at[s], recv_sem.at[s], device)
+    for s, device in enumerate(near):
+        copy = remote(mine_ref, ids_ref.at[z], ids_send.at[s], ids_recv.at[s], device)
         copy.start()
         copies.append(copy)
-    out_ref[z] = ids_ref[...]
+    ids_ref[z] = mine_ref[...]
+    before = (lax.broadcasted_iota(jnp.int32, (128, 128), 0)
+              < lax.broadcasted_iota(jnp.int32, (128, 128), 1)).astype(F32)
+    above = (lax.broadcasted_iota(jnp.int32, (32, 32), 1)
+             < lax.broadcasted_iota(jnp.int32, (32, 32), 0)).astype(F32).astype(BF)
+    both = jnp.concatenate([before, jnp.ones((128, 128), F32)], axis=0).astype(BF)
+    owners = lax.broadcasted_iota(jnp.int32, (32, 128), 0)
+    ks = lax.broadcasted_iota(jnp.int32, (384, 128), 0)
+    lane = lax.broadcasted_iota(jnp.int32, (32, 128), 1)
     for copy in copies:
         copy.wait()
-
-
-def request_kernel(len_ref, ids_ref, msg_ref, slot_ref):
-    ids = ids_ref[...]
+    ids = ids_ref[...].reshape(32, 128)
     owner = ids >> 14
     low, high = (ids & 127).astype(F32), ((ids >> 7) & 127).astype(F32)
-    before = (lax.broadcasted_iota(jnp.int32, (128, 128), 0)
-              < lax.broadcasted_iota(jnp.int32, (128, 128), 1)).astype(F32).astype(BF)
-    above = (lax.broadcasted_iota(jnp.int32, (32, 32), 1)
-             < lax.broadcasted_iota(jnp.int32, (32, 32), 0)).astype(F32).astype(BF)
-    ones = jnp.ones((128, 128), BF)
+    ones = [jnp.where(owner == o, 1.0, 0.0).astype(BF) for o in range(32)]
+    rows_above = dot(above, jnp.concatenate(ones, axis=1)).astype(BF)
+    prior = dot(
+        jnp.concatenate(
+            [jnp.concatenate(ones, axis=0),
+             jnp.concatenate([rows_above[:, 128 * o : 128 * o + 128] for o in range(32)], axis=0)], axis=1),
+        both)
     rank = jnp.zeros((32, 128), F32)
     for o in range(32):
-        hit = owner == o
-        one = jnp.where(hit, 1.0, 0.0).astype(BF)
-        prior = dot(one, before) + dot(dot(above, one).astype(BF), ones)
-        rank = rank + jnp.where(hit, prior, 0.0)
+        rank = rank + jnp.where(owner == o, prior[32 * o : 32 * o + 32], 0.0)
     rank_i = rank.astype(jnp.int32)
-    slot_ref[...] = owner * CAP + rank_i
-    owners = lax.broadcasted_iota(jnp.int32, (32, 128), 0)
-    ks = lax.broadcasted_iota(jnp.int32, (384, 128), 0)
     acc = jnp.zeros((64, 384), F32)
     count = jnp.zeros((32, 128), F32)
-    for a in range(32):
-        hit = owners == owner[a : a + 1, :]
-        count = count + jnp.where(hit, 1.0, 0.0)
-        left = jnp.concatenate(
-            [jnp.where(hit, low[a : a + 1, :], 0.0), jnp.where(hit, high[a : a + 1, :], 0.0)], axis=0)
-        right = jnp.where(ks == rank_i[a : a + 1, :], 1.0, 0.0)
-        acc = acc + dot_t(left.astype(BF), right.astype(BF))
+    for a in range(0, 32, 2):
+        lefts, rights = [], []
+        for b in (a, a + 1):
+            hit = owners == owner[b : b + 1, :]
+            count = count + jnp.where(hit, 1.0, 0.0)
+            lefts.append(jnp.concatenate(
+                [jnp.where(hit, low[b : b + 1, :], 0.0), jnp.where(hit, high[b : b + 1, :], 0.0)], axis=0).astype(BF))
+            rights.append(jnp.where(ks == rank_i[b : b + 1, :], 1.0, 0.0).astype(BF))
+        acc = acc + dot_t(jnp.concatenate(lefts, axis=1), jnp.concatenate(rights, axis=1))
     req = (acc[32:] * 128.0 + acc[:32]).astype(jnp.int32)
     for j in range(3):
         msg_ref[:, j, :] = req[:, 128 * j : 128 * j + 128]
-    total = jnp.sum(count, axis=1, keepdims=True).astype(jnp.int32)
-    lane = lax.broadcasted_iota(jnp.int32, (32, 128), 1)
-    tail = jnp.where(lane == 0, total, 0)
-    tail = jnp.where(lane == 1, len_ref[0], jnp.where(lane == 2, len_ref[1], tail))
+    tail = jnp.where(lane == 1, len_ref[0], jnp.where(lane == 2, len_ref[1], 0))
     msg_ref[:, 3, :] = tail
-
-
-def ask_kernel(msg_ref, out_ref, send_sem, recv_sem):
-    r, z, _, _, _ = place()
-    peers = [((r + s) % 32, z) for s in range(1, 32)]
-    greet(peers)
+    slot_ref[...] = owner * CAP + rank_i
     copies = []
     for s, device in enumerate(peers):
         copy = remote(msg_ref.at[device[0]], out_ref.at[r], send_sem.at[s], recv_sem.at[s], device)
@@ -117,30 +113,6 @@
     out_ref[r] = msg_ref[r]
     for copy in copies:
         copy.wait()
-
-
-def lookup_kernel(asked_ref, table_ref, out_ref, wide, stage):
-    def widen(i, _):
-        rows = pl.ds(pl.multiple_of(i * 256, 256), 256)
-        wide[rows, :] = table_ref[rows, :].astype(F32)
-        return 0
-
-    lax.fori_loop(0, 64, widen, 0)
-    stage[...] = jnp.zeros_like(stage)
-
-    def block(p, _):
-        def some(j, _):
-            base = j * 16
-            row, col = base // 128, lax.rem(base, 128)
-            for i in range(16):
-                stage[pl.ds(base + i, 1), :] = wide[pl.ds(asked_ref[p, row, col + i], 1), :]
-            return 0
-
-        lax.fori_loop(0, (asked_ref[p, 3, 0] + 15) // 16, some, 0)
-        out_ref[p] = stage[0:CAP, :].astype(BF)
-        return 0
-
-    lax.fori_loop(0, 32, block, 0)
 
 
 def routes():
@@ -159,7 +131,7 @@
     return sorted(out, key=key)
 
 
-def back_kernel(src_ref, out_ref, relay, own, send_sem, recv_sem, hop_send, hop_recv, own_sem):
+def lookup_kernel(asked_ref, table_ref, out_ref, wide, stage, block, relay, send_sem, recv_sem, hop_send, hop_recv):
     r, z, y, x, k = place()
 
     def row(dy, dx, dk):
@@ -168,21 +140,45 @@
     flows = routes()
     hops = [f for f in flows if f[3] is not None]
     direct = [f for f in flows if f[3] is None]
-    greet([((r + s) % 32, z) for s in range(1, 32)])
-    first, final = [], []
-    for i, (dy, dx, dk, (hy, hx)) in enumerate(hops):
-        copy = remote(src_ref.at[row(dy, dx, dk)], relay.at[i], hop_send.at[i], hop_recv.at[i], (row(hy, hx, 0), z))
-        copy.start()
-        first.append(copy)
-    for i, (dy, dx, dk, _) in enumerate(direct):
-        copy = remote(src_ref.at[row(dy, dx, dk)], out_ref.at[r], send_sem.at[i], recv_sem.at[i], (row(dy, dx, dk), z))
-        copy.start()
-        final.append(copy)
-    take = pltpu.make_async_copy(src_ref.at[r], own, own_sem)
-    take.start()
-    take.wait()
-    put = pltpu.make_async_copy(own, out_ref.at[r], own_sem)
-    put.start()
+    barrier = pltpu.get_barrier_semaphore()
+    for s in range(1, 32):
+        pl.semaphore_signal(barrier, inc=1, device_id=((r + s) % 32, z), device_id_type=MESH)
+
+    def widen(i, _):
+        rows = pl.ds(pl.multiple_of(i * 256, 256), 256)
+        wide[rows, :] = table_ref[rows, :].astype(F32)
+        return 0
+
+    lax.fori_loop(0, 64, widen, 0)
+    pl.semaphore_wait(barrier, 31)
+
+    def fill(p, dst):
+        def some(j, _):
+            base = j * 43
+            for i in range(43):
+                at = base + i
+                stage[pl.ds(at, 1), :] = wide[pl.ds(asked_ref[p, at // 128, lax.rem(at, 128)], 1), :]
+            return 0
+
+        lax.fori_loop(0, 8, some, 0)
+        dst[...] = stage[...].astype(BF)
+
+    first, final, waiting = [], [], None
+    for n, (dy, dx, dk, hop) in enumerate(hops + direct):
+        p = row(dy, dx, dk)
+        fill(p, block.at[n])
+        if hop is not None:
+            copy = remote(block.at[n], relay.at[n], hop_send.at[n], hop_recv.at[n], (row(*hop, 0), z))
+            first.append(copy)
+        else:
+            i = n - len(hops)
+            copy = remote(block.at[n], out_ref.at[r], send_sem.at[i], recv_sem.at[i], (p, z))
+            final.append(copy)
+        if waiting is not None:
+            waiting.start()
+        waiting = copy
+    fill(r, out_ref.at[r])
+    waiting.start()
     for i, (dy, dx, dk, (hy, hx)) in enumerate(hops):
         first[i].wait_recv()
         n = len(direct) + i
@@ -190,135 +186,113 @@
                       (row(dy - hy, dx - hx, dk), z))
         copy.start()
         final.append(copy)
-    put.wait()
     for copy in first:
         copy.wait_send()
     for copy in final:
         copy.wait()
 
 
-def compact_kernel(slot_ref, src_ref, out_ref, wide, stage):
-    def widen(i, _):
-        wide[pl.ds(pl.multiple_of(i * CAP, 8), CAP), :] = src_ref[i].astype(F32)
-        return 0
-
-    lax.fori_loop(0, 32, widen, 0)
-
-    def some(j, _):
-        a, col = j // 8, lax.rem(j, 8) * 16
-        h, zz, jj = lax.rem(a, 8) // 4, a // 8, lax.rem(a, 4)
-        base = h * 2048 + zz * 512 + jj * 128 + col
-        for i in range(16):
-            stage[pl.ds(base + i, 1), :] = wide[pl.ds(slot_ref[a, col + i], 1), :]
-        return 0
-
-    lax.fori_loop(0, 256, some, 0)
-
-    def narrow(i, _):
-        rows = pl.ds(pl.multiple_of(i * 256, 256), 256)
-        out_ref[rows, :] = stage[rows, :].astype(BF)
-        return 0
-
-    lax.fori_loop(0, 16, narrow, 0)
-
-
-def spread_kernel(src_ref, out_ref, relay, send_sem, relay_send, relay_recv, recv_sem, pass_send, pass_recv,
-                  own_send, own_recv, own_sem, bounce):
+def spread_kernel(slot_ref, back_ref, out_ref, wide, stage, emb, relay, send_sem, relay_send, relay_recv, recv_sem,
+                  pass_send, pass_recv, own_send, own_recv):
     r, z, y, x, k = place()
     base = r - k
     other = (base + 1 - k, z)
     up, down = (z + 1) % 4, (z + 3) % 4
     holder = z // 2
-
-    def part(i):
-        return pl.ds(1024 * i, 1024)
-
-    mine = part(0) if False else pl.ds(pl.multiple_of(1024 * k, 1024), 1024)
+    mine = pl.ds(pl.multiple_of(1024 * k, 1024), 1024)
     theirs = pl.ds(pl.multiple_of(1024 * (1 - k), 1024), 1024)
     peers = [(base + 1 - k, z)]
     for kk in range(2):
         for s in (1, 3):
             peers.append((base + kk, (z + s) % 4))
-    greet(peers)
+    barrier = pltpu.get_barrier_semaphore()
+    for device in peers:
+        pl.semaphore_signal(barrier, inc=1, device_id=device, device_id_type=MESH)
+
+    def widen(i, _):
+        wide[pl.ds(pl.multiple_of(i * CAP, 8), CAP), :] = back_ref[i].astype(F32)
+        return 0
+
+    lax.fori_loop(0, 32, widen, 0)
+    pl.semaphore_wait(barrier, len(peers))
+
+    def part(i):
+        return pl.ds(1024 * i, 1024)
 
     def far(h, half):
-        step = 1 if half == 0 else 3
-        return remote(src_ref.at[h, part(half)], relay, relay_send, relay_recv, (base + half, (z + step) % 4))
+        return remote(emb.at[h, part(half)], relay, relay_send.at[half], relay_recv,
+                      (base + half, up if half == 0 else down))
 
     def near(h, half, step):
-        return remote(src_ref.at[h, part(half)], out_ref.at[z, part(half)],
+        return remote(emb.at[h, part(half)], out_ref.at[z, part(half)],
                       send_sem.at[step // 2, half], recv_sem.at[step // 2], (base + half, (z + step) % 4))
 
-    def own(h):
-        return remote(src_ref.at[h], out_ref.at[z], own_send, own_recv, other)
-
-    def inner(h):
-        return (pltpu.make_async_copy(src_ref.at[h], bounce, own_sem),
-                pltpu.make_async_copy(bounce, out_ref.at[z], own_sem))
-
-    dist = [(2 * k + h - z) % 4 for h in range(2)]
-    for h in range(2):
-        @pl.when(dist[h] == 2)
-        def _():
-            for half in range(2):
-                remote(src_ref.at[h, part(half)], relay, relay_send.at[half], relay_recv,
-                       (base + half, up if half == 0 else down)).start()
-
-    for h in range(2):
+    def own(h, half):
+        return remote(emb.at[h, part(half)], out_ref.at[z, part(half)], own_send.at[half], own_recv.at[half], other)
+
+    def send(h, half, act):
+        dist = (2 * k + h - z) % 4
+
+        @pl.when(dist == 2)
+        def _():
+            act(far(h, half))
+
         for step in (1, 3):
-            @pl.when(dist[h] == step)
+            @pl.when(dist == step)
             def _():
-                for half in range(2):
-                    near(h, half, step).start()
-
-        @pl.when(dist[h] == 0)
-        def _():
-            own(h).start()
-            take, put = inner(h)
-            take.start()
-            take.wait()
-            put.start()
-
-    back = jnp.where(k == 0, down, up)
+                act(near(h, half, step))
+
+        @pl.when(dist == 0)
+        def _():
+            act(own(h, half))
+
+    lead = jnp.where((2 * k - z) % 4 < 2, 1, 0)
+    pieces = [(h, half) for h in (lead, 1 - lead) for half in range(2)]
+    waiting = None
+    for h, half in pieces:
+        def gather(j, _):
+            a = (half * 2 + j // 4) * 8 + h * 4 + lax.rem(j, 4)
+            for i in range(128):
+                stage[pl.ds(j * 128 + i, 1), :] = wide[pl.ds(slot_ref[a, i], 1), :]
+            return 0
+
+        lax.fori_loop(0, 8, gather, 0)
+        emb[h, part(half), :] = stage[...].astype(BF)
+
+        @pl.when((2 * k + h - z) % 4 == 0)
+        def _():
+            out_ref[z, part(half), :] = stage[...].astype(BF)
+
+        if waiting is not None:
+            send(*waiting, lambda copy: copy.start())
+        waiting = (h, half)
+    send(*waiting, lambda copy: copy.start())
+
+    behind = jnp.where(k == 0, down, up)
     ahead = jnp.where(k == 0, up, down)
-    relayed = remote(relay, out_ref.at[back, mine], pass_send.at[3], recv_sem.at[2], (r, ahead))
-    remote(src_ref.at[0, part(0)], relay, relay_send.at[0], relay_recv, (r, ahead)).wait_recv()
+    relayed = remote(relay, out_ref.at[behind, mine], pass_send.at[3], recv_sem.at[2], (r, ahead))
+    far(0, 0).wait_recv()
     relayed.start()
     passed = []
     for i, source in enumerate((down, up, (z + 2) % 4)):
         got = out_ref.at[source, mine]
-        remote(got, got, send_sem.at[0, 0], recv_sem.at[i], other).wait_recv()
+        remote(got, got, pass_send.at[i], recv_sem.at[i], other).wait_recv()
         copy = remote(got, got, pass_send.at[i], pass_recv.at[i], other)
         copy.start()
         passed.append(copy)
 
-    for i, copy in enumerate(passed):
-        copy.wait_send()
-        source = (down, up, (z + 2) % 4)[i]
-        remote(out_ref.at[source, theirs], out_ref.at[source, theirs], pass_send.at[i], pass_recv.at[i],
-               other).wait_recv()
+    for i, source in enumerate((down, up, (z + 2) % 4)):
+        passed[i].wait_send()
+        got = out_ref.at[source, theirs]
+        remote(got, got, pass_send.at[i], pass_recv.at[i], other).wait_recv()
     relayed.wait_send()
-
-    for h in range(2):
-        @pl.when(dist[h] == 2)
-        def _():
-            for half in range(2):
-                remote(src_ref.at[h, part(half)], relay, relay_send.at[half], relay_recv,
-                       (base + half, up if half == 0 else down)).wait_send()
-        for step in (1, 3):
-            @pl.when(dist[h] == step)
-            def _():
-                for half in range(2):
-                    near(h, half, step).wait_send()
-
-        @pl.when(dist[h] == 0)
-        def _():
-            own(h).wait_send()
-            inner(h)[1].wait()
+    for h, half in pieces:
+        send(h, half, lambda copy: copy.wait_send())
 
     @pl.when(k != holder)
     def _():
-        own(0).wait_recv()
+        for half in range(2):
+            own(0, half).wait_recv()
 
 
 def layer_kernel(len_ref, x_ref, gain_ref, wqkv_ref, wout_ref, gain2_ref, win_hbm, wdown_hbm, out_ref,
@@ -529,56 +503,31 @@
 
 def local(token_ids, lengths, table, attn_gain, w_qkv, w_out, mlp_gain, w_in, w_down):
     dma = pltpu.SemaphoreType.DMA
-    ids = pl.pallas_call(
-        ids_kernel,
-        out_shape=jax.ShapeDtypeStruct((4, 8, 128), jnp.int32),
-        in_specs=[VM], out_specs=VM,
-        scratch_shapes=[dma((3,)), dma((3,))],
-        compiler_params=params(1),
-    )(token_ids.reshape(8, 128))
-    msg, slot = pl.pallas_call(
-        request_kernel,
+    asked, slot = pl.pallas_call(
+        ask_kernel,
         out_shape=[jax.ShapeDtypeStruct((32, 4, 128), jnp.int32), jax.ShapeDtypeStruct((32, 128), jnp.int32)],
         in_specs=[SM, VM], out_specs=[VM, VM],
-        compiler_params=params(),
-    )(lengths, ids.reshape(32, 128))
-    asked = pl.pallas_call(
-        ask_kernel,
-        out_shape=jax.ShapeDtypeStruct((32, 4, 128), jnp.int32),
-        in_specs=[VM], out_specs=VM,
-        scratch_shapes=[dma((31,)), dma((31,))],
-        compiler_params=params(2),
-    )(msg)
-    looked = pl.pallas_call(
+        scratch_shapes=[pltpu.VMEM((4, 8, 128), jnp.int32), pltpu.VMEM((32, 4, 128), jnp.int32),
+                        dma((3,)), dma((3,)), dma((31,)), dma((31,))],
+        compiler_params=params(1),
+    )(lengths, token_ids.reshape(8, 128))
+    returned = pl.pallas_call(
         lookup_kernel,
         out_shape=jax.ShapeDtypeStruct((32, CAP, 128), BF),
         in_specs=[SM, VM], out_specs=VM,
-        scratch_shapes=[pltpu.VMEM((16384, 128), F32), pltpu.VMEM((352, 128), F32)],
-        compiler_params=params(),
+        scratch_shapes=[pltpu.VMEM((16384, 128), F32), pltpu.VMEM((CAP, 128), F32), pltpu.VMEM((31, CAP, 128), BF),
+                        pltpu.VMEM((14, CAP, 128), BF), dma((31,)), dma((31,)), dma((14,)), dma((14,))],
+        compiler_params=params(2),
     )(asked, table)
-    returned = pl.pallas_call(
-        back_kernel,
-        out_shape=jax.ShapeDtypeStruct((32, CAP, 128), BF),
-        in_specs=[ANY], out_specs=ANY,
-        scratch_shapes=[pltpu.VMEM((14, CAP, 128), BF), pltpu.VMEM((CAP, 128), BF), dma((31,)), dma((31,)),
-                        dma((14,)), dma((14,)), dma],
-        compiler_params=params(3),
-    )(looked)
-    embedded = pl.pallas_call(
-        compact_kernel,
-        out_shape=jax.ShapeDtypeStruct((4096, 128), BF),
-        in_specs=[SM, VM], out_specs=VM,
-        scratch_shapes=[pltpu.VMEM((32 * CAP, 128), F32), pltpu.VMEM((4096, 128), F32)],
-        compiler_params=params(),
-    )(slot, returned)
     full = pl.pallas_call(
         spread_kernel,
         out_shape=jax.ShapeDtypeStruct((4, 2048, 128), BF),
-        in_specs=[ANY], out_specs=ANY,
-        scratch_shapes=[pltpu.VMEM((1024, 128), BF), dma((2, 2)), dma((2,)), dma, dma((3,)), dma((4,)), dma((3,)),
-                        dma, dma, dma, pltpu.VMEM((2048, 128), BF)],
-        compiler_params=params(4),
-    )(embedded.reshape(2, 2048, 128))
+        in_specs=[SM, VM], out_specs=VM,
+        scratch_shapes=[pltpu.VMEM((32 * CAP, 128), F32), pltpu.VMEM((1024, 128), F32), pltpu.VMEM((2, 2048, 128), BF),
+                        pltpu.VMEM((1024, 128), BF), dma((2, 2)), dma((2,)), dma, dma((3,)), dma((4,)), dma((3,)),
+                        dma((2,)), dma((2,))],
+        compiler_params=params(3),
+    )(slot, returned)
     r, z = lax.axis_index("rows"), lax.axis_index("cols")
     length = lax.dynamic_slice(asked, (r - r % 2 + z // 2, 3, 1 + z % 2), (1, 1, 1)).reshape(1)
     done = pl.pallas_call(
@@ -597,7 +546,7 @@
         in_specs=[ANY], out_specs=ANY,
         scratch_shapes=[pltpu.VMEM((256, D), BF), pltpu.VMEM((512, D), BF), dma((3,)), dma((2,)), dma, dma((2, 2)),
                         dma, dma],
-        compiler_params=params(5),
+        compiler_params=params(4),
     )(done.reshape(2, 512, D))
 
 

time: 177 us -> 199 us (1.12)
  Pallas kernels: 172 us -> 194 us
    pallas_call x1, Pallas kernels: 17.6 us -> 98.3 us  [local(): pl.pallas_call(lookup_kernel, out_shape=jax.ShapeDtypeStruct((32, CAP, 12...]
    pallas_call x5 -> x1, Pallas kernels: 82.2 us -> 20.1 us  [local(): pl.pallas_call(ask_kernel, out_shape=[jax.ShapeDtypeStruct((32, 4, 128),...]
    pallas_call x1, Pallas kernels: 19.2 us -> 23.3 us  [local(): pl.pallas_call(spread_kernel, out_shape=jax.ShapeDtypeStruct((4, 2048, 12...]
where the time goes in v2:
time: 199 us
  Pallas kernels  194 us (97%)
  local copies, waits for them, and re-layouts  4.84 us (2%)
    pallas_call x1, Pallas kernels, local(): pl.pallas_call(lookup_kernel, out_shape=jax.ShapeDtypeStruct((32, CAP, 12...  98.3 us
    pallas_call x1, Pallas kernels, local(): pl.pallas_call(layer_kernel, out_shape=jax.ShapeDtypeStruct((1024, D), BF...  37.1 us
    pallas_call x1, Pallas kernels, local(): pl.pallas_call(spread_kernel, out_shape=jax.ShapeDtypeStruct((4, 2048, 12...  23.3 us
    pallas_call x1, Pallas kernels, local(): pl.pallas_call(ask_kernel, out_shape=[jax.ShapeDtypeStruct((32, 4, 128),...  20.1 us
    pallas_call x1, Pallas kernels, local(): pl.pallas_call(give_kernel, out_shape=jax.ShapeDtypeStruct((2, 512, D), B...  15.6 us

profile of v2, /device:TPU:1, one launch (start us, length us, event | category | flops | bytes accessed | tf_op | source)
XLA Modules:
  0.0 199.1 jit_solution(9408561856185805738)
XLA Ops:
  0.0 1.3 reshape.15.mine_ref
  1.3 20.1 %shard_map.91 = (s32[32,4,128]{2,1,0:T(4,128)}, s32[32,128]{1,0:T(8,128)}) custom-call(s32[2]{0:T(128)} %len_ref.1, s32[8,128]{1,0:T(8,128)} %reshape.15.mine_ref), custom_call_target="tpu_custom_call" | custom-call | tf_op jit(solution)/shard_map/pallas_call | solution.py:506
  21.4 1.3 constant_dynamic-slice_fusion
  22.6 98.3 %shard_map.92.back_ref = bf16[32,344,128]{2,1,0:T(8,128)(2,1)} custom-call(s32[32,4,128]{2,1,0:T(4,128)} %get-tuple-element.7.asked_ref, bf16[16384,128]{1,0:T(8,128)(2,1)} %table_ref.1), custom_call_target="tpu_custom_call" | custom-call | tf_op jit(solution)/shard_map/pallas_call | solution.py:514
  120.9 23.3 %shard_map.93.x_ref = bf16[4,2048,128]{2,1,0:T(8,128)(2,1)} custom-call(s32[32,128]{1,0:T(8,128)} %get-tuple-element.8.slot_ref, bf16[32,344,128]{2,1,0:T(8,128)(2,1)} %shard_map.92.back_ref), custom_call_target="tpu_custom_call" | custom-call | tf_op jit(solution)/shard_map/pallas_call | solution.py:522
  144.2 37.1 %shard_map.94 = bf16[1024,512]{1,0:T(8,128)(2,1)} custom-call(s32[1]{0:T(128)} %bitcast.len_ref, bf16[4,2048,128]{2,1,0:T(8,128)(2,1)} %shard_map.93.x_ref, f32[1,512]{1,0:T(1,128)} %bitcast.5, bf16[512,1536]{1,0:T(8,128)(2,1)} %wqkv_ref.1, bf16[512,512]{1,0:T(8,128)(2,1)} %wout_ref.1, f32[1,512]{1,0:T(1,128)} %bitcast.6, bf16[512,4096]{1,0:T(8,128)(2,1)} %win_hbm.1, ...), custom_call_target="tpu_custom_call" | custom-call | tf_op jit(solution)/shard_map/pallas_call | solution.py:533
  181.3 15.6 %shard_map.95 = bf16[2,512,512]{2,1,0:T(8,128)(2,1)} custom-call(bf16[2,512,512]{2,1,0:T(8,128)(2,1)} %bitcast.4), custom_call_target="tpu_custom_call" | custom-call | tf_op jit(solution)/shard_map/pallas_call | solution.py:543
  196.9 2.3 %copy.11 = bf16[2,512,512]{2,1,0:T(8,128)(2,1)} copy(bf16[2,512,512]{2,1,0:T(8,128)(2,1)} %shard_map.95) | data formatting | bytes 2097152

commit v3 on v2

--- a/solution.py
+++ b/solution.py
@@ -156,8 +156,7 @@
         def some(j, _):
             base = j * 43
             for i in range(43):
-                at = base + i
-                stage[pl.ds(at, 1), :] = wide[pl.ds(asked_ref[p, at // 128, lax.rem(at, 128)], 1), :]
+                stage[pl.ds(base + i, 1), :] = wide[pl.ds(asked_ref[p * 512 + base + i], 1), :]
             return 0
 
         lax.fori_loop(0, 8, some, 0)
@@ -518,7 +517,7 @@
         scratch_shapes=[pltpu.VMEM((16384, 128), F32), pltpu.VMEM((CAP, 128), F32), pltpu.VMEM((31, CAP, 128), BF),
                         pltpu.VMEM((14, CAP, 128), BF), dma((31,)), dma((31,)), dma((14,)), dma((14,))],
         compiler_params=params(2),
-    )(asked, table)
+    )(asked.reshape(32 * 512), table)
     full = pl.pallas_call(
         spread_kernel,
         out_shape=jax.ShapeDtypeStruct((4, 2048, 128), BF),

time: 199 us -> 144 us (0.72)
  Pallas kernels: 194 us -> 138 us
    pallas_call x1, Pallas kernels: 98.3 us -> 42.5 us  [local(): pl.pallas_call(lookup_kernel, out_shape=jax.ShapeDtypeStruct((32, CAP, 12...]
where the time goes in v3:
time: 144 us; the launch traced here: 143 us
  Pallas kernels  138 us (96%)
  local copies, waits for them, and re-layouts  4.84 us (3%)
    pallas_call x1, Pallas kernels, local(): pl.pallas_call(lookup_kernel, out_shape=jax.ShapeDtypeStruct((32, CAP, 12...  42.5 us
    pallas_call x1, Pallas kernels, local(): pl.pallas_call(layer_kernel, out_shape=jax.ShapeDtypeStruct((1024, D), BF...  37.3 us
    pallas_call x1, Pallas kernels, local(): pl.pallas_call(spread_kernel, out_shape=jax.ShapeDtypeStruct((4, 2048, 12...  22.9 us
    pallas_call x1, Pallas kernels, local(): pl.pallas_call(ask_kernel, out_shape=[jax.ShapeDtypeStruct((32, 4, 128),...  20.1 us
    pallas_call x1, Pallas kernels, local(): pl.pallas_call(give_kernel, out_shape=jax.ShapeDtypeStruct((2, 512, D), B...  15.6 us

profile of v3, /device:TPU:1, one launch (start us, length us, event | category | flops | bytes accessed | tf_op | source)
XLA Modules:
  0.0 143.2 jit_solution(12014909293191629523)
XLA Ops:
  0.0 1.3 reshape.18.mine_ref
  1.3 20.1 %shard_map.91 = (s32[32,4,128]{2,1,0:T(4,128)}, s32[32,128]{1,0:T(8,128)}) custom-call(s32[2]{0:T(128)} %len_ref.1, s32[8,128]{1,0:T(8,128)} %reshape.18.mine_ref), custom_call_target="tpu_custom_call" | custom-call | tf_op jit(solution)/shard_map/pallas_call | solution.py:505
  21.4 1.3 constant_dynamic-slice_fusion
  22.6 42.5 %shard_map.92.back_ref = bf16[32,344,128]{2,1,0:T(8,128)(2,1)} custom-call(s32[16384]{0:T(1024)} %bitcast.6, bf16[16384,128]{1,0:T(8,128)(2,1)} %table_ref.1), custom_call_target="tpu_custom_call" | custom-call | tf_op jit(solution)/shard_map/pallas_call | solution.py:513
  65.1 22.9 %shard_map.93.x_ref = bf16[4,2048,128]{2,1,0:T(8,128)(2,1)} custom-call(s32[32,128]{1,0:T(8,128)} %get-tuple-element.8.slot_ref, bf16[32,344,128]{2,1,0:T(8,128)(2,1)} %shard_map.92.back_ref), custom_call_target="tpu_custom_call" | custom-call | tf_op jit(solution)/shard_map/pallas_call | solution.py:521
  88.1 37.3 %shard_map.94 = bf16[1024,512]{1,0:T(8,128)(2,1)} custom-call(s32[1]{0:T(128)} %bitcast.len_ref, bf16[4,2048,128]{2,1,0:T(8,128)(2,1)} %shard_map.93.x_ref, f32[1,512]{1,0:T(1,128)} %bitcast.7, bf16[512,1536]{1,0:T(8,128)(2,1)} %wqkv_ref.1, bf16[512,512]{1,0:T(8,128)(2,1)} %wout_ref.1, f32[1,512]{1,0:T(1,128)} %bitcast.8, bf16[512,4096]{1,0:T(8,128)(2,1)} %win_hbm.1, ...), custom_call_target="tpu_custom_call" | custom-call | tf_op jit(solution)/shard_map/pallas_call | solution.py:532
  125.3 15.6 %shard_map.95 = bf16[2,512,512]{2,1,0:T(8,128)(2,1)} custom-call(bf16[2,512,512]{2,1,0:T(8,128)(2,1)} %bitcast.5), custom_call_target="tpu_custom_call" | custom-call | tf_op jit(solution)/shard_map/pallas_call | solution.py:542
  140.9 2.3 %copy.11 = bf16[2,512,512]{2,1,0:T(8,128)(2,1)} copy(bf16[2,512,512]{2,1,0:T(8,128)(2,1)} %shard_map.95) | data formatting | bytes 2097152

commit v4 on v3

--- a/solution.py
+++ b/solution.py
@@ -295,100 +295,146 @@
 
 
 def layer_kernel(len_ref, x_ref, gain_ref, wqkv_ref, wout_ref, gain2_ref, win_hbm, wdown_hbm, out_ref,
-                 nrm, qs, ke, ko, ve, vo, sc, att, win_ref, wdown_ref, sems):
-    k = lax.axis_index("rows") % 2
+                 nrm, qs, ke, ko, vt, wvt, sc, att, obuf, relay, win_ref, wdown_ref, sems,
+                 send_sem, far_recv, recv_sem, pass_send):
+    r, z, _, _, k = place()
+    base = r - k
+    up, down = (z + 1) % 4, (z + 3) % 4
+    holder, slot = z // 2, z % 2
+    peers = [(base + 1 - k, z)]
+    for kk in range(2):
+        for s in (1, 3):
+            peers.append((base + kk, (z + s) % 4))
+    barrier = pltpu.get_barrier_semaphore()
+    for device in peers:
+        pl.semaphore_signal(barrier, inc=1, device_id=device, device_id_type=MESH)
     get_in = pltpu.make_async_copy(win_hbm, win_ref, sems.at[0])
     get_down = pltpu.make_async_copy(wdown_hbm, wdown_ref, sems.at[1])
     get_in.start()
     get_down.start()
     length = len_ref[0]
-    quarters = (k, 3 - k)
-
-    def norm(i, _):
+
+    def worker(q):
+        return jnp.where((q == 0) | (q == 3), 0, 1)
+
+    def quarter_of(step):
+        early = jnp.where(z < 2, 1, 0)
+        return jnp.where(step == early, k, 3 - k)
+
+    def block(b):
+        return pl.ds(256 * b, 256)
+
+    def near(step, b, q):
+        return remote(obuf.at[step, block(b)], out_ref.at[slot, block(b)], send_sem.at[step, b],
+                      recv_sem.at[slot, b], (base + holder, q))
+
+    def own(step, b):
+        return remote(obuf.at[step, block(b)], out_ref.at[slot, block(b)], send_sem.at[step, b],
+                      recv_sem.at[slot, b], (base + 1 - k, z))
+
+    def far(b):
+        return remote(obuf.at[0, block(b)], relay, send_sem.at[0, b], far_recv, (r, (up, down)[b]))
+
+    def passing(b):
+        source, target = ((down, up), (up, down))[b]
+        return remote(relay, out_ref.at[source % 2, block(b)], pass_send, recv_sem.at[source % 2, b],
+                      (base + source // 2, target))
+
+    def send(step, b, act):
+        q = quarter_of(step)
+        dist = (q - z) % 4
+
+        @pl.when((dist == 1) | (dist == 3))
+        def _():
+            act(near(step, b, q))
+
+        @pl.when((dist == 0) & (holder != k))
+        def _():
+            act(own(step, b))
+
+        if step == 0:
+            @pl.when(dist == 2)
+            def _():
+                act(far(b))
+
+    for c in range(4):
+        wvt[128 * c : 128 * c + 128, :] = wqkv_ref[:, 2 * D + 128 * c : 2 * D + 128 * c + 128].astype(F32).T.astype(BF)
+
+    def project(i, _):
         rows = pl.ds(pl.multiple_of(i * 256, 256), 256)
         parts = [x_ref[c, rows, :].astype(F32) for c in range(4)]
         square = parts[0] * parts[0]
         for part in parts[1:]:
             square = square + part * part
         scale = lax.rsqrt(jnp.sum(square, axis=1, keepdims=True) * (1.0 / D) + 1e-6)
-        for c in range(4):
-            nrm[rows, 128 * c : 128 * c + 128] = (parts[c] * scale * gain_ref[:, 128 * c : 128 * c + 128]).astype(BF)
-        return 0
-
-    lax.fori_loop(0, 8, norm, 0)
-
-    def project(i, _):
-        rows = pl.ds(pl.multiple_of(i * 256, 256), 256)
-        here = nrm[rows, :]
+        here = jnp.concatenate(
+            [(parts[c] * scale * gain_ref[:, 128 * c : 128 * c + 128]).astype(BF) for c in range(4)], axis=1)
+        nrm[rows, :] = here
         keys = dot(here, wqkv_ref[:, D : 2 * D])
-        vals = dot(here, wqkv_ref[:, 2 * D :])
+        vals = dot_t(wvt[...], here)
         lane = lax.broadcasted_iota(jnp.int32, (256, 128), 1)
         pos = lax.broadcasted_iota(jnp.int32, (256, 128), 0) + i * 256
         bias = jnp.where(pos < length, 0.0, NEG)
+        tail = jnp.where(lax.broadcasted_iota(jnp.int32, (16, 256), 0) == 0, 1.0, 0.0).astype(BF)
         for c in range(4):
             cols = slice(128 * c, 128 * c + 128)
             ke[rows, cols] = jnp.where(lane == 64, bias, keys[:, cols]).astype(BF)
             ko[rows, cols] = jnp.where(lane == 0, bias, keys[:, cols]).astype(BF)
-            ve[rows, cols] = jnp.where(lane == 64, 1.0, vals[:, cols]).astype(BF)
-            vo[rows, cols] = jnp.where(lane == 0, 1.0, vals[:, cols]).astype(BF)
+        for h in range(8):
+            vt[h, 0:64, rows] = vals[64 * h : 64 * h + 64, :].astype(BF)
+            vt[h, 64:80, rows] = tail
         return 0
 
     lax.fori_loop(0, 8, project, 0)
-    for a in range(2):
-        rows = pl.ds(pl.multiple_of(quarters[a] * 512, 512), 512)
-        qs[512 * a : 512 * a + 512, :] = (dot(nrm[rows, :], wqkv_ref[:, :D]) * (0.125 * LOG2E)).astype(BF)
-
-    def attend(kk):
+
+    def attend(quarter):
         def heads(hp, _):
             cols = pl.ds(pl.multiple_of(hp * 128, 128), 128)
             lane = lax.broadcasted_iota(jnp.int32, (256, 128), 1)
-            tri = (lax.broadcasted_iota(jnp.int32, (256, 256), 1)
-                   <= lax.broadcasted_iota(jnp.int32, (256, 256), 0))
-            for a, quarter in enumerate((kk, 3 - kk)):
-                for j in range(2):
-                    n = 2 * quarter + j + 1
-                    at = 512 * a + 256 * j
-                    q = qs[at : at + 256, cols].astype(F32)
-                    accs = []
-                    for odd in range(2):
-                        kref, vref = (ko, vo) if odd else (ke, ve)
-                        if odd:
-                            qa = jnp.where(lane >= 64, q, jnp.where(lane == 0, 1.0, 0.0)).astype(BF)
-                        else:
-                            qa = jnp.where(lane < 64, q, jnp.where(lane == 64, 1.0, 0.0)).astype(BF)
-                        top = None
-                        for c in range(n):
-                            s = dot_t(qa, kref[256 * c : 256 * c + 256, cols])
-                            if c == n - 1:
-                                s = jnp.where(tri, s, NEG)
-                            sc[odd, c] = s
-                            m = jnp.maximum(s[:, :128], s[:, 128:])
-                            top = m if top is None else jnp.maximum(top, m)
-                        top = jnp.max(top, axis=1, keepdims=True)
-                        acc = jnp.zeros((256, 128), F32)
-                        for c in range(n):
-                            p = jnp.exp2(sc[odd, c] - top).astype(BF)
-                            acc = acc + dot(p, vref[256 * c : 256 * c + 256, cols])
-                        accs.append(acc)
-                    even = accs[0] / accs[0][:, 64:65]
-                    odd_ = accs[1] / accs[1][:, 0:1]
-                    att[at : at + 256, cols] = jnp.where(lane < 64, even, odd_).astype(BF)
+            tri = (lax.broadcasted_iota(jnp.int32, (256, 256), 0)
+                   <= lax.broadcasted_iota(jnp.int32, (256, 256), 1))
+            for j in range(2):
+                n = 2 * quarter + j + 1
+                at = 256 * j
+                q = qs[at : at + 256, cols].astype(F32)
+                outs = []
+                for odd in range(2):
+                    kref = ko if odd else ke
+                    if odd:
+                        qa = jnp.where(lane >= 64, q, jnp.where(lane == 0, 1.0, 0.0)).astype(BF)
+                    else:
+                        qa = jnp.where(lane < 64, q, jnp.where(lane == 64, 1.0, 0.0)).astype(BF)
+                    top = None
+                    for c in range(n):
+                        s = dot_t(kref[256 * c : 256 * c + 256, cols], qa)
+                        if c == n - 1:
+                            s = jnp.where(tri, s, NEG)
+                        sc[odd, c] = s
+                        m = jnp.max(s.reshape(4, 8, 8, 256), axis=1)
+                        top = m if top is None else jnp.maximum(top, m)
+                    top = jnp.max(jnp.max(top, axis=0), axis=0, keepdims=True)
+                    acc = None
+                    for c in range(n):
+                        p = jnp.exp2(sc[odd, c] - top).astype(BF)
+                        o = dot(vt[2 * hp + odd, :, 256 * c : 256 * c + 256], p)
+                        acc = o if acc is None else acc + o
+                    outs.append(acc[0:64, :] / acc[64:65, :])
+                att[at : at + 256, cols] = jnp.concatenate(outs, axis=0).T.astype(BF)
             return 0
 
         lax.fori_loop(0, 4, heads, 0)
 
-    for kk in range(2):
-        @pl.when(k == kk)
-        def _():
-            attend(kk)
-
-    get_in.wait()
-    get_down.wait()
-
-    def mlp(i, _):
-        rows = pl.ds(pl.multiple_of(i * 256, 256), 256)
-        quarter = jnp.where(i < 2, quarters[0], quarters[1])
-        src = pl.ds(pl.multiple_of(quarter * 512 + lax.rem(i, 2) * 256, 256), 256)
+    def compute_attention(quarter):
+        rows = pl.ds(pl.multiple_of(quarter * 512, 512), 512)
+        qs[...] = (dot(nrm[rows, :], wqkv_ref[:, :D]) * (0.125 * LOG2E)).astype(BF)
+        for q in range(4):
+            @pl.when(quarter == q)
+            def _():
+                attend(q)
+
+    def mlp(step, b, quarter):
+        rows = pl.ds(pl.multiple_of(256 * b, 256), 256)
+        src = pl.ds(pl.multiple_of(quarter * 512 + b * 256, 256), 256)
         resid = jnp.concatenate([x_ref[c, src, :].astype(F32) for c in range(4)], axis=1)
         hidden = (resid + dot(att[rows, :], wout_ref[...])).astype(BF).astype(F32)
         scale = lax.rsqrt(jnp.mean(hidden * hidden, axis=1, keepdims=True) + 1e-6)
@@ -398,106 +444,60 @@
             cols = slice(512 * f, 512 * f + 512)
             up_cols = slice(FF + 512 * f, FF + 512 * f + 512)
             gate = dot(normed, win_ref[:, cols])
-            up = dot(normed, win_ref[:, up_cols])
-            act = (gate / (1.0 + jnp.exp(-gate)) * up).astype(BF)
+            high = dot(normed, win_ref[:, up_cols])
+            act = (gate / (1.0 + jnp.exp(-gate)) * high).astype(BF)
             out = out + dot(act, wdown_ref[cols, :])
-        out_ref[rows, :] = out.astype(BF)
+        obuf[step, rows, :] = out.astype(BF)
+
+        @pl.when((quarter == z) & (holder == k))
+        def _():
+            out_ref[slot, rows, :] = out.astype(BF)
+
+    def run(step, _):
+        quarter = quarter_of(step)
+        compute_attention(quarter)
+
+        @pl.when(step == 0)
+        def _():
+            get_in.wait()
+            get_down.wait()
+            pl.semaphore_wait(barrier, len(peers))
+
+        @pl.when(step == 1)
+        def _():
+            for b in range(2):
+                @pl.when(worker((up, down)[b]) == k)
+                def _():
+                    far(b).wait_recv()
+                    passing(b).start()
+
+        def each(b, _):
+            mlp(step, b, quarter)
+            for ss in range(2):
+                for bb in range(2):
+                    @pl.when((step == ss) & (b == bb))
+                    def _():
+                        send(ss, bb, lambda copy: copy.start())
+            return 0
+
+        lax.fori_loop(0, 2, each, 0)
         return 0
 
-    lax.fori_loop(0, 4, mlp, 0)
-
-
-def give_kernel(src_ref, out_ref, relay, bounce, send_sem, far_send, relay_recv, recv_sem, pass_send, own_sem):
-    r, z, y, x, k = place()
-    base = r - k
-    up, down = (z + 1) % 4, (z + 3) % 4
-    across = (z + 2) % 4
-    holder, slot = z // 2, z % 2
-    peers = [(base + 1 - k, z)]
-    for kk in range(2):
-        for s in (1, 3):
-            peers.append((base + kk, (z + s) % 4))
-    greet(peers)
-
-    def worker(q):
-        return jnp.where((q == 0) | (q == 3), 0, 1)
-
-    def piece(q, rows=pl.ds(0, 512)):
-        at = jnp.where(q < 2, 0, 1)
-        return src_ref.at[at, rows]
-
-    halves = (pl.ds(0, 256), pl.ds(256, 256))
-    via = (up, down)
-
-    def far(half):
-        return remote(piece(across, halves[half]), relay, far_send.at[half], relay_recv, (r, via[half]))
-
-    def near(i):
-        return remote(piece(via[i]), out_ref.at[slot], send_sem.at[i], recv_sem.at[slot, 0], (base + holder, via[i]))
-
-    def own():
-        return remote(piece(z), out_ref.at[slot], send_sem.at[2], recv_sem.at[slot, 0], (base + 1 - k, z))
-
-    @pl.when(worker(across) == k)
-    def _():
-        far(0).start()
-        far(1).start()
-
-    for i in range(2):
-        @pl.when(worker(via[i]) == k)
-        def _():
-            near(i).start()
-
-    @pl.when((worker(z) == k) & (holder != k))
-    def _():
-        own().start()
-
-    @pl.when((worker(z) == k) & (holder == k))
-    def _():
-        take = pltpu.make_async_copy(piece(z), bounce, own_sem)
-        take.start()
-        take.wait()
-        put = pltpu.make_async_copy(bounce, out_ref.at[slot], own_sem)
-        put.start()
-        put.wait()
-
-    def passing(half):
-        source, target = (down, up) if half == 0 else (up, down)
-        return remote(relay, out_ref.at[source % 2, halves[half]], pass_send, recv_sem.at[source % 2, half],
-                      (base + source // 2, target))
-
-    for half in range(2):
-        @pl.when(worker(via[half]) == k)
-        def _():
-            far(half).wait_recv()
-            passing(half).start()
-            passing(half).wait_send()
+    lax.fori_loop(0, 2, run, 0)
 
     for h in range(2):
-        source = 2 * k + h
-        dist = (source - z) % 4
-        @pl.when((dist == 1) | (dist == 3) | ((dist == 0) & (worker(z) != k)))
-        def _():
-            remote(src_ref.at[0], out_ref.at[h], send_sem.at[0], recv_sem.at[h, 0], (base + 1 - k, z)).wait_recv()
-        @pl.when(dist == 2)
-        def _():
-            for half in range(2):
-                remote(src_ref.at[0, halves[half]], out_ref.at[h, halves[half]], send_sem.at[0],
-                       recv_sem.at[h, half], (base + 1 - k, z)).wait_recv()
-
-    @pl.when(worker(across) == k)
-    def _():
-        far(0).wait_send()
-        far(1).wait_send()
-
-    for i in range(2):
-        @pl.when(worker(via[i]) == k)
-        def _():
-            near(i).wait_send()
-
-    @pl.when((worker(z) == k) & (holder != k))
-    def _():
-        own().wait_send()
+        @pl.when((2 * k + h != z) | (worker(z) != k))
+        def _():
+            for b in range(2):
+                remote(obuf.at[0, block(b)], out_ref.at[h, block(b)], send_sem.at[0, b], recv_sem.at[h, b],
+                       (base + 1 - k, z)).wait_recv()
+    for ss in range(2):
+        for b in range(2):
+            send(ss, b, lambda copy: copy.wait_send())
+    for b in range(2):
+        @pl.when(worker((up, down)[b]) == k)
+        def _():
+            passing(b).wait_send()
 
 
 def local(token_ids, lengths, table, attn_gain, w_qkv, w_out, mlp_gain, w_in, w_down):
@@ -529,24 +529,17 @@
     )(slot, returned)
     r, z = lax.axis_index("rows"), lax.axis_index("cols")
     length = lax.dynamic_slice(asked, (r - r % 2 + z // 2, 3, 1 + z % 2), (1, 1, 1)).reshape(1)
-    done = pl.pallas_call(
+    return pl.pallas_call(
         layer_kernel,
-        out_shape=jax.ShapeDtypeStruct((1024, D), BF),
+        out_shape=jax.ShapeDtypeStruct((2, 512, D), BF),
         in_specs=[SM, VM, VM, VM, VM, VM, ANY, ANY], out_specs=VM,
-        scratch_shapes=[pltpu.VMEM((2048, D), BF), pltpu.VMEM((1024, D), BF)]
-        + [pltpu.VMEM((2048, D), BF)] * 4
-        + [pltpu.VMEM((2, 8, 256, 256), F32), pltpu.VMEM((1024, D), BF),
-           pltpu.VMEM((D, 2 * FF), BF), pltpu.VMEM((FF, D), BF), dma((2,))],
-        compiler_params=params(),
+        scratch_shapes=[pltpu.VMEM((2048, D), BF), pltpu.VMEM((512, D), BF), pltpu.VMEM((2048, D), BF),
+                        pltpu.VMEM((2048, D), BF), pltpu.VMEM((8, 80, 2048), BF), pltpu.VMEM((D, D), BF),
+                        pltpu.VMEM((2, 8, 256, 256), F32), pltpu.VMEM((512, D), BF), pltpu.VMEM((2, 512, D), BF),
+                        pltpu.VMEM((256, D), BF), pltpu.VMEM((D, 2 * FF), BF), pltpu.VMEM((FF, D), BF), dma((2,)),
+                        dma((2, 2)), dma, dma((2, 2)), dma],
+        compiler_params=params(4),
     )(length, full, attn_gain.reshape(1, D), w_qkv, w_out, mlp_gain.reshape(1, D), w_in, w_down)
-    return pl.pallas_call(
-        give_kernel,
-        out_shape=jax.ShapeDtypeStruct((2, 512, D), BF),
-        in_specs=[ANY], out_specs=ANY,
-        scratch_shapes=[pltpu.VMEM((256, D), BF), pltpu.VMEM((512, D), BF), dma((3,)), dma((2,)), dma, dma((2, 2)),
-                        dma, dma],
-        compiler_params=params(4),
-    )(done.reshape(2, 512, D))
 
 
 def solution(mesh):

time: 144 us -> 131 us (0.910)
  Pallas kernels: 138 us -> 126 us
    pallas_call x2 -> x1, Pallas kernels: 52.9 us -> 40.5 us  [local(): pl.pallas_call(layer_kernel, out_shape=jax.ShapeDtypeStruct((2, 512, D),...]
where the time goes in v4:
time: 131 us
  Pallas kernels  126 us (96%)
  local copies, waits for them, and re-layouts  4.81 us (4%)
    pallas_call x1, Pallas kernels, local(): pl.pallas_call(lookup_kernel, out_shape=jax.ShapeDtypeStruct((32, CAP, 12...  42.5 us
    pallas_call x1, Pallas kernels, local(): pl.pallas_call(layer_kernel, out_shape=jax.ShapeDtypeStruct((2, 512, D),...  40.5 us
    pallas_call x1, Pallas kernels, local(): pl.pallas_call(spread_kernel, out_shape=jax.ShapeDtypeStruct((4, 2048, 12...  22.9 us
    pallas_call x1, Pallas kernels, local(): pl.pallas_call(ask_kernel, out_shape=[jax.ShapeDtypeStruct((32, 4, 128),...  20.1 us

profile of v4, /device:TPU:1, one launch (start us, length us, event | category | flops | bytes accessed | tf_op | source)
XLA Modules:
  0.0 130.8 jit_solution(16095270484120809787)
XLA Ops:
  0.0 1.3 reshape.15.mine_ref
  1.3 20.1 %shard_map.91 = (s32[32,4,128]{2,1,0:T(4,128)}, s32[32,128]{1,0:T(8,128)}) custom-call(s32[2]{0:T(128)} %len_ref.1, s32[8,128]{1,0:T(8,128)} %reshape.15.mine_ref), custom_call_target="tpu_custom_call" | custom-call | tf_op jit(solution)/shard_map/pallas_call | solution.py:505
  21.4 1.3 constant_dynamic-slice_fusion
  22.6 42.5 %shard_map.92.back_ref = bf16[32,344,128]{2,1,0:T(8,128)(2,1)} custom-call(s32[16384]{0:T(1024)} %bitcast.4, bf16[16384,128]{1,0:T(8,128)(2,1)} %table_ref.1), custom_call_target="tpu_custom_call" | custom-call | tf_op jit(solution)/shard_map/pallas_call | solution.py:513
  65.1 22.9 %shard_map.93.x_ref = bf16[4,2048,128]{2,1,0:T(8,128)(2,1)} custom-call(s32[32,128]{1,0:T(8,128)} %get-tuple-element.8.slot_ref, bf16[32,344,128]{2,1,0:T(8,128)(2,1)} %shard_map.92.back_ref), custom_call_target="tpu_custom_call" | custom-call | tf_op jit(solution)/shard_map/pallas_call | solution.py:521
  88.0 40.5 %shard_map.94 = bf16[2,512,512]{2,1,0:T(8,128)(2,1)} custom-call(s32[1]{0:T(128)} %bitcast.len_ref, bf16[4,2048,128]{2,1,0:T(8,128)(2,1)} %shard_map.93.x_ref, f32[1,512]{1,0:T(1,128)} %bitcast.5, bf16[512,1536]{1,0:T(8,128)(2,1)} %wqkv_ref.1, bf16[512,512]{1,0:T(8,128)(2,1)} %wout_ref.1, f32[1,512]{1,0:T(1,128)} %bitcast.6, bf16[512,4096]{1,0:T(8,128)(2,1)} %win_hbm.1, ...), custom_call_target="tpu_custom_call" | custom-call | tf_op jit(solution)/shard_map/pallas_call | solution.py:532
  128.6 2.3 %copy.11 = bf16[2,512,512]{2,1,0:T(8,128)(2,1)} copy(bf16[2,512,512]{2,1,0:T(8,128)(2,1)} %shard_map.94) | data formatting | bytes 2097152

commit v5 on v4

--- a/solution.py
+++ b/solution.py
@@ -295,7 +295,7 @@
 
 
 def layer_kernel(len_ref, x_ref, gain_ref, wqkv_ref, wout_ref, gain2_ref, win_hbm, wdown_hbm, out_ref,
-                 nrm, qs, ke, ko, vt, wvt, sc, att, obuf, relay, win_ref, wdown_ref, sems,
+                 nrm, qs, ke, ko, vt, wvt, sc, att, hid, act, obuf, relay, win_ref, wdown_ref, sems,
                  send_sem, far_recv, recv_sem, pass_send):
     r, z, _, _, k = place()
     base = r - k
@@ -361,7 +361,7 @@
         wvt[128 * c : 128 * c + 128, :] = wqkv_ref[:, 2 * D + 128 * c : 2 * D + 128 * c + 128].astype(F32).T.astype(BF)
 
     def project(i, _):
-        rows = pl.ds(pl.multiple_of(i * 256, 256), 256)
+        rows = pl.ds(pl.multiple_of(i * 512, 512), 512)
         parts = [x_ref[c, rows, :].astype(F32) for c in range(4)]
         square = parts[0] * parts[0]
         for part in parts[1:]:
@@ -372,10 +372,10 @@
         nrm[rows, :] = here
         keys = dot(here, wqkv_ref[:, D : 2 * D])
         vals = dot_t(wvt[...], here)
-        lane = lax.broadcasted_iota(jnp.int32, (256, 128), 1)
-        pos = lax.broadcasted_iota(jnp.int32, (256, 128), 0) + i * 256
+        lane = lax.broadcasted_iota(jnp.int32, (512, 128), 1)
+        pos = lax.broadcasted_iota(jnp.int32, (512, 128), 0) + i * 512
         bias = jnp.where(pos < length, 0.0, NEG)
-        tail = jnp.where(lax.broadcasted_iota(jnp.int32, (16, 256), 0) == 0, 1.0, 0.0).astype(BF)
+        tail = jnp.where(lax.broadcasted_iota(jnp.int32, (16, 512), 0) == 0, 1.0, 0.0).astype(BF)
         for c in range(4):
             cols = slice(128 * c, 128 * c + 128)
             ke[rows, cols] = jnp.where(lane == 64, bias, keys[:, cols]).astype(BF)
@@ -385,44 +385,67 @@
             vt[h, 64:80, rows] = tail
         return 0
 
-    lax.fori_loop(0, 8, project, 0)
+    lax.fori_loop(0, 4, project, 0)
 
     def attend(quarter):
-        def heads(hp, _):
-            cols = pl.ds(pl.multiple_of(hp * 128, 128), 128)
-            lane = lax.broadcasted_iota(jnp.int32, (256, 128), 1)
-            tri = (lax.broadcasted_iota(jnp.int32, (256, 256), 0)
-                   <= lax.broadcasted_iota(jnp.int32, (256, 256), 1))
-            for j in range(2):
-                n = 2 * quarter + j + 1
-                at = 256 * j
-                q = qs[at : at + 256, cols].astype(F32)
-                outs = []
-                for odd in range(2):
-                    kref = ko if odd else ke
-                    if odd:
-                        qa = jnp.where(lane >= 64, q, jnp.where(lane == 0, 1.0, 0.0)).astype(BF)
-                    else:
-                        qa = jnp.where(lane < 64, q, jnp.where(lane == 64, 1.0, 0.0)).astype(BF)
-                    top = None
-                    for c in range(n):
-                        s = dot_t(kref[256 * c : 256 * c + 256, cols], qa)
-                        if c == n - 1:
-                            s = jnp.where(tri, s, NEG)
-                        sc[odd, c] = s
-                        m = jnp.max(s.reshape(4, 8, 8, 256), axis=1)
-                        top = m if top is None else jnp.maximum(top, m)
-                    top = jnp.max(jnp.max(top, axis=0), axis=0, keepdims=True)
-                    acc = None
-                    for c in range(n):
-                        p = jnp.exp2(sc[odd, c] - top).astype(BF)
+        lane = lax.broadcasted_iota(jnp.int32, (256, 128), 1)
+        tri = (lax.broadcasted_iota(jnp.int32, (256, 256), 0)
+               <= lax.broadcasted_iota(jnp.int32, (256, 256), 1))
+        order = [(0, 0), (0, 1), (1, 0), (1, 1)]
+
+        def tiles(j):
+            return 2 * quarter + j + 1
+
+        def columns(hp):
+            return pl.ds(pl.multiple_of(hp * 128, 128), 128)
+
+        def query(hp, g):
+            j, odd = order[g]
+            q = qs[256 * j : 256 * j + 256, columns(hp)].astype(F32)
+            if odd:
+                return jnp.where(lane >= 64, q, jnp.where(lane == 0, 1.0, 0.0)).astype(BF)
+            return jnp.where(lane < 64, q, jnp.where(lane == 64, 1.0, 0.0)).astype(BF)
+
+        def score(hp, g, qa, c, top):
+            j, odd = order[g]
+            s = dot_t((ko if odd else ke)[256 * c : 256 * c + 256, columns(hp)], qa)
+            if c == tiles(j) - 1:
+                s = jnp.where(tri, s, NEG)
+            sc[g % 2, c] = s
+            m = jnp.max(s.reshape(4, 8, 8, 256), axis=1)
+            return m if top is None else jnp.maximum(top, m)
+
+        def finish(top):
+            return jnp.max(jnp.max(top, axis=0), axis=0, keepdims=True)
+
+        def first_scores(hp):
+            qa, top = query(hp, 0), None
+            for c in range(tiles(0)):
+                top = score(hp, 0, qa, c, top)
+            return finish(top)
+
+        def heads(hp, top):
+            outs = []
+            after = jnp.minimum(hp + 1, 3)
+            for g, (j, odd) in enumerate(order):
+                ahead, hp_ahead = (g + 1) % 4, hp if g < 3 else after
+                qa, top_ahead, acc = query(hp_ahead, ahead), None, None
+                n, n_ahead = tiles(j), tiles(order[ahead][0])
+                for c in range(max(n, n_ahead)):
+                    if c < n_ahead:
+                        top_ahead = score(hp_ahead, ahead, qa, c, top_ahead)
+                    if c < n:
+                        p = jnp.exp2(sc[g % 2, c] - top).astype(BF)
                         o = dot(vt[2 * hp + odd, :, 256 * c : 256 * c + 256], p)
                         acc = o if acc is None else acc + o
-                    outs.append(acc[0:64, :] / acc[64:65, :])
-                att[at : at + 256, cols] = jnp.concatenate(outs, axis=0).T.astype(BF)
-            return 0
-
-        lax.fori_loop(0, 4, heads, 0)
+                outs.append(acc[0:64, :] / acc[64:65, :])
+                if odd:
+                    att[256 * j : 256 * j + 256, columns(hp)] = jnp.concatenate(outs, axis=0).T.astype(BF)
+                    outs = []
+                top = finish(top_ahead)
+            return top
+
+        lax.fori_loop(0, 4, heads, first_scores(0))
 
     def compute_attention(quarter):
         rows = pl.ds(pl.multiple_of(quarter * 512, 512), 512)
@@ -432,26 +455,28 @@
             def _():
                 attend(q)
 
-    def mlp(step, b, quarter):
+    def mlp(quarter):
+        src = pl.ds(pl.multiple_of(quarter * 512, 512), 512)
+        resid = jnp.concatenate([x_ref[c, src, :].astype(F32) for c in range(4)], axis=1)
+        hidden = (resid + dot(att[...], wout_ref[...])).astype(BF)
+        hid[...] = hidden
+        hidden = hidden.astype(F32)
+        scale = lax.rsqrt(jnp.mean(hidden * hidden, axis=1, keepdims=True) + 1e-6)
+        att[...] = (hidden * scale * gain2_ref[...]).astype(BF)
+
+        for f in range(0, FF, 256):
+            gate = dot(att[...], win_ref[:, f : f + 256])
+            high = dot(att[...], win_ref[:, FF + f : FF + f + 256])
+            act[:, f : f + 256] = (gate / (1.0 + jnp.exp(-gate)) * high).astype(BF)
+
+    def lower(step, b, quarter):
         rows = pl.ds(pl.multiple_of(256 * b, 256), 256)
-        src = pl.ds(pl.multiple_of(quarter * 512 + b * 256, 256), 256)
-        resid = jnp.concatenate([x_ref[c, src, :].astype(F32) for c in range(4)], axis=1)
-        hidden = (resid + dot(att[rows, :], wout_ref[...])).astype(BF).astype(F32)
-        scale = lax.rsqrt(jnp.mean(hidden * hidden, axis=1, keepdims=True) + 1e-6)
-        normed = (hidden * scale * gain2_ref[...]).astype(BF)
-        out = hidden
-        for f in range(4):
-            cols = slice(512 * f, 512 * f + 512)
-            up_cols = slice(FF + 512 * f, FF + 512 * f + 512)
-            gate = dot(normed, win_ref[:, cols])
-            high = dot(normed, win_ref[:, up_cols])
-            act = (gate / (1.0 + jnp.exp(-gate)) * high).astype(BF)
-            out = out + dot(act, wdown_ref[cols, :])
-        obuf[step, rows, :] = out.astype(BF)
+        out = (hid[rows, :].astype(F32) + dot(act[rows, :], wdown_ref[...])).astype(BF)
+        obuf[step, rows, :] = out
 
         @pl.when((quarter == z) & (holder == k))
         def _():
-            out_ref[slot, rows, :] = out.astype(BF)
+            out_ref[slot, rows, :] = out
 
     def run(step, _):
         quarter = quarter_of(step)
@@ -471,8 +496,10 @@
                     far(b).wait_recv()
                     passing(b).start()
 
+        mlp(quarter)
+
         def each(b, _):
-            mlp(step, b, quarter)
+            lower(step, b, quarter)
             for ss in range(2):
                 for bb in range(2):
                     @pl.when((step == ss) & (b == bb))
@@ -535,7 +562,8 @@
         in_specs=[SM, VM, VM, VM, VM, VM, ANY, ANY], out_specs=VM,
         scratch_shapes=[pltpu.VMEM((2048, D), BF), pltpu.VMEM((512, D), BF), pltpu.VMEM((2048, D), BF),
                         pltpu.VMEM((2048, D), BF), pltpu.VMEM((8, 80, 2048), BF), pltpu.VMEM((D, D), BF),
-                        pltpu.VMEM((2, 8, 256, 256), F32), pltpu.VMEM((512, D), BF), pltpu.VMEM((2, 512, D), BF),
+                        pltpu.VMEM((2, 8, 256, 256), F32), pltpu.VMEM((512, D), BF), pltpu.VMEM((512, D), BF),
+                        pltpu.VMEM((512, FF), BF), pltpu.VMEM((2, 512, D), BF),
                         pltpu.VMEM((256, D), BF), pltpu.VMEM((D, 2 * FF), BF), pltpu.VMEM((FF, D), BF), dma((2,)),
                         dma((2, 2)), dma, dma((2, 2)), dma],
         compiler_params=params(4),

time: 131 us -> 127 us (0.969)
  Pallas kernels: 126 us -> 122 us
    pallas_call x1, Pallas kernels: 40.5 us -> 36.2 us  [local(): pl.pallas_call(layer_kernel, out_shape=jax.ShapeDtypeStruct((2, 512, D),...]
where the time goes in v5:
time: 127 us; the launch traced here: 126 us
  Pallas kernels  122 us (96%)
  local copies, waits for them, and re-layouts  4.81 us (4%)
    pallas_call x1, Pallas kernels, local(): pl.pallas_call(lookup_kernel, out_shape=jax.ShapeDtypeStruct((32, CAP, 12...  42.5 us
    pallas_call x1, Pallas kernels, local(): pl.pallas_call(layer_kernel, out_shape=jax.ShapeDtypeStruct((2, 512, D),...  36.2 us
    pallas_call x1, Pallas kernels, local(): pl.pallas_call(spread_kernel, out_shape=jax.ShapeDtypeStruct((4, 2048, 12...  22.9 us
    pallas_call x1, Pallas kernels, local(): pl.pallas_call(ask_kernel, out_shape=[jax.ShapeDtypeStruct((32, 4, 128),...  20.1 us

profile of v5, /device:TPU:1, one launch (start us, length us, event | category | flops | bytes accessed | tf_op | source)
XLA Modules:
  0.0 126.5 jit_solution(16083871376441249297)
XLA Ops:
  0.0 1.3 %reshape.15.mine_ref = s32[8,128]{1,0:T(8,128)} reshape(s32[2,512]{1,0:T(2,128)} %param.9) | data formatting | bytes 8192 | tf_op jit(solution)/shard_map/reshape | solution.py:539
  1.3 20.1 %shard_map.91 = (s32[32,4,128]{2,1,0:T(4,128)}, s32[32,128]{1,0:T(8,128)}) custom-call(s32[2]{0:T(128)} %len_ref.1, s32[8,128]{1,0:T(8,128)} %reshape.15.mine_ref), custom_call_target="tpu_custom_call" | custom-call | tf_op jit(solution)/shard_map/pallas_call | solution.py:532
  21.4 1.3 constant_dynamic-slice_fusion
  22.6 42.5 %shard_map.92.back_ref = bf16[32,344,128]{2,1,0:T(8,128)(2,1)} custom-call(s32[16384]{0:T(1024)} %bitcast.4, bf16[16384,128]{1,0:T(8,128)(2,1)} %table_ref.1), custom_call_target="tpu_custom_call" | custom-call | tf_op jit(solution)/shard_map/pallas_call | solution.py:540
  65.1 22.9 %shard_map.93.x_ref = bf16[4,2048,128]{2,1,0:T(8,128)(2,1)} custom-call(s32[32,128]{1,0:T(8,128)} %get-tuple-element.8.slot_ref, bf16[32,344,128]{2,1,0:T(8,128)(2,1)} %shard_map.92.back_ref), custom_call_target="tpu_custom_call" | custom-call | tf_op jit(solution)/shard_map/pallas_call | solution.py:548
  88.0 36.2 %shard_map.94 = bf16[2,512,512]{2,1,0:T(8,128)(2,1)} custom-call(s32[1]{0:T(128)} %bitcast.len_ref, bf16[4,2048,128]{2,1,0:T(8,128)(2,1)} %shard_map.93.x_ref, f32[1,512]{1,0:T(1,128)} %bitcast.5, bf16[512,1536]{1,0:T(8,128)(2,1)} %wqkv_ref.1, bf16[512,512]{1,0:T(8,128)(2,1)} %wout_ref.1, f32[1,512]{1,0:T(1,128)} %bitcast.6, bf16[512,4096]{1,0:T(8,128)(2,1)} %win_hbm.1, ...), custom_call_target="tpu_custom_call" | custom-call | tf_op jit(solution)/shard_map/pallas_call | solution.py:559
  124.2 2.3 %copy.11 = bf16[2,512,512]{2,1,0:T(8,128)(2,1)} copy(bf16[2,512,512]{2,1,0:T(8,128)(2,1)} %shard_map.94) | data formatting | bytes 2097152

commit v6 on v5

--- a/solution.py
+++ b/solution.py
@@ -51,68 +51,6 @@
     if collective_id is not None:
         kw = dict(collective_id=collective_id, has_side_effects=True)
     return pltpu.CompilerParams(vmem_limit_bytes=vmem * 2**20, **kw)
-
-
-def ask_kernel(len_ref, mine_ref, out_ref, slot_ref, ids_ref, msg_ref, ids_send, ids_recv, send_sem, recv_sem):
-    r, z, _, _, _ = place()
-    near = [(r, (z + s) % 4) for s in (1, 2, 3)]
-    peers = [((r + s) % 32, z) for s in range(1, 32)]
-    greet(near + peers)
-    copies = []
-    for s, device in enumerate(near):
-        copy = remote(mine_ref, ids_ref.at[z], ids_send.at[s], ids_recv.at[s], device)
-        copy.start()
-        copies.append(copy)
-    ids_ref[z] = mine_ref[...]
-    before = (lax.broadcasted_iota(jnp.int32, (128, 128), 0)
-              < lax.broadcasted_iota(jnp.int32, (128, 128), 1)).astype(F32)
-    above = (lax.broadcasted_iota(jnp.int32, (32, 32), 1)
-             < lax.broadcasted_iota(jnp.int32, (32, 32), 0)).astype(F32).astype(BF)
-    both = jnp.concatenate([before, jnp.ones((128, 128), F32)], axis=0).astype(BF)
-    owners = lax.broadcasted_iota(jnp.int32, (32, 128), 0)
-    ks = lax.broadcasted_iota(jnp.int32, (384, 128), 0)
-    lane = lax.broadcasted_iota(jnp.int32, (32, 128), 1)
-    for copy in copies:
-        copy.wait()
-    ids = ids_ref[...].reshape(32, 128)
-    owner = ids >> 14
-    low, high = (ids & 127).astype(F32), ((ids >> 7) & 127).astype(F32)
-    ones = [jnp.where(owner == o, 1.0, 0.0).astype(BF) for o in range(32)]
-    rows_above = dot(above, jnp.concatenate(ones, axis=1)).astype(BF)
-    prior = dot(
-        jnp.concatenate(
-            [jnp.concatenate(ones, axis=0),
-             jnp.concatenate([rows_above[:, 128 * o : 128 * o + 128] for o in range(32)], axis=0)], axis=1),
-        both)
-    rank = jnp.zeros((32, 128), F32)
-    for o in range(32):
-        rank = rank + jnp.where(owner == o, prior[32 * o : 32 * o + 32], 0.0)
-    rank_i = rank.astype(jnp.int32)
-    acc = jnp.zeros((64, 384), F32)
-    count = jnp.zeros((32, 128), F32)
-    for a in range(0, 32, 2):
-        lefts, rights = [], []
-        for b in (a, a + 1):
-            hit = owners == owner[b : b + 1, :]
-            count = count + jnp.where(hit, 1.0, 0.0)
-            lefts.append(jnp.concatenate(
-                [jnp.where(hit, low[b : b + 1, :], 0.0), jnp.where(hit, high[b : b + 1, :], 0.0)], axis=0).astype(BF))
-            rights.append(jnp.where(ks == rank_i[b : b + 1, :], 1.0, 0.0).astype(BF))
-        acc = acc + dot_t(jnp.concatenate(lefts, axis=1), jnp.concatenate(rights, axis=1))
-    req = (acc[32:] * 128.0 + acc[:32]).astype(jnp.int32)
-    for j in range(3):
-        msg_ref[:, j, :] = req[:, 128 * j : 128 * j + 128]
-    tail = jnp.where(lane == 1, len_ref[0], jnp.where(lane == 2, len_ref[1], 0))
-    msg_ref[:, 3, :] = tail
-    slot_ref[...] = owner * CAP + rank_i
-    copies = []
-    for s, device in enumerate(peers):
-        copy = remote(msg_ref.at[device[0]], out_ref.at[r], send_sem.at[s], recv_sem.at[s], device)
-        copy.start()
-        copies.append(copy)
-    out_ref[r] = msg_ref[r]
-    for copy in copies:
-        copy.wait()
 
 
 def routes():
@@ -131,18 +69,82 @@
     return sorted(out, key=key)
 
 
-def lookup_kernel(asked_ref, table_ref, out_ref, wide, stage, block, relay, send_sem, recv_sem, hop_send, hop_recv):
+def requests(ids, lens, msg_ref, slot_ref):
+    before = (lax.broadcasted_iota(jnp.int32, (128, 128), 0)
+              < lax.broadcasted_iota(jnp.int32, (128, 128), 1)).astype(F32)
+    above = (lax.broadcasted_iota(jnp.int32, (32, 32), 1)
+             < lax.broadcasted_iota(jnp.int32, (32, 32), 0)).astype(F32).astype(BF)
+    both = jnp.concatenate([before, jnp.ones((128, 128), F32)], axis=0).astype(BF)
+    owners = lax.broadcasted_iota(jnp.int32, (32, 128), 0)
+    column = lax.broadcasted_iota(jnp.int32, (4 * 128, 128), 0)
+    ks = jnp.where((column & 127) < CAP // 4, (column >> 7) * (CAP // 4) + (column & 127), -1)
+    lane = lax.broadcasted_iota(jnp.int32, (32, 128), 1)
+    owner = ids >> 14
+    low, high = (ids & 127).astype(F32), ((ids >> 7) & 127).astype(F32)
+    ones = [jnp.where(owner == o, 1.0, 0.0).astype(BF) for o in range(32)]
+    rows_above = dot(above, jnp.concatenate(ones, axis=1)).astype(BF)
+    prior = dot(
+        jnp.concatenate(
+            [jnp.concatenate(ones, axis=0),
+             jnp.concatenate([rows_above[:, 128 * o : 128 * o + 128] for o in range(32)], axis=0)], axis=1),
+        both)
+    rank = jnp.zeros((32, 128), F32)
+    for o in range(32):
+        rank = rank + jnp.where(owner == o, prior[32 * o : 32 * o + 32], 0.0)
+    rank_i = rank.astype(jnp.int32)
+    slot_ref[...] = jnp.clip(owner * CAP + rank_i, 0, 32 * CAP - 1)
+    acc = jnp.zeros((64, 4 * 128), F32)
+    for a in range(0, 32, 2):
+        lefts, rights = [], []
+        for b in (a, a + 1):
+            hit = owners == owner[b : b + 1, :]
+            lefts.append(jnp.concatenate(
+                [jnp.where(hit, low[b : b + 1, :], 0.0), jnp.where(hit, high[b : b + 1, :], 0.0)], axis=0).astype(BF))
+            rights.append(jnp.where(ks == rank_i[b : b + 1, :], 1.0, 0.0).astype(BF))
+        acc = acc + dot_t(jnp.concatenate(lefts, axis=1), jnp.concatenate(rights, axis=1))
+    req = (acc[32:] * 128.0 + acc[:32]).astype(jnp.int32)
+    req0 = jnp.where(lane == 126, lens[0], jnp.where(lane == 127, lens[1], req[:, :128]))
+    msg_ref[:, 0, :] = req0
+    for j in range(1, 4):
+        msg_ref[:, j, :] = req[:, 128 * j : 128 * j + 128]
+
+
+def front_kernel(len_ref, tok_ref, table_hbm, out_ref, lens_ref,
+                 ids_ref, msg_ref, asked_v, asked_s, slot_v, slot_s, table_ref, wide, stage, block, relay, back, emb,
+                 relay_z, ids_send, ids_recv, ask_send, ask_recv, copy_sem, send_sem, recv_sem, hop_send, hop_recv,
+                 z_send, z_relay_send, z_relay_recv, z_recv, pass_send, pass_recv, own_send, own_recv):
     r, z, y, x, k = place()
-
-    def row(dy, dx, dk):
-        return (((y + dy) % 4) * 4 + (x + dx) % 4) * 2 + (k + dk) % 2
-
-    flows = routes()
-    hops = [f for f in flows if f[3] is not None]
-    direct = [f for f in flows if f[3] is None]
-    barrier = pltpu.get_barrier_semaphore()
-    for s in range(1, 32):
-        pl.semaphore_signal(barrier, inc=1, device_id=((r + s) % 32, z), device_id_type=MESH)
+    base = r - k
+    other = (base + 1 - k, z)
+    up, down = (z + 1) % 4, (z + 3) % 4
+    holder = z // 2
+    column = [(r, (z + s) % 4) for s in (1, 2, 3)]
+    plane = [((r + s) % 32, z) for s in range(1, 32)]
+    load = pltpu.make_async_copy(table_hbm, table_ref, copy_sem.at[0])
+    load.start()
+    greet(column + plane + [(base + 1 - k, up), (base + 1 - k, down)])
+
+    copies = []
+    for s, device in enumerate(column):
+        copy = remote(tok_ref, ids_ref.at[z], ids_send.at[s], ids_recv.at[s], device)
+        copy.start()
+        copies.append(copy)
+    ids_ref[z] = tok_ref[...]
+    for copy in copies:
+        copy.wait()
+    ids = jnp.concatenate(
+        [ids_ref[c, h : h + 1, 128 * j : 128 * j + 128] for c in range(4) for h in range(2) for j in range(4)], axis=0)
+    requests(ids, (len_ref[0], len_ref[1]), msg_ref, slot_v)
+
+    copies = []
+    for s, device in enumerate(plane):
+        copy = remote(msg_ref.at[device[0]], asked_v.at[r], ask_send.at[s], ask_recv.at[s], device)
+        copy.start()
+        copies.append(copy)
+    asked_v[r] = msg_ref[r]
+    to_slots = pltpu.make_async_copy(slot_v, slot_s, copy_sem.at[1])
+    to_slots.start()
+    load.wait()
 
     def widen(i, _):
         rows = pl.ds(pl.multiple_of(i * 256, 256), 256)
@@ -150,18 +152,30 @@
         return 0
 
     lax.fori_loop(0, 64, widen, 0)
-    pl.semaphore_wait(barrier, 31)
+    for copy in copies:
+        copy.wait()
+    asked_v[...] = jnp.clip(asked_v[...], 0, 16383)
+    to_asked = pltpu.make_async_copy(asked_v, asked_s, copy_sem.at[2])
+    to_asked.start()
+    to_asked.wait()
+    to_slots.wait()
+    lens_ref[...] = asked_v[base + holder, 0:1, :]
+
+    def row(dy, dx, dk):
+        return (((y + dy) % 4) * 4 + (x + dx) % 4) * 2 + (k + dk) % 2
 
     def fill(p, dst):
         def some(j, _):
-            base = j * 43
-            for i in range(43):
-                stage[pl.ds(base + i, 1), :] = wide[pl.ds(asked_ref[p * 512 + base + i], 1), :]
+            for i in range(CAP // 4):
+                stage[pl.ds(j * (CAP // 4) + i, 1), :] = wide[pl.ds(asked_s[p, j, i], 1), :]
             return 0
 
-        lax.fori_loop(0, 8, some, 0)
-        dst[...] = stage[...].astype(BF)
-
+        lax.fori_loop(0, 4, some, 0)
+        dst[...] = stage[0:CAP, :].astype(BF)
+
+    flows = routes()
+    hops = [f for f in flows if f[3] is not None]
+    direct = [f for f in flows if f[3] is None]
     first, final, waiting = [], [], None
     for n, (dy, dx, dk, hop) in enumerate(hops + direct):
         p = row(dy, dx, dk)
@@ -171,60 +185,42 @@
             first.append(copy)
         else:
             i = n - len(hops)
-            copy = remote(block.at[n], out_ref.at[r], send_sem.at[i], recv_sem.at[i], (p, z))
-            final.append(copy)
+            copy = remote(block.at[n], back.at[r], send_sem.at[i], recv_sem.at[i], (p, z))
+            final.append((copy, row(-dy, -dx, dk)))
         if waiting is not None:
             waiting.start()
         waiting = copy
-    fill(r, out_ref.at[r])
+    fill(r, back.at[r])
     waiting.start()
     for i, (dy, dx, dk, (hy, hx)) in enumerate(hops):
         first[i].wait_recv()
         n = len(direct) + i
-        copy = remote(relay.at[i], out_ref.at[row(-hy, -hx, 0)], send_sem.at[n], recv_sem.at[n],
+        copy = remote(relay.at[i], back.at[row(-hy, -hx, 0)], send_sem.at[n], recv_sem.at[n],
                       (row(dy - hy, dx - hx, dk), z))
         copy.start()
-        final.append(copy)
-    for copy in first:
-        copy.wait_send()
-    for copy in final:
-        copy.wait()
-
-
-def spread_kernel(slot_ref, back_ref, out_ref, wide, stage, emb, relay, send_sem, relay_send, relay_recv, recv_sem,
-                  pass_send, pass_recv, own_send, own_recv):
-    r, z, y, x, k = place()
-    base = r - k
-    other = (base + 1 - k, z)
-    up, down = (z + 1) % 4, (z + 3) % 4
-    holder = z // 2
+        final.append((copy, row(-dy, -dx, dk)))
+
+    def spread(source):
+        wide[pl.ds(pl.multiple_of(source * CAP, 8), CAP), :] = back[source].astype(F32)
+
+    spread(r)
+    for copy, source in final:
+        copy.wait_recv()
+        spread(source)
+
     mine = pl.ds(pl.multiple_of(1024 * k, 1024), 1024)
     theirs = pl.ds(pl.multiple_of(1024 * (1 - k), 1024), 1024)
-    peers = [(base + 1 - k, z)]
-    for kk in range(2):
-        for s in (1, 3):
-            peers.append((base + kk, (z + s) % 4))
-    barrier = pltpu.get_barrier_semaphore()
-    for device in peers:
-        pl.semaphore_signal(barrier, inc=1, device_id=device, device_id_type=MESH)
-
-    def widen(i, _):
-        wide[pl.ds(pl.multiple_of(i * CAP, 8), CAP), :] = back_ref[i].astype(F32)
-        return 0
-
-    lax.fori_loop(0, 32, widen, 0)
-    pl.semaphore_wait(barrier, len(peers))
 
     def part(i):
         return pl.ds(1024 * i, 1024)
 
     def far(h, half):
-        return remote(emb.at[h, part(half)], relay, relay_send.at[half], relay_recv,
+        return remote(emb.at[h, part(half)], relay_z, z_relay_send.at[half], z_relay_recv,
                       (base + half, up if half == 0 else down))
 
     def near(h, half, step):
         return remote(emb.at[h, part(half)], out_ref.at[z, part(half)],
-                      send_sem.at[step // 2, half], recv_sem.at[step // 2], (base + half, (z + step) % 4))
+                      z_send.at[step // 2, half], z_recv.at[step // 2], (base + half, (z + step) % 4))
 
     def own(h, half):
         return remote(emb.at[h, part(half)], out_ref.at[z, part(half)], own_send.at[half], own_recv.at[half], other)
@@ -252,7 +248,7 @@
         def gather(j, _):
             a = (half * 2 + j // 4) * 8 + h * 4 + lax.rem(j, 4)
             for i in range(128):
-                stage[pl.ds(j * 128 + i, 1), :] = wide[pl.ds(slot_ref[a, i], 1), :]
+                stage[pl.ds(j * 128 + i, 1), :] = wide[pl.ds(slot_s[a, i], 1), :]
             return 0
 
         lax.fori_loop(0, 8, gather, 0)
@@ -269,16 +265,20 @@
 
     behind = jnp.where(k == 0, down, up)
     ahead = jnp.where(k == 0, up, down)
-    relayed = remote(relay, out_ref.at[behind, mine], pass_send.at[3], recv_sem.at[2], (r, ahead))
+    relayed = remote(relay_z, out_ref.at[behind, mine], pass_send.at[3], z_recv.at[2], (r, ahead))
     far(0, 0).wait_recv()
     relayed.start()
     passed = []
     for i, source in enumerate((down, up, (z + 2) % 4)):
         got = out_ref.at[source, mine]
-        remote(got, got, pass_send.at[i], recv_sem.at[i], other).wait_recv()
+        remote(got, got, pass_send.at[i], z_recv.at[i], other).wait_recv()
         copy = remote(got, got, pass_send.at[i], pass_recv.at[i], other)
         copy.start()
         passed.append(copy)
+    for copy in first:
+        copy.wait_send()
+    for copy, _ in final:
+        copy.wait_send()
 
     for i, source in enumerate((down, up, (z + 2) % 4)):
         passed[i].wait_send()
@@ -312,7 +312,7 @@
     get_down = pltpu.make_async_copy(wdown_hbm, wdown_ref, sems.at[1])
     get_in.start()
     get_down.start()
-    length = len_ref[0]
+    length = len_ref[0, 126 + z % 2]
 
     def worker(q):
         return jnp.where((q == 0) | (q == 3), 0, 1)
@@ -529,33 +529,20 @@
 
 def local(token_ids, lengths, table, attn_gain, w_qkv, w_out, mlp_gain, w_in, w_down):
     dma = pltpu.SemaphoreType.DMA
-    asked, slot = pl.pallas_call(
-        ask_kernel,
-        out_shape=[jax.ShapeDtypeStruct((32, 4, 128), jnp.int32), jax.ShapeDtypeStruct((32, 128), jnp.int32)],
-        in_specs=[SM, VM], out_specs=[VM, VM],
-        scratch_shapes=[pltpu.VMEM((4, 8, 128), jnp.int32), pltpu.VMEM((32, 4, 128), jnp.int32),
-                        dma((3,)), dma((3,)), dma((31,)), dma((31,))],
+    full, lens = pl.pallas_call(
+        front_kernel,
+        out_shape=[jax.ShapeDtypeStruct((4, 2048, 128), BF), jax.ShapeDtypeStruct((1, 128), jnp.int32)],
+        in_specs=[SM, VM, ANY], out_specs=[VM, VM],
+        scratch_shapes=[
+            pltpu.VMEM((4, 2, 512), jnp.int32), pltpu.VMEM((32, 4, 128), jnp.int32), pltpu.VMEM((32, 4, 128), jnp.int32),
+            pltpu.SMEM((32, 4, 128), jnp.int32), pltpu.VMEM((32, 128), jnp.int32), pltpu.SMEM((32, 128), jnp.int32),
+            pltpu.VMEM((16384, 128), BF), pltpu.VMEM((16384, 128), F32), pltpu.VMEM((1024, 128), F32),
+            pltpu.VMEM((31, CAP, 128), BF), pltpu.VMEM((14, CAP, 128), BF), pltpu.VMEM((32, CAP, 128), BF),
+            pltpu.VMEM((2, 2048, 128), BF), pltpu.VMEM((1024, 128), BF),
+            dma((3,)), dma((3,)), dma((31,)), dma((31,)), dma((3,)), dma((31,)), dma((31,)), dma((14,)), dma((14,)),
+            dma((2, 2)), dma((2,)), dma, dma((3,)), dma((4,)), dma((3,)), dma((2,)), dma((2,))],
         compiler_params=params(1),
-    )(lengths, token_ids.reshape(8, 128))
-    returned = pl.pallas_call(
-        lookup_kernel,
-        out_shape=jax.ShapeDtypeStruct((32, CAP, 128), BF),
-        in_specs=[SM, VM], out_specs=VM,
-        scratch_shapes=[pltpu.VMEM((16384, 128), F32), pltpu.VMEM((CAP, 128), F32), pltpu.VMEM((31, CAP, 128), BF),
-                        pltpu.VMEM((14, CAP, 128), BF), dma((31,)), dma((31,)), dma((14,)), dma((14,))],
-        compiler_params=params(2),
-    )(asked.reshape(32 * 512), table)
-    full = pl.pallas_call(
-        spread_kernel,
-        out_shape=jax.ShapeDtypeStruct((4, 2048, 128), BF),
-        in_specs=[SM, VM], out_specs=VM,
-        scratch_shapes=[pltpu.VMEM((32 * CAP, 128), F32), pltpu.VMEM((1024, 128), F32), pltpu.VMEM((2, 2048, 128), BF),
-                        pltpu.VMEM((1024, 128), BF), dma((2, 2)), dma((2,)), dma, dma((3,)), dma((4,)), dma((3,)),
-                        dma((2,)), dma((2,))],
-        compiler_params=params(3),
-    )(slot, returned)
-    r, z = lax.axis_index("rows"), lax.axis_index("cols")
-    length = lax.dynamic_slice(asked, (r - r % 2 + z // 2, 3, 1 + z % 2), (1, 1, 1)).reshape(1)
+    )(lengths, token_ids, table)
     return pl.pallas_call(
         layer_kernel,
         out_shape=jax.ShapeDtypeStruct((2, 512, D), BF),
@@ -566,8 +553,8 @@
                         pltpu.VMEM((512, FF), BF), pltpu.VMEM((2, 512, D), BF),
                         pltpu.VMEM((256, D), BF), pltpu.VMEM((D, 2 * FF), BF), pltpu.VMEM((FF, D), BF), dma((2,)),
                         dma((2, 2)), dma, dma((2, 2)), dma],
-        compiler_params=params(4),
-    )(length, full, attn_gain.reshape(1, D), w_qkv, w_out, mlp_gain.reshape(1, D), w_in, w_down)
+        compiler_params=params(2),
+    )(lens, full, attn_gain.reshape(1, D), w_qkv, w_out, mlp_gain.reshape(1, D), w_in, w_down)
 
 
 def solution(mesh):

time: 127 us -> 115 us (0.906)
  Pallas kernels: 122 us -> 111 us
  local copies, waits for them, and re-layouts: 4.81 us -> 2.26 us
    pallas_call x3 -> x1, Pallas kernels: 85.5 us -> 75.6 us  [local(): pl.pallas_call(front_kernel, out_shape=[jax.ShapeDtypeStruct((4, 2048, 12...]
    reshape x1 -> x0, local copies, waits for them, and re-layouts: 1.29 us -> none  [local(): token_ids.reshape(8, 128)]
where the time goes in v6:
time: 115 us; the launch traced here: 114 us
  Pallas kernels  111 us (97%)
  local copies, waits for them, and re-layouts  2.26 us (2%)
    pallas_call x1, Pallas kernels, local(): pl.pallas_call(front_kernel, out_shape=[jax.ShapeDtypeStruct((4, 2048, 12...  75.6 us
    pallas_call x1, Pallas kernels, local(): pl.pallas_call(layer_kernel, out_shape=jax.ShapeDtypeStruct((2, 512, D),...  35.6 us

profile of v6, /device:TPU:1, one launch (start us, length us, event | category | flops | bytes accessed | tf_op | source)
XLA Modules:
  0.0 113.5 jit_solution(10312238069500936240)
XLA Ops:
  0.0 75.6 %shard_map.91 = (bf16[4,2048,128]{2,1,0:T(8,128)(2,1)}, s32[1,128]{1,0:T(1,128)}) custom-call(s32[2]{0:T(128)} %len_ref.1, s32[2,512]{1,0:T(2,128)} %tok_ref.1, bf16[16384,128]{1,0:T(8,128)(2,1)} %table_hbm.1), custom_call_target="tpu_custom_call" | custom-call | tf_op jit(solution)/shard_map/pallas_call | solution.py:532
  75.7 35.6 %shard_map.92 = bf16[2,512,512]{2,1,0:T(8,128)(2,1)} custom-call(s32[1,128]{1,0:T(1,128)} %get-tuple-element.7.len_ref, bf16[4,2048,128]{2,1,0:T(8,128)(2,1)} %get-tuple-element.8.x_ref, f32[1,512]{1,0:T(1,128)} %bitcast.2, bf16[512,1536]{1,0:T(8,128)(2,1)} %wqkv_ref.1, bf16[512,512]{1,0:T(8,128)(2,1)} %wout_ref.1, f32[1,512]{1,0:T(1,128)} %bitcast.3, ...), custom_call_target="tpu_custom_call" | custom-call | tf_op jit(solution)/shard_map/pallas_call | solution.py:546
  111.2 2.3 %copy.11 = bf16[2,512,512]{2,1,0:T(8,128)(2,1)} copy(bf16[2,512,512]{2,1,0:T(8,128)(2,1)} %shard_map.92) | data formatting | bytes 2097152

commit v7 on v6

--- a/solution.py
+++ b/solution.py
@@ -313,49 +313,37 @@
     get_in.start()
     get_down.start()
     length = len_ref[0, 126 + z % 2]
-
-    def worker(q):
-        return jnp.where((q == 0) | (q == 3), 0, 1)
+    ahead, behind = jnp.where(k == 0, up, down), jnp.where(k == 0, down, up)
 
     def quarter_of(step):
-        early = jnp.where(z < 2, 1, 0)
-        return jnp.where(step == early, k, 3 - k)
-
-    def block(b):
-        return pl.ds(256 * b, 256)
-
-    def near(step, b, q):
-        return remote(obuf.at[step, block(b)], out_ref.at[slot, block(b)], send_sem.at[step, b],
-                      recv_sem.at[slot, b], (base + holder, q))
-
-    def own(step, b):
-        return remote(obuf.at[step, block(b)], out_ref.at[slot, block(b)], send_sem.at[step, b],
-                      recv_sem.at[slot, b], (base + 1 - k, z))
-
-    def far(b):
-        return remote(obuf.at[0, block(b)], relay, send_sem.at[0, b], far_recv, (r, (up, down)[b]))
-
-    def passing(b):
-        source, target = ((down, up), (up, down))[b]
-        return remote(relay, out_ref.at[source % 2, block(b)], pass_send, recv_sem.at[source % 2, b],
-                      (base + source // 2, target))
-
-    def send(step, b, act):
+        return jnp.where(step == 0, (z + 2) % 4, jnp.where(step == 1, ahead, jnp.where(step == 2, behind, z)))
+
+    def half_of(quarter):
+        return (quarter + k) % 2
+
+    def rows_of(half):
+        return pl.ds(pl.multiple_of(256 * half, 256), 256)
+
+    def block(step):
+        return obuf.at[pl.ds(256 * step, 256)]
+
+    def landing(step):
+        return out_ref.at[slot, rows_of(half_of(quarter_of(step)))]
+
+    def far():
+        return remote(block(0), relay, send_sem.at[0], far_recv, (r, ahead))
+
+    def near(step):
         q = quarter_of(step)
-        dist = (q - z) % 4
-
-        @pl.when((dist == 1) | (dist == 3))
-        def _():
-            act(near(step, b, q))
-
-        @pl.when((dist == 0) & (holder != k))
-        def _():
-            act(own(step, b))
-
-        if step == 0:
-            @pl.when(dist == 2)
-            def _():
-                act(far(b))
+        return remote(block(step), landing(step), send_sem.at[step], recv_sem.at[slot, half_of(q)], (base + holder, q))
+
+    def own():
+        return remote(block(3), landing(3), send_sem.at[3], recv_sem.at[slot, half_of(z)], (base + 1 - k, z))
+
+    def passing():
+        half = half_of(ahead)
+        return remote(relay, out_ref.at[behind % 2, rows_of(half)], pass_send, recv_sem.at[behind % 2, half],
+                      (base + behind // 2, ahead))
 
     for c in range(4):
         wvt[128 * c : 128 * c + 128, :] = wqkv_ref[:, 2 * D + 128 * c : 2 * D + 128 * c + 128].astype(F32).T.astype(BF)
@@ -386,145 +374,133 @@
         return 0
 
     lax.fori_loop(0, 4, project, 0)
-
-    def attend(quarter):
+    pl.semaphore_wait(barrier, len(peers))
+
+    def attend(n, at):
         lane = lax.broadcasted_iota(jnp.int32, (256, 128), 1)
         tri = (lax.broadcasted_iota(jnp.int32, (256, 256), 0)
                <= lax.broadcasted_iota(jnp.int32, (256, 256), 1))
-        order = [(0, 0), (0, 1), (1, 0), (1, 1)]
-
-        def tiles(j):
-            return 2 * quarter + j + 1
 
         def columns(hp):
             return pl.ds(pl.multiple_of(hp * 128, 128), 128)
 
-        def query(hp, g):
-            j, odd = order[g]
-            q = qs[256 * j : 256 * j + 256, columns(hp)].astype(F32)
+        def query(hp, odd):
+            q = qs[:, columns(hp)].astype(F32)
             if odd:
                 return jnp.where(lane >= 64, q, jnp.where(lane == 0, 1.0, 0.0)).astype(BF)
             return jnp.where(lane < 64, q, jnp.where(lane == 64, 1.0, 0.0)).astype(BF)
 
-        def score(hp, g, qa, c, top):
-            j, odd = order[g]
+        def score(hp, odd, qa, c, top):
             s = dot_t((ko if odd else ke)[256 * c : 256 * c + 256, columns(hp)], qa)
-            if c == tiles(j) - 1:
+            if c == n - 1:
                 s = jnp.where(tri, s, NEG)
-            sc[g % 2, c] = s
+            sc[odd, c] = s
             m = jnp.max(s.reshape(4, 8, 8, 256), axis=1)
             return m if top is None else jnp.maximum(top, m)
 
         def finish(top):
             return jnp.max(jnp.max(top, axis=0), axis=0, keepdims=True)
 
-        def first_scores(hp):
-            qa, top = query(hp, 0), None
-            for c in range(tiles(0)):
-                top = score(hp, 0, qa, c, top)
-            return finish(top)
+        qa, top = query(0, 0), None
+        for c in range(n):
+            top = score(0, 0, qa, c, top)
 
         def heads(hp, top):
             outs = []
-            after = jnp.minimum(hp + 1, 3)
-            for g, (j, odd) in enumerate(order):
-                ahead, hp_ahead = (g + 1) % 4, hp if g < 3 else after
-                qa, top_ahead, acc = query(hp_ahead, ahead), None, None
-                n, n_ahead = tiles(j), tiles(order[ahead][0])
-                for c in range(max(n, n_ahead)):
-                    if c < n_ahead:
-                        top_ahead = score(hp_ahead, ahead, qa, c, top_ahead)
-                    if c < n:
-                        p = jnp.exp2(sc[g % 2, c] - top).astype(BF)
-                        o = dot(vt[2 * hp + odd, :, 256 * c : 256 * c + 256], p)
-                        acc = o if acc is None else acc + o
+            for odd in range(2):
+                hp_next = hp if odd == 0 else jnp.minimum(hp + 1, 3)
+                qa, top_next, acc = query(hp_next, 1 - odd), None, None
+                for c in range(n):
+                    top_next = score(hp_next, 1 - odd, qa, c, top_next)
+                    p = jnp.exp2(sc[odd, c] - top).astype(BF)
+                    o = dot(vt[2 * hp + odd, :, 256 * c : 256 * c + 256], p)
+                    acc = o if acc is None else acc + o
                 outs.append(acc[0:64, :] / acc[64:65, :])
-                if odd:
-                    att[256 * j : 256 * j + 256, columns(hp)] = jnp.concatenate(outs, axis=0).T.astype(BF)
-                    outs = []
-                top = finish(top_ahead)
+                top = finish(top_next)
+            att[at, columns(hp)] = jnp.concatenate(outs, axis=0).T.astype(BF)
             return top
 
-        lax.fori_loop(0, 4, heads, first_scores(0))
-
-    def compute_attention(quarter):
-        rows = pl.ds(pl.multiple_of(quarter * 512, 512), 512)
-        qs[...] = (dot(nrm[rows, :], wqkv_ref[:, :D]) * (0.125 * LOG2E)).astype(BF)
-        for q in range(4):
-            @pl.when(quarter == q)
-            def _():
-                attend(q)
-
-    def mlp(quarter):
-        src = pl.ds(pl.multiple_of(quarter * 512, 512), 512)
-        resid = jnp.concatenate([x_ref[c, src, :].astype(F32) for c in range(4)], axis=1)
-        hidden = (resid + dot(att[...], wout_ref[...])).astype(BF)
-        hid[...] = hidden
+        lax.fori_loop(0, 4, heads, finish(top))
+
+    def mlp(steps):
+        rows = slice(0, 256 * len(steps))
+        resid = []
+        for step in steps:
+            quarter = quarter_of(step)
+            src = pl.ds(pl.multiple_of(quarter * 512 + half_of(quarter) * 256, 256), 256)
+            resid.append(jnp.concatenate([x_ref[c, src, :].astype(F32) for c in range(4)], axis=1))
+        hidden = (jnp.concatenate(resid, axis=0) + dot(att[rows, :], wout_ref[...])).astype(BF)
+        hid[rows, :] = hidden
         hidden = hidden.astype(F32)
         scale = lax.rsqrt(jnp.mean(hidden * hidden, axis=1, keepdims=True) + 1e-6)
-        att[...] = (hidden * scale * gain2_ref[...]).astype(BF)
-
+        att[rows, :] = (hidden * scale * gain2_ref[...]).astype(BF)
         for f in range(0, FF, 256):
-            gate = dot(att[...], win_ref[:, f : f + 256])
-            high = dot(att[...], win_ref[:, FF + f : FF + f + 256])
-            act[:, f : f + 256] = (gate / (1.0 + jnp.exp(-gate)) * high).astype(BF)
-
-    def lower(step, b, quarter):
-        rows = pl.ds(pl.multiple_of(256 * b, 256), 256)
-        out = (hid[rows, :].astype(F32) + dot(act[rows, :], wdown_ref[...])).astype(BF)
-        obuf[step, rows, :] = out
-
-        @pl.when((quarter == z) & (holder == k))
-        def _():
-            out_ref[slot, rows, :] = out
+            gate = dot(att[rows, :], win_ref[:, f : f + 256])
+            high = dot(att[rows, :], win_ref[:, FF + f : FF + f + 256])
+            act[rows, f : f + 256] = (gate / (1.0 + jnp.exp(-gate)) * high).astype(BF)
+        return (hid[rows, :].astype(F32) + dot(act[rows, :], wdown_ref[...])).astype(BF)
 
     def run(step, _):
         quarter = quarter_of(step)
-        compute_attention(quarter)
-
-        @pl.when(step == 0)
+        half = half_of(quarter)
+
+        @pl.when(step == 3)
+        def _():
+            far().wait_recv()
+            passing().start()
+
+        src = pl.ds(pl.multiple_of(quarter * 512 + half * 256, 256), 256)
+        qs[...] = (dot(nrm[src, :], wqkv_ref[:, :D]) * (0.125 * LOG2E)).astype(BF)
+        at = rows_of(jnp.where(step == 1, 1, 0))
+        for n in range(1, 9):
+            @pl.when(2 * quarter + half + 1 == n)
+            def _():
+                attend(n, at)
+
+        @pl.when(step == 1)
         def _():
             get_in.wait()
             get_down.wait()
-            pl.semaphore_wait(barrier, len(peers))
-
-        @pl.when(step == 1)
+            obuf[0:512, :] = mlp((0, 1))
+            far().start()
+            near(1).start()
+
+        @pl.when(step >= 2)
         def _():
-            for b in range(2):
-                @pl.when(worker((up, down)[b]) == k)
-                def _():
-                    far(b).wait_recv()
-                    passing(b).start()
-
-        mlp(quarter)
-
-        def each(b, _):
-            lower(step, b, quarter)
-            for ss in range(2):
-                for bb in range(2):
-                    @pl.when((step == ss) & (b == bb))
-                    def _():
-                        send(ss, bb, lambda copy: copy.start())
-            return 0
-
-        lax.fori_loop(0, 2, each, 0)
+            out = mlp((step,))
+            obuf[pl.ds(pl.multiple_of(256 * step, 256), 256), :] = out
+
+            @pl.when(step == 2)
+            def _():
+                near(2).start()
+
+            @pl.when((step == 3) & (holder == k))
+            def _():
+                out_ref[slot, rows_of(half), :] = out
+
+            @pl.when((step == 3) & (holder != k))
+            def _():
+                own().start()
+
         return 0
 
-    lax.fori_loop(0, 2, run, 0)
+    lax.fori_loop(0, 4, run, 0)
 
     for h in range(2):
-        @pl.when((2 * k + h != z) | (worker(z) != k))
-        def _():
-            for b in range(2):
-                remote(obuf.at[0, block(b)], out_ref.at[h, block(b)], send_sem.at[0, b], recv_sem.at[h, b],
+        for b in range(2):
+            @pl.when((2 * k + h != z) | ((z + k) % 2 != b))
+            def _():
+                remote(block(0), out_ref.at[h, pl.ds(256 * b, 256)], send_sem.at[0], recv_sem.at[h, b],
                        (base + 1 - k, z)).wait_recv()
-    for ss in range(2):
-        for b in range(2):
-            send(ss, b, lambda copy: copy.wait_send())
-    for b in range(2):
-        @pl.when(worker((up, down)[b]) == k)
-        def _():
-            passing(b).wait_send()
+    far().wait_send()
+    near(1).wait_send()
+    near(2).wait_send()
+
+    @pl.when(holder != k)
+    def _():
+        own().wait_send()
+
+    passing().wait_send()
 
 
 def local(token_ids, lengths, table, attn_gain, w_qkv, w_out, mlp_gain, w_in, w_down):
@@ -547,12 +523,12 @@
         layer_kernel,
         out_shape=jax.ShapeDtypeStruct((2, 512, D), BF),
         in_specs=[SM, VM, VM, VM, VM, VM, ANY, ANY], out_specs=VM,
-        scratch_shapes=[pltpu.VMEM((2048, D), BF), pltpu.VMEM((512, D), BF), pltpu.VMEM((2048, D), BF),
+        scratch_shapes=[pltpu.VMEM((2048, D), BF), pltpu.VMEM((256, D), BF), pltpu.VMEM((2048, D), BF),
                         pltpu.VMEM((2048, D), BF), pltpu.VMEM((8, 80, 2048), BF), pltpu.VMEM((D, D), BF),
                         pltpu.VMEM((2, 8, 256, 256), F32), pltpu.VMEM((512, D), BF), pltpu.VMEM((512, D), BF),
-                        pltpu.VMEM((512, FF), BF), pltpu.VMEM((2, 512, D), BF),
-                        pltpu.VMEM((256, D), BF), pltpu.VMEM((D, 2 * FF), BF), pltpu.VMEM((FF, D), BF), dma((2,)),
-                        dma((2, 2)), dma, dma((2, 2)), dma],
+                        pltpu.VMEM((512, FF), BF), pltpu.VMEM((1024, D), BF), pltpu.VMEM((256, D), BF),
+                        pltpu.VMEM((D, 2 * FF), BF), pltpu.VMEM((FF, D), BF), dma((2,)),
+                        dma((4,)), dma, dma((2, 2)), dma],
         compiler_params=params(2),
     )(lens, full, attn_gain.reshape(1, D), w_qkv, w_out, mlp_gain.reshape(1, D), w_in, w_down)
 

time: 115 us -> 112 us (0.974); the launches traced: 114 us -> 112 us
  Pallas kernels: 111 us -> 109 us
    pallas_call x1, Pallas kernels: 35.6 us -> 33.8 us  [local(): pl.pallas_call(layer_kernel, out_shape=jax.ShapeDtypeStruct((2, 512, D),...]
where the time goes in v7:
time: 112 us
  Pallas kernels  109 us (97%)
  local copies, waits for them, and re-layouts  2.26 us (2%)
    pallas_call x1, Pallas kernels, local(): pl.pallas_call(front_kernel, out_shape=[jax.ShapeDtypeStruct((4, 2048, 12...  75.6 us
    pallas_call x1, Pallas kernels, local(): pl.pallas_call(layer_kernel, out_shape=jax.ShapeDtypeStruct((2, 512, D),...  33.8 us
    unnamed x1, local copies, waits for them, and re-layouts  2.26 us

profile of v7, /device:TPU:1, one launch (start us, length us, event | category | flops | bytes accessed | tf_op | source)
XLA Modules:
  0.0 111.8 jit_solution(16649933356973583638)
XLA Ops:
  0.0 75.6 %shard_map.91 = (bf16[4,2048,128]{2,1,0:T(8,128)(2,1)}, s32[1,128]{1,0:T(1,128)}) custom-call(s32[2]{0:T(128)} %len_ref.1, s32[2,512]{1,0:T(2,128)} %tok_ref.1, bf16[16384,128]{1,0:T(8,128)(2,1)} %table_hbm.1), custom_call_target="tpu_custom_call" | custom-call | tf_op jit(solution)/shard_map/pallas_call | solution.py:508
  75.7 33.8 %shard_map.92 = bf16[2,512,512]{2,1,0:T(8,128)(2,1)} custom-call(s32[1,128]{1,0:T(1,128)} %get-tuple-element.7.len_ref, bf16[4,2048,128]{2,1,0:T(8,128)(2,1)} %get-tuple-element.8.x_ref, f32[1,512]{1,0:T(1,128)} %bitcast.2, bf16[512,1536]{1,0:T(8,128)(2,1)} %wqkv_ref.1, bf16[512,512]{1,0:T(8,128)(2,1)} %wout_ref.1, f32[1,512]{1,0:T(1,128)} %bitcast.3, ...), custom_call_target="tpu_custom_call" | custom-call | tf_op jit(solution)/shard_map/pallas_call | solution.py:522
  109.5 2.3 %copy.11 = bf16[2,512,512]{2,1,0:T(8,128)(2,1)} copy(bf16[2,512,512]{2,1,0:T(8,128)(2,1)} %shard_map.92) | data formatting | bytes 2097152

commit v8 on v7

--- a/solution.py
+++ b/solution.py
@@ -109,10 +109,18 @@
         msg_ref[:, j, :] = req[:, 128 * j : 128 * j + 128]
 
 
-def front_kernel(len_ref, tok_ref, table_hbm, out_ref, lens_ref,
+def whole_kernel(len_ref, tok_ref, table_hbm, gain_ref, wqkv_hbm, wout_hbm, gain2_ref, win_hbm, wdown_hbm, out_ref, *rest):
+    front, layer = rest[: -len(LAYER)], rest[-len(LAYER) :]
+    start, prepare, project, late = layer_kernel(
+        gain_ref, wqkv_hbm, wout_hbm, gain2_ref, win_hbm, wdown_hbm, out_ref, layer, front[0])
+    front_kernel(len_ref, tok_ref, table_hbm, *front, start, prepare, project)
+    late()
+
+
+def front_kernel(len_ref, tok_ref, table_hbm, out_ref,
                  ids_ref, msg_ref, asked_v, asked_s, slot_v, slot_s, table_ref, wide, stage, block, relay, back, emb,
                  relay_z, ids_send, ids_recv, ask_send, ask_recv, copy_sem, send_sem, recv_sem, hop_send, hop_recv,
-                 z_send, z_relay_send, z_relay_recv, z_recv, pass_send, pass_recv, own_send, own_recv):
+                 z_send, z_relay_send, z_relay_recv, z_recv, pass_send, pass_recv, own_send, own_recv, start, prepare, project):
     r, z, y, x, k = place()
     base = r - k
     other = (base + 1 - k, z)
@@ -122,6 +130,7 @@
     plane = [((r + s) % 32, z) for s in range(1, 32)]
     load = pltpu.make_async_copy(table_hbm, table_ref, copy_sem.at[0])
     load.start()
+    start()
     greet(column + plane + [(base + 1 - k, up), (base + 1 - k, down)])
 
     copies = []
@@ -159,7 +168,7 @@
     to_asked.start()
     to_asked.wait()
     to_slots.wait()
-    lens_ref[...] = asked_v[base + holder, 0:1, :]
+    length = asked_s[base + holder, 0, 126 + z % 2]
 
     def row(dy, dx, dk):
         return (((y + dy) % 4) * 4 + (x + dx) % 4) * 2 + (k + dk) % 2
@@ -200,6 +209,8 @@
         copy.start()
         final.append((copy, row(-dy, -dx, dk)))
 
+    prepare()
+
     def spread(source):
         wide[pl.ds(pl.multiple_of(source * CAP, 8), CAP), :] = back[source].astype(F32)
 
@@ -280,6 +291,12 @@
     for copy, _ in final:
         copy.wait_send()
 
+    @pl.when(k != holder)
+    def _():
+        for half in range(2):
+            own(0, half).wait_recv()
+
+    project(2 * k, 2 * k + 2, length)
     for i, source in enumerate((down, up, (z + 2) % 4)):
         passed[i].wait_send()
         got = out_ref.at[source, theirs]
@@ -287,32 +304,23 @@
     relayed.wait_send()
     for h, half in pieces:
         send(h, half, lambda copy: copy.wait_send())
-
-    @pl.when(k != holder)
-    def _():
-        for half in range(2):
-            own(0, half).wait_recv()
-
-
-def layer_kernel(len_ref, x_ref, gain_ref, wqkv_ref, wout_ref, gain2_ref, win_hbm, wdown_hbm, out_ref,
-                 nrm, qs, ke, ko, vt, wvt, sc, att, hid, act, obuf, relay, win_ref, wdown_ref, sems,
-                 send_sem, far_recv, recv_sem, pass_send):
+    project(2 - 2 * k, 4 - 2 * k, length)
+
+
+LAYER = [(2048, D, BF), (1024, D, BF), (2048, D, BF), (2048, D, BF), (8, 80, 2048, BF), (D, D, BF), (2, 8, 256, 256, F32),
+         (8, 80, 256, F32), (512, D, BF), (512, D, BF), (512, FF, BF), (1024, D, BF), (256, D, BF), (D, 3 * D, BF), (D, D, BF),
+         (D, 2 * FF, BF), (FF, D, BF), 4, (4,), (), (2, 2), ()]
+
+
+def layer_kernel(gain_ref, wqkv_hbm, wout_hbm, gain2_ref, win_hbm, wdown_hbm, out_ref, scratch, x_ref):
+    (nrm, qs, ke, ko, vt, wvt, sc, ot, att, hid, act, obuf, relay, wqkv_ref, wout_ref, win_ref, wdown_ref, sems,
+     send_sem, far_recv, recv_sem, pass_send) = scratch
     r, z, _, _, k = place()
     base = r - k
     up, down = (z + 1) % 4, (z + 3) % 4
     holder, slot = z // 2, z % 2
-    peers = [(base + 1 - k, z)]
-    for kk in range(2):
-        for s in (1, 3):
-            peers.append((base + kk, (z + s) % 4))
-    barrier = pltpu.get_barrier_semaphore()
-    for device in peers:
-        pl.semaphore_signal(barrier, inc=1, device_id=device, device_id_type=MESH)
-    get_in = pltpu.make_async_copy(win_hbm, win_ref, sems.at[0])
-    get_down = pltpu.make_async_copy(wdown_hbm, wdown_ref, sems.at[1])
-    get_in.start()
-    get_down.start()
-    length = len_ref[0, 126 + z % 2]
+    gets = [pltpu.make_async_copy(src, dst, sems.at[i]) for i, (src, dst) in enumerate(
+        [(wqkv_hbm, wqkv_ref), (wout_hbm, wout_ref), (win_hbm, win_ref), (wdown_hbm, wdown_ref)])]
     ahead, behind = jnp.where(k == 0, up, down), jnp.where(k == 0, down, up)
 
     def quarter_of(step):
@@ -345,10 +353,21 @@
         return remote(relay, out_ref.at[behind % 2, rows_of(half)], pass_send, recv_sem.at[behind % 2, half],
                       (base + behind // 2, ahead))
 
-    for c in range(4):
-        wvt[128 * c : 128 * c + 128, :] = wqkv_ref[:, 2 * D + 128 * c : 2 * D + 128 * c + 128].astype(F32).T.astype(BF)
-
-    def project(i, _):
+    def start():
+        for get in gets:
+            get.start()
+
+    def prepare():
+        for get in gets:
+            get.wait()
+        for c in range(4):
+            rows = slice(128 * c, 128 * c + 128)
+            wvt[rows, :] = wqkv_ref[:, 2 * D + 128 * c : 2 * D + 128 * c + 128].astype(F32).T.astype(BF)
+
+    def project_rows(low, high, length):
+        lax.fori_loop(low, high, functools.partial(project, length), 0)
+
+    def project(length, i, _):
         rows = pl.ds(pl.multiple_of(i * 512, 512), 512)
         parts = [x_ref[c, rows, :].astype(F32) for c in range(4)]
         square = parts[0] * parts[0]
@@ -373,19 +392,18 @@
             vt[h, 64:80, rows] = tail
         return 0
 
-    lax.fori_loop(0, 4, project, 0)
-    pl.semaphore_wait(barrier, len(peers))
-
-    def attend(n, at):
+
+    def attend(n, step):
         lane = lax.broadcasted_iota(jnp.int32, (256, 128), 1)
         tri = (lax.broadcasted_iota(jnp.int32, (256, 256), 0)
                <= lax.broadcasted_iota(jnp.int32, (256, 256), 1))
+        here = pl.ds(pl.multiple_of(256 * step, 256), 256)
 
         def columns(hp):
             return pl.ds(pl.multiple_of(hp * 128, 128), 128)
 
         def query(hp, odd):
-            q = qs[:, columns(hp)].astype(F32)
+            q = qs[here, columns(hp)].astype(F32)
             if odd:
                 return jnp.where(lane >= 64, q, jnp.where(lane == 0, 1.0, 0.0)).astype(BF)
             return jnp.where(lane < 64, q, jnp.where(lane == 64, 1.0, 0.0)).astype(BF)
@@ -401,26 +419,34 @@
         def finish(top):
             return jnp.max(jnp.max(top, axis=0), axis=0, keepdims=True)
 
-        qa, top = query(0, 0), None
-        for c in range(n):
-            top = score(0, 0, qa, c, top)
-
-        def heads(hp, top):
-            outs = []
+        def pair(hp, tops, more):
+            new = []
             for odd in range(2):
-                hp_next = hp if odd == 0 else jnp.minimum(hp + 1, 3)
-                qa, top_next, acc = query(hp_next, 1 - odd), None, None
+                qa, top, acc = query(hp + 1, odd) if more else None, None, None
                 for c in range(n):
-                    top_next = score(hp_next, 1 - odd, qa, c, top_next)
-                    p = jnp.exp2(sc[odd, c] - top).astype(BF)
+                    p = jnp.exp2(sc[odd, c] - tops[odd]).astype(BF)
                     o = dot(vt[2 * hp + odd, :, 256 * c : 256 * c + 256], p)
                     acc = o if acc is None else acc + o
-                outs.append(acc[0:64, :] / acc[64:65, :])
-                top = finish(top_next)
-            att[at, columns(hp)] = jnp.concatenate(outs, axis=0).T.astype(BF)
-            return top
-
-        lax.fori_loop(0, 4, heads, finish(top))
+                    if more:
+                        top = score(hp + 1, odd, qa, c, top)
+                ot[2 * hp + odd] = acc
+                if more:
+                    new.append(finish(top))
+            return tuple(new)
+
+        tops = []
+        for odd in range(2):
+            qa, top = query(0, odd), None
+            for c in range(n):
+                top = score(0, odd, qa, c, top)
+            tops.append(finish(top))
+        tops = lax.fori_loop(0, 3, lambda hp, tops: pair(hp, tops, True), tuple(tops))
+        pair(3, tops, False)
+
+    def normalise(at):
+        for hp in range(4):
+            outs = [ot[2 * hp + odd, 0:64, :] / ot[2 * hp + odd, 64:65, :] for odd in range(2)]
+            att[at, 128 * hp : 128 * hp + 128] = jnp.concatenate(outs, axis=0).T.astype(BF)
 
     def mlp(steps):
         rows = slice(0, 256 * len(steps))
@@ -449,18 +475,15 @@
             far().wait_recv()
             passing().start()
 
-        src = pl.ds(pl.multiple_of(quarter * 512 + half * 256, 256), 256)
-        qs[...] = (dot(nrm[src, :], wqkv_ref[:, :D]) * (0.125 * LOG2E)).astype(BF)
-        at = rows_of(jnp.where(step == 1, 1, 0))
         for n in range(1, 9):
             @pl.when(2 * quarter + half + 1 == n)
             def _():
-                attend(n, at)
+                attend(n, step)
+
+        normalise(rows_of(jnp.where(step == 1, 1, 0)))
 
         @pl.when(step == 1)
         def _():
-            get_in.wait()
-            get_down.wait()
             obuf[0:512, :] = mlp((0, 1))
             far().start()
             near(1).start()
@@ -484,53 +507,57 @@
 
         return 0
 
-    lax.fori_loop(0, 4, run, 0)
-
-    for h in range(2):
-        for b in range(2):
-            @pl.when((2 * k + h != z) | ((z + k) % 2 != b))
-            def _():
-                remote(block(0), out_ref.at[h, pl.ds(256 * b, 256)], send_sem.at[0], recv_sem.at[h, b],
-                       (base + 1 - k, z)).wait_recv()
-    far().wait_send()
-    near(1).wait_send()
-    near(2).wait_send()
-
-    @pl.when(holder != k)
-    def _():
-        own().wait_send()
-
-    passing().wait_send()
+    def late():
+        mine = []
+        for step in range(4):
+            quarter = quarter_of(step)
+            src = pl.ds(pl.multiple_of(quarter * 512 + half_of(quarter) * 256, 256), 256)
+            mine.append(nrm[src, :])
+        qs[...] = (dot(jnp.concatenate(mine, axis=0), wqkv_ref[:, :D]) * (0.125 * LOG2E)).astype(BF)
+        lax.fori_loop(0, 4, run, 0)
+
+        for h in range(2):
+            for b in range(2):
+                @pl.when((2 * k + h != z) | ((z + k) % 2 != b))
+                def _():
+                    remote(block(0), out_ref.at[h, pl.ds(256 * b, 256)], send_sem.at[0], recv_sem.at[h, b],
+                           (base + 1 - k, z)).wait_recv()
+        far().wait_send()
+        near(1).wait_send()
+        near(2).wait_send()
+
+        @pl.when(holder != k)
+        def _():
+            own().wait_send()
+
+        passing().wait_send()
+
+    return start, prepare, project_rows, late
 
 
 def local(token_ids, lengths, table, attn_gain, w_qkv, w_out, mlp_gain, w_in, w_down):
     dma = pltpu.SemaphoreType.DMA
-    full, lens = pl.pallas_call(
-        front_kernel,
-        out_shape=[jax.ShapeDtypeStruct((4, 2048, 128), BF), jax.ShapeDtypeStruct((1, 128), jnp.int32)],
-        in_specs=[SM, VM, ANY], out_specs=[VM, VM],
+    layer = []
+    for entry in LAYER:
+        if isinstance(entry, tuple) and entry and not isinstance(entry[-1], int):
+            layer.append(pltpu.VMEM(entry[:-1], entry[-1]))
+        else:
+            layer.append(dma if entry == () else dma((entry,) if isinstance(entry, int) else entry))
+    return pl.pallas_call(
+        whole_kernel,
+        out_shape=jax.ShapeDtypeStruct((2, 512, D), BF),
+        in_specs=[SM, VM, ANY, VM, ANY, ANY, VM, ANY, ANY], out_specs=VM,
         scratch_shapes=[
+            pltpu.VMEM((4, 2048, 128), BF),
             pltpu.VMEM((4, 2, 512), jnp.int32), pltpu.VMEM((32, 4, 128), jnp.int32), pltpu.VMEM((32, 4, 128), jnp.int32),
             pltpu.SMEM((32, 4, 128), jnp.int32), pltpu.VMEM((32, 128), jnp.int32), pltpu.SMEM((32, 128), jnp.int32),
             pltpu.VMEM((16384, 128), BF), pltpu.VMEM((16384, 128), F32), pltpu.VMEM((1024, 128), F32),
             pltpu.VMEM((31, CAP, 128), BF), pltpu.VMEM((14, CAP, 128), BF), pltpu.VMEM((32, CAP, 128), BF),
             pltpu.VMEM((2, 2048, 128), BF), pltpu.VMEM((1024, 128), BF),
             dma((3,)), dma((3,)), dma((31,)), dma((31,)), dma((3,)), dma((31,)), dma((31,)), dma((14,)), dma((14,)),
-            dma((2, 2)), dma((2,)), dma, dma((3,)), dma((4,)), dma((3,)), dma((2,)), dma((2,))],
-        compiler_params=params(1),
-    )(lengths, token_ids, table)
-    return pl.pallas_call(
-        layer_kernel,
-        out_shape=jax.ShapeDtypeStruct((2, 512, D), BF),
-        in_specs=[SM, VM, VM, VM, VM, VM, ANY, ANY], out_specs=VM,
-        scratch_shapes=[pltpu.VMEM((2048, D), BF), pltpu.VMEM((256, D), BF), pltpu.VMEM((2048, D), BF),
-                        pltpu.VMEM((2048, D), BF), pltpu.VMEM((8, 80, 2048), BF), pltpu.VMEM((D, D), BF),
-                        pltpu.VMEM((2, 8, 256, 256), F32), pltpu.VMEM((512, D), BF), pltpu.VMEM((512, D), BF),
-                        pltpu.VMEM((512, FF), BF), pltpu.VMEM((1024, D), BF), pltpu.VMEM((256, D), BF),
-                        pltpu.VMEM((D, 2 * FF), BF), pltpu.VMEM((FF, D), BF), dma((2,)),
-                        dma((4,)), dma, dma((2, 2)), dma],
-        compiler_params=params(2),
-    )(lens, full, attn_gain.reshape(1, D), w_qkv, w_out, mlp_gain.reshape(1, D), w_in, w_down)
+            dma((2, 2)), dma((2,)), dma, dma((3,)), dma((4,)), dma((3,)), dma((2,)), dma((2,))] + layer,
+        compiler_params=params(1, 63),
+    )(lengths, token_ids, table, attn_gain.reshape(1, D), w_qkv, w_out, mlp_gain.reshape(1, D), w_in, w_down)
 
 
 def solution(mesh):

time: 112 us -> 105 us (0.938)
  Pallas kernels: 109 us -> 102 us
    pallas_call x2 -> x1, Pallas kernels: 109 us -> 102 us  [local(): pl.pallas_call(whole_kernel, out_shape=jax.ShapeDtypeStruct((2, 512, D),...]
where the time goes in v8:
time: 105 us
  Pallas kernels  102 us (97%)
  local copies, waits for them, and re-layouts  2.26 us (2%)
    pallas_call x1, Pallas kernels, local(): pl.pallas_call(whole_kernel, out_shape=jax.ShapeDtypeStruct((2, 512, D),...  102 us
    unnamed x1, local copies, waits for them, and re-layouts  2.26 us

profile of v8, /device:TPU:1, one launch (start us, length us, event | category | flops | bytes accessed | tf_op | source)
XLA Modules:
  0.0 104.5 jit_solution(3559275694496754210)
XLA Ops:
  0.0 102.2 %shard_map.91 = bf16[2,512,512]{2,1,0:T(8,128)(2,1)} custom-call(s32[2]{0:T(128)} %len_ref.1, s32[2,512]{1,0:T(2,128)} %tok_ref.1, bf16[16384,128]{1,0:T(8,128)(2,1)} %table_hbm.1, f32[1,512]{1,0:T(1,128)} %bitcast.2, bf16[512,1536]{1,0:T(8,128)(2,1)} %wqkv_hbm.1, bf16[512,512]{1,0:T(8,128)(2,1)} %wout_hbm.1, f32[1,512]{1,0:T(1,128)} %bitcast.3, ...), custom_call_target="tpu_custom_call" | custom-call | tf_op jit(solution)/shard_map/pallas_call | solution.py:546
  102.3 2.3 %copy.11 = bf16[2,512,512]{2,1,0:T(8,128)(2,1)} copy(bf16[2,512,512]{2,1,0:T(8,128)(2,1)} %shard_map.91) | data formatting | bytes 2097152

commit v9 on v8

--- a/solution.py
+++ b/solution.py
@@ -1,5 +1,3 @@
-import functools
-
 import jax
 import jax.numpy as jnp
 from jax import lax
@@ -120,7 +118,7 @@
 def front_kernel(len_ref, tok_ref, table_hbm, out_ref,
                  ids_ref, msg_ref, asked_v, asked_s, slot_v, slot_s, table_ref, wide, stage, block, relay, back, emb,
                  relay_z, ids_send, ids_recv, ask_send, ask_recv, copy_sem, send_sem, recv_sem, hop_send, hop_recv,
-                 z_send, z_relay_send, z_relay_recv, z_recv, pass_send, pass_recv, own_send, own_recv, start, prepare, project):
+                 z_send, z_relay_send, z_relay_recv, z_recv, relay_pass, pass_send, pass_recv, own_send, own_recv, start, prepare, project):
     r, z, y, x, k = place()
     base = r - k
     other = (base + 1 - k, z)
@@ -219,92 +217,96 @@
         copy.wait_recv()
         spread(source)
 
-    mine = pl.ds(pl.multiple_of(1024 * k, 1024), 1024)
-    theirs = pl.ds(pl.multiple_of(1024 * (1 - k), 1024), 1024)
-
-    def part(i):
-        return pl.ds(1024 * i, 1024)
-
-    def far(h, half):
-        return remote(emb.at[h, part(half)], relay_z, z_relay_send.at[half], z_relay_recv,
-                      (base + half, up if half == 0 else down))
-
-    def near(h, half, step):
-        return remote(emb.at[h, part(half)], out_ref.at[z, part(half)],
-                      z_send.at[step // 2, half], z_recv.at[step // 2], (base + half, (z + step) % 4))
-
-    def own(h, half):
-        return remote(emb.at[h, part(half)], out_ref.at[z, part(half)], own_send.at[half], own_recv.at[half], other)
-
-    def send(h, half, act):
+    def rows(c):
+        return pl.ds(pl.multiple_of(512 * c, 512), 512)
+
+    def far(h, c):
+        return remote(emb.at[h, rows(c)], relay_z.at[rows(c % 2)], z_relay_send.at[c], z_relay_recv.at[c % 2],
+                      (base + c // 2, (up, down)[c // 2]))
+
+    def near(h, c, step):
+        return remote(emb.at[h, rows(c)], out_ref.at[z, rows(c)],
+                      z_send.at[step // 2, c], z_recv.at[step // 2, c % 2], (base + c // 2, (z + step) % 4))
+
+    def own(h, c):
+        return remote(emb.at[h, rows(c)], out_ref.at[z, rows(c)], own_send.at[c], own_recv.at[c], other)
+
+    def send(h, c, act):
         dist = (2 * k + h - z) % 4
 
         @pl.when(dist == 2)
         def _():
-            act(far(h, half))
+            act(far(h, c))
 
         for step in (1, 3):
             @pl.when(dist == step)
             def _():
-                act(near(h, half, step))
+                act(near(h, c, step))
 
         @pl.when(dist == 0)
         def _():
-            act(own(h, half))
+            act(own(h, c))
 
     lead = jnp.where((2 * k - z) % 4 < 2, 1, 0)
-    pieces = [(h, half) for h in (lead, 1 - lead) for half in range(2)]
+    pieces = [(h, c) for h in (lead, 1 - lead) for c in (0, 2, 1, 3)]
     waiting = None
-    for h, half in pieces:
+    for h, c in pieces:
         def gather(j, _):
-            a = (half * 2 + j // 4) * 8 + h * 4 + lax.rem(j, 4)
+            a = c * 8 + h * 4 + j
             for i in range(128):
                 stage[pl.ds(j * 128 + i, 1), :] = wide[pl.ds(slot_s[a, i], 1), :]
             return 0
 
-        lax.fori_loop(0, 8, gather, 0)
-        emb[h, part(half), :] = stage[...].astype(BF)
+        lax.fori_loop(0, 4, gather, 0)
+        emb[h, rows(c), :] = stage[0:512, :].astype(BF)
 
         @pl.when((2 * k + h - z) % 4 == 0)
         def _():
-            out_ref[z, part(half), :] = stage[...].astype(BF)
+            out_ref[z, rows(c), :] = stage[0:512, :].astype(BF)
 
         if waiting is not None:
             send(*waiting, lambda copy: copy.start())
-        waiting = (h, half)
+        waiting = (h, c)
     send(*waiting, lambda copy: copy.start())
 
     behind = jnp.where(k == 0, down, up)
     ahead = jnp.where(k == 0, up, down)
-    relayed = remote(relay_z, out_ref.at[behind, mine], pass_send.at[3], z_recv.at[2], (r, ahead))
-    far(0, 0).wait_recv()
-    relayed.start()
+    sources = (down, up, (z + 2) % 4)
+    relayed = []
+    for j in range(2):
+        copy = remote(relay_z.at[rows(j)], out_ref.at[behind, rows(2 * k + j)], relay_pass.at[j], z_recv.at[2, j], (r, ahead))
+        far(0, j).wait_recv()
+        copy.start()
+        relayed.append(copy)
     passed = []
-    for i, source in enumerate((down, up, (z + 2) % 4)):
-        got = out_ref.at[source, mine]
-        remote(got, got, pass_send.at[i], z_recv.at[i], other).wait_recv()
-        copy = remote(got, got, pass_send.at[i], pass_recv.at[i], other)
-        copy.start()
-        passed.append(copy)
+    for j in range(2):
+        for i, source in enumerate(sources):
+            got = out_ref.at[source, rows(2 * k + j)]
+            remote(got, got, pass_send.at[i, j], z_recv.at[i, j], other).wait_recv()
+            copy = remote(got, got, pass_send.at[i, j], pass_recv.at[i, j], other)
+            copy.start()
+            passed.append(copy)
+
+        if j == 0:
+            @pl.when(k != holder)
+            def _():
+                for c in range(4):
+                    own(0, c).wait_recv()
+
+        project(2 * k + j, length)
+    for j in range(2):
+        for i, source in enumerate(sources):
+            got = out_ref.at[source, rows(2 * (1 - k) + j)]
+            remote(got, got, pass_send.at[i, j], pass_recv.at[i, j], other).wait_recv()
+        project(2 * (1 - k) + j, length)
     for copy in first:
         copy.wait_send()
     for copy, _ in final:
         copy.wait_send()
-
-    @pl.when(k != holder)
-    def _():
-        for half in range(2):
-            own(0, half).wait_recv()
-
-    project(2 * k, 2 * k + 2, length)
-    for i, source in enumerate((down, up, (z + 2) % 4)):
-        passed[i].wait_send()
-        got = out_ref.at[source, theirs]
-        remote(got, got, pass_send.at[i], pass_recv.at[i], other).wait_recv()
-    relayed.wait_send()
-    for h, half in pieces:
-        send(h, half, lambda copy: copy.wait_send())
-    project(2 - 2 * k, 4 - 2 * k, length)
+    for copy in passed + relayed:
+        copy.wait_send()
+    for h, c in pieces:
+        send(h, c, lambda copy: copy.wait_send())
 
 
 LAYER = [(2048, D, BF), (1024, D, BF), (2048, D, BF), (2048, D, BF), (8, 80, 2048, BF), (D, D, BF), (2, 8, 256, 256, F32),
@@ -364,10 +366,7 @@
             rows = slice(128 * c, 128 * c + 128)
             wvt[rows, :] = wqkv_ref[:, 2 * D + 128 * c : 2 * D + 128 * c + 128].astype(F32).T.astype(BF)
 
-    def project_rows(low, high, length):
-        lax.fori_loop(low, high, functools.partial(project, length), 0)
-
-    def project(length, i, _):
+    def project(i, length):
         rows = pl.ds(pl.multiple_of(i * 512, 512), 512)
         parts = [x_ref[c, rows, :].astype(F32) for c in range(4)]
         square = parts[0] * parts[0]
@@ -390,7 +389,6 @@
         for h in range(8):
             vt[h, 0:64, rows] = vals[64 * h : 64 * h + 64, :].astype(BF)
             vt[h, 64:80, rows] = tail
-        return 0
 
 
     def attend(n, step):
@@ -532,7 +530,7 @@
 
         passing().wait_send()
 
-    return start, prepare, project_rows, late
+    return start, prepare, project, late
 
 
 def local(token_ids, lengths, table, attn_gain, w_qkv, w_out, mlp_gain, w_in, w_down):
@@ -545,7 +543,7 @@
             layer.append(dma if entry == () else dma((entry,) if isinstance(entry, int) else entry))
     return pl.pallas_call(
         whole_kernel,
-        out_shape=jax.ShapeDtypeStruct((2, 512, D), BF),
+        out_shape=pltpu.VMEM((2, 512, D), BF),
         in_specs=[SM, VM, ANY, VM, ANY, ANY, VM, ANY, ANY], out_specs=VM,
         scratch_shapes=[
             pltpu.VMEM((4, 2048, 128), BF),
@@ -555,8 +553,8 @@
             pltpu.VMEM((31, CAP, 128), BF), pltpu.VMEM((14, CAP, 128), BF), pltpu.VMEM((32, CAP, 128), BF),
             pltpu.VMEM((2, 2048, 128), BF), pltpu.VMEM((1024, 128), BF),
             dma((3,)), dma((3,)), dma((31,)), dma((31,)), dma((3,)), dma((31,)), dma((31,)), dma((14,)), dma((14,)),
-            dma((2, 2)), dma((2,)), dma, dma((3,)), dma((4,)), dma((3,)), dma((2,)), dma((2,))] + layer,
-        compiler_params=params(1, 63),
+            dma((2, 4)), dma((4,)), dma((2,)), dma((3, 2)), dma((2,)), dma((3, 2)), dma((3, 2)), dma((4,)), dma((4,))] + layer,
+        compiler_params=params(1, 61),
     )(lengths, token_ids, table, attn_gain.reshape(1, D), w_qkv, w_out, mlp_gain.reshape(1, D), w_in, w_down)
 
 

time: 105 us -> 101 us (0.962)
  Pallas kernels: 102 us -> 100 us
  local copies, waits for them, and re-layouts: 2.26 us -> 0.97 us
    pallas_call x1, Pallas kernels: 102 us -> 100 us  [local(): pl.pallas_call(whole_kernel, out_shape=pltpu.VMEM((2, 512, D), BF), in_sp...]
    unnamed x1, local copies, waits for them, and re-layouts: 2.26 us -> 0.97 us
where the time goes in v9:
time: 101 us
  Pallas kernels  100 us (99%)
    pallas_call x1, Pallas kernels, local(): pl.pallas_call(whole_kernel, out_shape=pltpu.VMEM((2, 512, D), BF), in_sp...  100 us

profile of v9, /device:TPU:1, one launch (start us, length us, event | category | flops | bytes accessed | tf_op | source)
XLA Modules:
  0.0 101.3 jit_solution(9626721921133695298)
XLA Ops:
  0.0 100.3 %shard_map.91 = bf16[2,512,512]{2,1,0:T(8,128)(2,1)S(1)} custom-call(s32[2]{0:T(128)} %len_ref.1, s32[2,512]{1,0:T(2,128)} %tok_ref.1, bf16[16384,128]{1,0:T(8,128)(2,1)} %table_hbm.1, f32[1,512]{1,0:T(1,128)} %bitcast.2, bf16[512,1536]{1,0:T(8,128)(2,1)} %wqkv_hbm.1, bf16[512,512]{1,0:T(8,128)(2,1)} %wout_hbm.1, f32[1,512]{1,0:T(1,128)} %bitcast.3, ...), custom_call_target="tpu_custom_call" | custom-call | tf_op jit(solution)/shard_map/pallas_call | solution.py:544
  100.3 1.0 copy.11

commit v10 on v9

--- a/solution.py
+++ b/solution.py
@@ -63,7 +63,10 @@
                 if dx == 2 or dy == 2:
                     hop = (side if dy == 2 else 0, side if dx == 2 else 0)
                 out.append((dy, dx, dk, hop))
-    key = lambda f: (f[3] is None, (f[0] * 5 + f[1] * 3 + f[2] * 7) % 11)
+    def key(f):
+        near = f[3] is None and (f[0] == 0 or f[1] == 0)
+        return (0 if near else 1 if f[3] else 2, f[2] == 0 if f[0] or f[1] else False, (f[0] * 5 + f[1] * 3 + f[2] * 7) % 11)
+
     return sorted(out, key=key)
 
 
@@ -74,8 +77,7 @@
              < lax.broadcasted_iota(jnp.int32, (32, 32), 0)).astype(F32).astype(BF)
     both = jnp.concatenate([before, jnp.ones((128, 128), F32)], axis=0).astype(BF)
     owners = lax.broadcasted_iota(jnp.int32, (32, 128), 0)
-    column = lax.broadcasted_iota(jnp.int32, (4 * 128, 128), 0)
-    ks = jnp.where((column & 127) < CAP // 4, (column >> 7) * (CAP // 4) + (column & 127), -1)
+    ks = lax.broadcasted_iota(jnp.int32, (384, 128), 0)
     lane = lax.broadcasted_iota(jnp.int32, (32, 128), 1)
     owner = ids >> 14
     low, high = (ids & 127).astype(F32), ((ids >> 7) & 127).astype(F32)
@@ -91,7 +93,7 @@
         rank = rank + jnp.where(owner == o, prior[32 * o : 32 * o + 32], 0.0)
     rank_i = rank.astype(jnp.int32)
     slot_ref[...] = jnp.clip(owner * CAP + rank_i, 0, 32 * CAP - 1)
-    acc = jnp.zeros((64, 4 * 128), F32)
+    acc = jnp.zeros((64, 384), F32)
     for a in range(0, 32, 2):
         lefts, rights = [], []
         for b in (a, a + 1):
@@ -101,10 +103,10 @@
             rights.append(jnp.where(ks == rank_i[b : b + 1, :], 1.0, 0.0).astype(BF))
         acc = acc + dot_t(jnp.concatenate(lefts, axis=1), jnp.concatenate(rights, axis=1))
     req = (acc[32:] * 128.0 + acc[:32]).astype(jnp.int32)
-    req0 = jnp.where(lane == 126, lens[0], jnp.where(lane == 127, lens[1], req[:, :128]))
-    msg_ref[:, 0, :] = req0
-    for j in range(1, 4):
-        msg_ref[:, j, :] = req[:, 128 * j : 128 * j + 128]
+    msg_ref[...] = jnp.zeros_like(msg_ref)
+    msg_ref[:, 0, :] = jnp.where(lane == 126, lens[0], jnp.where(lane == 127, lens[1], 0))
+    for j in range(4):
+        msg_ref[:, j, 0 : CAP // 4] = req[:, CAP // 4 * j : CAP // 4 * (j + 1)]
 
 
 def whole_kernel(len_ref, tok_ref, table_hbm, gain_ref, wqkv_hbm, wout_hbm, gain2_ref, win_hbm, wdown_hbm, out_ref, *rest):
@@ -117,7 +119,7 @@
 
 def front_kernel(len_ref, tok_ref, table_hbm, out_ref,
                  ids_ref, msg_ref, asked_v, asked_s, slot_v, slot_s, table_ref, wide, stage, block, relay, back, emb,
-                 relay_z, ids_send, ids_recv, ask_send, ask_recv, copy_sem, send_sem, recv_sem, hop_send, hop_recv,
+                 relay_z, ids_send, ids_recv, ask_send, ask_recv, copy_sem, list_sem, send_sem, recv_sem, hop_send, hop_recv,
                  z_send, z_relay_send, z_relay_recv, z_recv, relay_pass, pass_send, pass_recv, own_send, own_recv, start, prepare, project):
     r, z, y, x, k = place()
     base = r - k
@@ -159,14 +161,7 @@
         return 0
 
     lax.fori_loop(0, 64, widen, 0)
-    for copy in copies:
-        copy.wait()
-    asked_v[...] = jnp.clip(asked_v[...], 0, 16383)
-    to_asked = pltpu.make_async_copy(asked_v, asked_s, copy_sem.at[2])
-    to_asked.start()
-    to_asked.wait()
     to_slots.wait()
-    length = asked_s[base + holder, 0, 126 + z % 2]
 
     def row(dy, dx, dk):
         return (((y + dy) % 4) * 4 + (x + dx) % 4) * 2 + (k + dk) % 2
@@ -180,23 +175,40 @@
         lax.fori_loop(0, 4, some, 0)
         dst[...] = stage[0:CAP, :].astype(BF)
 
+    def take(p, n, arrived=True):
+        if arrived:
+            remote(msg_ref.at[0], asked_v.at[p], ask_send.at[0], ask_recv.at[(r - p) % 32 - 1], other).wait_recv()
+        asked_v[p] = jnp.clip(asked_v[p], 0, 16383)
+        copy = pltpu.make_async_copy(asked_v.at[p], asked_s.at[p], list_sem.at[n])
+        copy.start()
+        return copy
+
     flows = routes()
     hops = [f for f in flows if f[3] is not None]
     direct = [f for f in flows if f[3] is None]
     first, final, waiting = [], [], None
-    for n, (dy, dx, dk, hop) in enumerate(hops + direct):
+    lists = [take(row(*flows[0][:3]), 0)]
+    for n, flow in enumerate(flows):
+        dy, dx, dk, hop = flow
         p = row(dy, dx, dk)
+        lists.append(take(row(*flows[n + 1][:3]), n + 1) if n + 1 < len(flows) else take(r, 31, False))
+        lists[n].wait()
         fill(p, block.at[n])
         if hop is not None:
-            copy = remote(block.at[n], relay.at[n], hop_send.at[n], hop_recv.at[n], (row(*hop, 0), z))
+            i = hops.index(flow)
+            copy = remote(block.at[n], relay.at[i], hop_send.at[i], hop_recv.at[i], (row(*hop, 0), z))
             first.append(copy)
         else:
-            i = n - len(hops)
+            i = direct.index(flow)
             copy = remote(block.at[n], back.at[r], send_sem.at[i], recv_sem.at[i], (p, z))
             final.append((copy, row(-dy, -dx, dk)))
         if waiting is not None:
             waiting.start()
         waiting = copy
+    lists[31].wait()
+    length = asked_s[base + holder, 0, 126 + z % 2]
+    for copy in copies:
+        copy.wait_send()
     fill(r, back.at[r])
     waiting.start()
     for i, (dy, dx, dk, (hy, hx)) in enumerate(hops):
@@ -552,7 +564,7 @@
             pltpu.VMEM((16384, 128), BF), pltpu.VMEM((16384, 128), F32), pltpu.VMEM((1024, 128), F32),
             pltpu.VMEM((31, CAP, 128), BF), pltpu.VMEM((14, CAP, 128), BF), pltpu.VMEM((32, CAP, 128), BF),
             pltpu.VMEM((2, 2048, 128), BF), pltpu.VMEM((1024, 128), BF),
-            dma((3,)), dma((3,)), dma((31,)), dma((31,)), dma((3,)), dma((31,)), dma((31,)), dma((14,)), dma((14,)),
+            dma((3,)), dma((3,)), dma((31,)), dma((31,)), dma((2,)), dma((32,)), dma((31,)), dma((31,)), dma((14,)), dma((14,)),
             dma((2, 4)), dma((4,)), dma((2,)), dma((3, 2)), dma((2,)), dma((3, 2)), dma((3, 2)), dma((4,)), dma((4,))] + layer,
         compiler_params=params(1, 61),
     )(lengths, token_ids, table, attn_gain.reshape(1, D), w_qkv, w_out, mlp_gain.reshape(1, D), w_in, w_down)

time: 101 us -> 101 us (level)
  no operation moved by 1% of the time
where the time goes in v10:
time: 101 us
  Pallas kernels  99.7 us (99%)
    pallas_call x1, Pallas kernels, local(): pl.pallas_call(whole_kernel, out_shape=pltpu.VMEM((2, 512, D), BF), in_sp...  99.7 us

profile of v10, /device:TPU:1, one launch (start us, length us, event | category | flops | bytes accessed | tf_op | source)
XLA Modules:
  0.0 100.7 jit_solution(17672596252999498835)
XLA Ops:
  0.0 99.7 %shard_map.91 = bf16[2,512,512]{2,1,0:T(8,128)(2,1)S(1)} custom-call(s32[2]{0:T(128)} %len_ref.1, s32[2,512]{1,0:T(2,128)} %tok_ref.1, bf16[16384,128]{1,0:T(8,128)(2,1)} %table_hbm.1, f32[1,512]{1,0:T(1,128)} %bitcast.2, bf16[512,1536]{1,0:T(8,128)(2,1)} %wqkv_hbm.1, bf16[512,512]{1,0:T(8,128)(2,1)} %wout_hbm.1, f32[1,512]{1,0:T(1,128)} %bitcast.3, ...), custom_call_target="tpu_custom_call" | custom-call | tf_op jit(solution)/shard_map/pallas_call | solution.py:556
  99.7 1.0 copy.11

commit v11 on v10

--- a/solution.py
+++ b/solution.py
@@ -77,7 +77,7 @@
              < lax.broadcasted_iota(jnp.int32, (32, 32), 0)).astype(F32).astype(BF)
     both = jnp.concatenate([before, jnp.ones((128, 128), F32)], axis=0).astype(BF)
     owners = lax.broadcasted_iota(jnp.int32, (32, 128), 0)
-    ks = lax.broadcasted_iota(jnp.int32, (384, 128), 0)
+    ks = lax.broadcasted_iota(jnp.int32, (176, 128), 0)
     lane = lax.broadcasted_iota(jnp.int32, (32, 128), 1)
     owner = ids >> 14
     low, high = (ids & 127).astype(F32), ((ids >> 7) & 127).astype(F32)
@@ -93,20 +93,27 @@
         rank = rank + jnp.where(owner == o, prior[32 * o : 32 * o + 32], 0.0)
     rank_i = rank.astype(jnp.int32)
     slot_ref[...] = jnp.clip(owner * CAP + rank_i, 0, 32 * CAP - 1)
-    acc = jnp.zeros((64, 384), F32)
+    upper = jnp.where(rank_i >= CAP // 2, 1, 0)
+    within = rank_i - upper * (CAP // 2)
+    acc = jnp.zeros((128, 176), F32)
     for a in range(0, 32, 2):
         lefts, rights = [], []
         for b in (a, a + 1):
-            hit = owners == owner[b : b + 1, :]
-            lefts.append(jnp.concatenate(
-                [jnp.where(hit, low[b : b + 1, :], 0.0), jnp.where(hit, high[b : b + 1, :], 0.0)], axis=0).astype(BF))
-            rights.append(jnp.where(ks == rank_i[b : b + 1, :], 1.0, 0.0).astype(BF))
+            part = slice(b, b + 1)
+            left = []
+            for half in range(2):
+                hit = owners == jnp.where(upper[part] == half, owner[part], -1)
+                left += [jnp.where(hit, low[part], 0.0), jnp.where(hit, high[part], 0.0)]
+            lefts.append(jnp.concatenate(left, axis=0).astype(BF))
+            rights.append(jnp.where(ks == jnp.where(within[part] < CAP // 2, within[part], -1), 1.0, 0.0).astype(BF))
         acc = acc + dot_t(jnp.concatenate(lefts, axis=1), jnp.concatenate(rights, axis=1))
-    req = (acc[32:] * 128.0 + acc[:32]).astype(jnp.int32)
+    req = [(acc[64 * half + 32 : 64 * half + 64] * 128.0 + acc[64 * half : 64 * half + 32]).astype(jnp.int32)
+           for half in range(2)]
     msg_ref[...] = jnp.zeros_like(msg_ref)
     msg_ref[:, 0, :] = jnp.where(lane == 126, lens[0], jnp.where(lane == 127, lens[1], 0))
     for j in range(4):
-        msg_ref[:, j, 0 : CAP // 4] = req[:, CAP // 4 * j : CAP // 4 * (j + 1)]
+        at = CAP // 4 * (j % 2)
+        msg_ref[:, j, 0 : CAP // 4] = req[j // 2][:, at : at + CAP // 4]
 
 
 def whole_kernel(len_ref, tok_ref, table_hbm, gain_ref, wqkv_hbm, wout_hbm, gain2_ref, win_hbm, wdown_hbm, out_ref, *rest):
@@ -455,7 +462,7 @@
 
     def normalise(at):
         for hp in range(4):
-            outs = [ot[2 * hp + odd, 0:64, :] / ot[2 * hp + odd, 64:65, :] for odd in range(2)]
+            outs = [ot[2 * hp + odd, 0:64, :] * (1.0 / ot[2 * hp + odd, 64:65, :]) for odd in range(2)]
             att[at, 128 * hp : 128 * hp + 128] = jnp.concatenate(outs, axis=0).T.astype(BF)
 
     def mlp(steps):

time: 101 us -> 99.7 us (0.987)
  Pallas kernels: 99.7 us -> 98.6 us
    pallas_call x1, Pallas kernels: 99.7 us -> 98.6 us  [local(): pl.pallas_call(whole_kernel, out_shape=pltpu.VMEM((2, 512, D), BF), in_sp...]
where the time goes in v11:
time: 99.7 us; the launch traced here: 99.6 us
  Pallas kernels  98.6 us (99%)
    pallas_call x1, Pallas kernels, local(): pl.pallas_call(whole_kernel, out_shape=pltpu.VMEM((2, 512, D), BF), in_sp...  98.6 us

profile of v11, /device:TPU:1, one launch (start us, length us, event | category | flops | bytes accessed | tf_op | source)
XLA Modules:
  0.0 99.6 jit_solution(6922832703635495716)
XLA Ops:
  0.0 98.6 %shard_map.91 = bf16[2,512,512]{2,1,0:T(8,128)(2,1)S(1)} custom-call(s32[2]{0:T(128)} %len_ref.1, s32[2,512]{1,0:T(2,128)} %tok_ref.1, bf16[16384,128]{1,0:T(8,128)(2,1)} %table_hbm.1, f32[1,512]{1,0:T(1,128)} %bitcast.2, bf16[512,1536]{1,0:T(8,128)(2,1)} %wqkv_hbm.1, bf16[512,512]{1,0:T(8,128)(2,1)} %wout_hbm.1, f32[1,512]{1,0:T(1,128)} %bitcast.3, ...), custom_call_target="tpu_custom_call" | custom-call | tf_op jit(solution)/shard_map/pallas_call | solution.py:563
  98.6 1.0 copy.11

commit v12 on v11

--- a/solution.py
+++ b/solution.py
@@ -65,7 +65,8 @@
                 out.append((dy, dx, dk, hop))
     def key(f):
         near = f[3] is None and (f[0] == 0 or f[1] == 0)
-        return (0 if near else 1 if f[3] else 2, f[2] == 0 if f[0] or f[1] else False, (f[0] * 5 + f[1] * 3 + f[2] * 7) % 11)
+        late = near and f[2] == 1 and (f[0] or f[1])
+        return (3 if late else 0 if near else 1 if f[3] else 2, f[2] == 0 if f[0] or f[1] else False, (f[0] * 5 + f[1] * 3 + f[2] * 7) % 11)
 
     return sorted(out, key=key)
 

time: 99.7 us -> 101 us (1.013)
  no operation moved by 1% of the time
where the time goes in v12:
time: 101 us
  Pallas kernels  99.6 us (99%)
    pallas_call x1, Pallas kernels, local(): pl.pallas_call(whole_kernel, out_shape=pltpu.VMEM((2, 512, D), BF), in_sp...  99.6 us

profile of v12, /device:TPU:1, one launch (start us, length us, event | category | flops | bytes accessed | tf_op | source)
XLA Modules:
  0.0 100.6 jit_solution(10417188497607940964)
XLA Ops:
  0.0 99.6 %shard_map.91 = bf16[2,512,512]{2,1,0:T(8,128)(2,1)S(1)} custom-call(s32[2]{0:T(128)} %len_ref.1, s32[2,512]{1,0:T(2,128)} %tok_ref.1, bf16[16384,128]{1,0:T(8,128)(2,1)} %table_hbm.1, f32[1,512]{1,0:T(1,128)} %bitcast.2, bf16[512,1536]{1,0:T(8,128)(2,1)} %wqkv_hbm.1, bf16[512,512]{1,0:T(8,128)(2,1)} %wout_hbm.1, f32[1,512]{1,0:T(1,128)} %bitcast.3, ...), custom_call_target="tpu_custom_call" | custom-call | tf_op jit(solution)/shard_map/pallas_call | solution.py:564
  99.6 1.0 copy.11
